TPU v7x, 128 devices: a whole 4x4x4 slice. The times are simulated.
128 devices in a mesh: az: 8 (over y, core), rg: 16 (over z, x).
Axes of the slice: x: 4, y: 4, z: 4, core: 2. Of those that a mesh axis runs over, the one named last changes fastest.
Arguments:
- master_raw: float32 [2, 2048, 20000], P(None, 'az', 'rg'), may hold values from -6 to 6
- slave_raw: float32 [2, 2048, 20000], P(None, 'az', 'rg'), may hold values from -6 to 6
- range_ref: float32 [2, 20000], replicated, may hold values from -4 to 4
- az_ref: float32 [2, 2048], replicated, may hold values from -4 to 4
- az_shift: int32 [4, 256], P(None, ('az', 'rg')), may hold values from -32 to 32, as said below
- rg_shift: int32 [4, 256], P(None, ('az', 'rg')), may hold values from -64 to 64, as said below
- valid_lines: int32 [256], replicated, may hold values from 1024 to 2048, as said below
Outputs:
- interferogram: float32 [2, 256, 2048], P(None, None, ('az', 'rg'))
Inputs may be any that keep to these rules, and one draw needn't show every extreme that they name: `az_shift`: azimuth offset of the slave in lines for each block of 512 lines and 64 samples. `rg_shift`: range offset of the slave in samples for each block of 512 lines and 64 samples. Lines 0 to valid_lines[t] - 1 of range tile t are valid.
All inputs are finite; a program needn't handle non-finite values.
Results may differ from a plain program's by a relative error of at most 0.0003.
Values sent between devices are 32-bit elements; how exact they have to be, the bound alone decides.
No kernel may reach another device: no remote copies, remote signals or barrier semaphores. Data moves between devices by JAX's collectives and lax.ppermute only.
A program may use at most 256 MiB of HBM per device.

v0:
```python
from functools import partial
import math

import jax
import jax.numpy as jnp
from jax import lax
from jax.sharding import PartitionSpec as P

LINES = 2048
RV = 16384
RP = 100
AP = 64
LOOK = 8
BA = 512
BR = 64
ASH = 32
RSH = 64
NBA = 4


def extended(shard, sides, width):
    for axis, dim in sides:
        devices, length = (lax.axis_size(axis), shard.shape[dim])
        up = [(i, (i + 1) % devices) for i in range(devices - 1)]
        down = [(j, i) for i, j in up]
        last = lax.slice_in_dim(shard, length - width, length, axis=dim)
        initial = lax.slice_in_dim(shard, 0, width, axis=dim)
        before = lax.ppermute(last, axis, up)
        after = lax.ppermute(initial, axis, down)
        shard = jnp.concatenate([before, shard, after], axis=dim)
    return shard


def twiddle_table(outer, inner, length):
    product = lax.broadcasted_iota(jnp.int32, (outer, inner), 0) * lax.broadcasted_iota(
        jnp.int32, (outer, inner), 1
    )
    angles = (product % length).astype(jnp.float32) * (-2.0 * math.pi / length)
    return (jnp.cos(angles), jnp.sin(angles))


def fourier_table(length):
    return twiddle_table(length, length, length)


def conjugate(pair_value):
    return (pair_value[0], -pair_value[1])


def complex_scale(pair_one, pair_two):
    return (
        pair_one[0] * pair_two[0] - pair_one[1] * pair_two[1],
        pair_one[0] * pair_two[1] + pair_one[1] * pair_two[0],
    )


def complex_einsum(equation, pair_one, pair_two):
    contract = partial(
        jnp.einsum, equation, precision=lax.Precision.HIGHEST, preferred_element_type=jnp.float32
    )
    return (
        contract(pair_one[0], pair_two[0]) - contract(pair_one[1], pair_two[1]),
        contract(pair_one[0], pair_two[1]) + contract(pair_one[1], pair_two[0]),
    )


def range_compress(signal, reference):
    line_count = signal.shape[1]
    length = signal.shape[2]
    inner = length // RP
    table_outer = fourier_table(RP)
    table_inner = fourier_table(inner)
    twiddle = twiddle_table(RP, inner, length)
    spectrum = (reference[0].reshape(inner, RP).T, reference[1].reshape(inner, RP).T)
    values = (signal[0].reshape(line_count, RP, inner), signal[1].reshape(line_count, RP, inner))
    values = complex_einsum("kp,lpq->lkq", table_outer, values)
    values = complex_scale(values, twiddle)
    values = complex_einsum("lkq,jq->lkj", values, table_inner)
    values = complex_scale(values, spectrum)
    values = complex_einsum("lkj,jq->lkq", values, conjugate(table_inner))
    values = complex_scale(values, conjugate(twiddle))
    values = complex_einsum("pk,lkq->lpq", conjugate(table_outer), values)
    return jnp.stack(
        [component.reshape(line_count, length)[:, :RV] * (1.0 / length) for component in values]
    )


def azimuth_compress(field, reference):
    length = field.shape[1]
    columns = field.shape[2]
    inner = length // AP
    table_outer = fourier_table(AP)
    table_inner = fourier_table(inner)
    twiddle_flat = twiddle_table(AP, inner, length)
    twiddle_wide = (twiddle_flat[0][:, :, None], twiddle_flat[1][:, :, None])
    spectrum = (
        reference[0].reshape(inner, AP).T[:, :, None],
        reference[1].reshape(inner, AP).T[:, :, None],
    )
    values = (field[0].reshape(AP, inner, columns), field[1].reshape(AP, inner, columns))
    values = complex_einsum("kp,pqc->kqc", table_outer, values)
    values = complex_scale(values, twiddle_wide)
    values = complex_einsum("kqc,jq->kjc", values, table_inner)
    values = complex_scale(values, spectrum)
    values = complex_einsum("kjc,jq->kqc", values, conjugate(table_inner))
    values = complex_scale(values, conjugate(twiddle_wide))
    values = complex_einsum("pk,kqc->pqc", conjugate(table_outer), values)
    return tuple((component.reshape(length, columns) * (1.0 / length) for component in values))


def box_filter(padded_grid, rows_out, cols_out):
    total = padded_grid[..., 0:rows_out, 0:cols_out]
    for row_step in range(3):
        for col_step in range(3):
            if row_step + col_step > 0:
                total = (
                    total
                    + padded_grid[
                        ..., row_step : row_step + rows_out, col_step : col_step + cols_out
                    ]
                )
    return total


def local(master_raw, slave_raw, range_ref, az_ref, az_shift, rg_shift, valid_lines):
    master_lines, slave_lines = (
        lax.all_to_all(master_raw, "rg", split_axis=1, concat_axis=2, tiled=True),
        lax.all_to_all(slave_raw, "rg", split_axis=1, concat_axis=2, tiled=True),
    )
    master_range = range_compress(master_lines, range_ref)
    slave_range = range_compress(slave_lines, range_ref)
    az_count = lax.axis_size("az")
    rg_count = lax.axis_size("rg")
    devices = az_count * rg_count
    columns = RV // devices
    lines_here = master_range.shape[1]

    def arrange(field):
        return field.reshape(2, 1, lines_here, devices, columns)

    master_turned, slave_turned = (
        lax.all_to_all(
            arrange(master_range), ("az", "rg"), split_axis=3, concat_axis=1, tiled=True
        ),
        lax.all_to_all(arrange(slave_range), ("az", "rg"), split_axis=3, concat_axis=1, tiled=True),
    )
    master_real, master_imag = azimuth_compress(master_turned.reshape(2, LINES, columns), az_ref)
    slave_focused = jnp.stack(azimuth_compress(slave_turned.reshape(2, LINES, columns), az_ref))
    widened = extended(slave_focused, ((("az", "rg"), 2),), RSH)
    padded = jnp.pad(widened, ((0, 0), (ASH, ASH), (0, 0)))
    blocks_here = columns // BR
    row_start = lax.broadcasted_iota(jnp.int32, (NBA, blocks_here), 0) * BA + ASH + az_shift
    col_start = lax.broadcasted_iota(jnp.int32, (NBA, blocks_here), 1) * BR + RSH + rg_shift

    def cutout(row_begin, col_begin):
        return lax.dynamic_slice(padded, (jnp.int32(0), row_begin, col_begin), (2, BA, BR))

    pieces = jax.vmap(jax.vmap(cutout))(row_start, col_start)
    moved = pieces.transpose(2, 0, 3, 1, 4).reshape(2, LINES, columns)
    flat_index = lax.axis_index(("az", "rg"))
    local_counts = lax.dynamic_slice(
        jnp.pad(valid_lines, 1), (flat_index * blocks_here,), (blocks_here + 2,)
    )
    col_counts = jnp.repeat(local_counts[1:-1], BR)
    valid_mask = (
        lax.broadcasted_iota(jnp.int32, (LINES, columns), 0) < col_counts[None, :]
    ).astype(jnp.float32)
    cross_real = (master_real * moved[0] + master_imag * moved[1]) * valid_mask
    cross_imag = (master_imag * moved[0] - master_real * moved[1]) * valid_mask
    rows_out = LINES // LOOK
    cols_out = columns // LOOK
    looks = (
        jnp.stack([cross_real, cross_imag])
        .reshape(2, rows_out, LOOK, cols_out, LOOK)
        .sum(axis=(2, 4))
    )
    wide_counts = jnp.concatenate(
        [local_counts[:1], jnp.repeat(local_counts[1:-1], BR // LOOK), local_counts[-1:]]
    )
    groups = lax.broadcasted_iota(jnp.int32, (rows_out, cols_out + 2), 0)
    pixels = (jnp.clip(wide_counts[None, :] - LOOK * groups, 0, LOOK) * LOOK).astype(jnp.float32)
    wide_looks = extended(looks, ((("az", "rg"), 2),), 1)
    box = box_filter(jnp.pad(wide_looks, ((0, 0), (1, 1), (0, 0))), rows_out, cols_out)
    box_pixels = box_filter(jnp.pad(pixels, ((1, 1), (0, 0))), rows_out, cols_out)
    return box / jnp.sqrt(jnp.maximum(box_pixels, 1.0))[None]


def solution(mesh):
    return jax.shard_map(
        local,
        mesh=mesh,
        in_specs=(
            P(None, "az", "rg"),
            P(None, "az", "rg"),
            P(),
            P(),
            P(None, ("az", "rg")),
            P(None, ("az", "rg")),
            P(),
        ),
        out_specs=P(None, None, ("az", "rg")),
        check_vma=False,
    )
```

profile of v0, /device:TPU:103, one launch (start us, length us, event | category | flops | bytes accessed | tf_op | source)
XLA Modules:
  0.0 546.5 jit_solution(1606375968032963177)
XLA Ops:
  0.0 6.5 %copy.303 = f32[2,256,1250]{2,0,1:T(2,128)} copy(f32[2,256,1250]{1,0,2:T(2,128)} %param.7) | data formatting | bytes 5120000 | tf_op args[0]
  6.5 6.3 %all-to-all-start = ((f32[2,256,1250]{2,0,1:T(2,128)}), f32[2,256,1250]{2,0,1:T(2,128)S(1)}, u32[]{:S(2)}, u32[]{:S(2)}) async-start(f32[2,256,1250]{2,0,1:T(2,128)} %copy.303), calls=%async_computation | async-start | bytes 5242880 | tf_op jit(solution)/shard_map/all_to_all | solution.py:127
  12.9 6.6 %copy.339 = f32[2,256,1250]{2,0,1:T(2,128)} copy(f32[2,256,1250]{1,0,2:T(2,128)} %param.8) | data formatting | bytes 5120000 | tf_op args[1]
  19.9 27.6 %all-to-all-done = f32[2,256,1250]{2,0,1:T(2,128)S(1)} async-done(((f32[2,256,1250]{2,0,1:T(2,128)}), f32[2,256,1250]{2,0,1:T(2,128)S(1)}, u32[]{:S(2)}, u32[]{:S(2)}) %all-to-all-start) | async-done | bytes 2560032 | tf_op jit(solution)/shard_map/all_to_all | solution.py:127
  47.5 8.8 %all-to-all-start.2 = ((f32[2,256,1250]{2,0,1:T(2,128)}), f32[2,256,1250]{2,0,1:T(2,128)}, u32[]{:S(2)}, u32[]{:S(2)}) async-start(f32[2,256,1250]{2,0,1:T(2,128)} %copy.339), calls=%async_computation.2 | async-start | bytes 5242880 | tf_op jit(solution)/shard_map/all_to_all | solution.py:128
  71.4 17.3 %all-to-all-done.2 = f32[2,256,1250]{2,0,1:T(2,128)} async-done(((f32[2,256,1250]{2,0,1:T(2,128)}), f32[2,256,1250]{2,0,1:T(2,128)}, u32[]{:S(2)}, u32[]{:S(2)}) %all-to-all-start.2) | async-done | bytes 2560032 | tf_op jit(solution)/shard_map/all_to_all | solution.py:128
  125.3 4.5 multiply_subtract_fusion.2
  165.2 3.7 fusion.74
  169.0 3.8 fusion.73
  198.3 13.4 %all-to-all-start.1 = ((f32[2,1,16,128,128]{4,2,0,1,3:T(8,128)}), f32[2,1,16,128,128]{4,2,0,1,3:T(8,128)}, u32[]{:S(2)}, u32[]{:S(2)}) async-start(f32[2,1,16,128,128]{4,2,0,1,3:T(8,128)} %pad_maximum_fusion.1), calls=%async_computation.1 | async-start | bytes 4194304 | tf_op jit(solution)/shard_map/all_to_all | solution.py:142
  211.8 4.3 convolution_subtract_fusion
  239.3 9.9 %all-to-all-start.3 = ((f32[2,1,16,128,128]{4,2,0,1,3:T(8,128)}), f32[2,1,16,128,128]{4,2,0,1,3:T(8,128)S(1)}, u32[]{:S(2)}, u32[]{:S(2)}) async-start(f32[2,1,16,128,128]{4,2,0,1,3:T(8,128)} %pad_maximum_fusion.2), calls=%async_computation.3 | async-start | bytes 4194304 | tf_op jit(solution)/shard_map/all_to_all | solution.py:145
  260.8 14.3 %all-to-all-done.3 = f32[2,1,16,128,128]{4,2,0,1,3:T(8,128)S(1)} async-done(((f32[2,1,16,128,128]{4,2,0,1,3:T(8,128)}), f32[2,1,16,128,128]{4,2,0,1,3:T(8,128)S(1)}, u32[]{:S(2)}, u32[]{:S(2)}) %all-to-all-start.3) | async-done | bytes 2097184 | tf_op jit(solution)/shard_map/all_to_all | solution.py:145
  308.8 5.7 %fusion.41 = (f32[64,32,128]{2,0,1:T(8,128)S(1)}, f32[64,32,128]{2,0,1:T(8,128)S(1)}, f32[64,32,128]{2,0,1:T(8,128)S(1)}, f32[64,32,128]{2,0,1:T(8,128)S(1)}) fusion(f32[64,32]{0,1:T(8,128)S(1)} %fusion.379, f32[64,32]{0,1:T(8,128)S(1)} %get-tuple-element.86, f32[32,64,128]{2,0,1:T(8,128)S(1)} %fusion.84, f32[32,64,128]{2,0,1:T(8,128)S(1)} %fusion.82, ...), kind=kLoop, calls=%fused_computation.88 | loop fusion | flops 4194304 | bytes 12599296 | tf_op jit(solution)/shard_map/sub | solution.py:52
  326.6 6.1 %collective-permute-start = (f32[2,2048,64]{1,2,0:T(8,128)}, f32[2,2048,64]{1,2,0:T(8,128)}, u32[]{:S(2)}, u32[]{:S(2)}) collective-permute-start(f32[2,2048,64]{1,2,0:T(8,128)} %copy.374), channel_id=1, source_target_pairs={{0,1},{1,2},{2,3},{3,4},{4,5},{5,6},{6,7},{7,8},{8,9},{9,10},{10,1... | collective-permute-start | bytes 3145736 | tf_op jit(solution)/shard_map/ppermute | solution.py:28
  341.7 11.9 %mul.1015 = f32[1,256,8,16,8]{4,3,2,1,0:T(8,128)} reshape(f32[64,32,128]{2,1,0:T(8,128)} %copy.338) | data formatting | bytes 2097152 | tf_op jit(solution)/shard_map/mul | solution.py:108
  356.6 11.2 %mul.1050 = f32[1,256,8,16,8]{4,3,2,1,0:T(8,128)} reshape(f32[64,32,128]{2,1,0:T(8,128)S(1)} %copy.382) | data formatting | bytes 2097152 | tf_op jit(solution)/shard_map/mul | solution.py:108
  374.3 5.3 select_maximum_fusion
  379.7 32.4 %while.1 = (s32[]{:T(128)}, f32[2,2112,256]{2,1,0:T(8,128)}, s32[8,3]{1,0:T(8,128)S(1)}, f32[8,2,512,64]{3,2,1,0:T(8,128)}, s32[]{:T(128)}) while((s32[]{:T(128)}, f32[2,2112,256]{2,1,0:T(8,128)}, s32[8,3]{1,0:T(8,128)S(1)}, f32[8,2,512,64]{3,2,1,0:T(8,128)}, s32[]{:T(128)}) %tuple.53), condition=%wide.while_cond, body=%wide.while_body.sunk | while | flops 2 | bytes 1050217 | solution.py:156
  380.3 3.5 bitcast_dynamic-update-slice_fusion.2
  388.4 3.5 bitcast_dynamic-update-slice_fusion.2
  392.5 3.5 bitcast_dynamic-update-slice_fusion.2
  404.5 3.5 bitcast_dynamic-update-slice_fusion.2
  412.0 3.7 copy.380
  417.2 11.9 %squeeze.8 = f32[1,256,8,16,8]{2,1,4,3,0:T(8,128)} reshape(f32[1,4,512,2,64]{2,1,4,3,0:T(4,128)} %get-tuple-element.65) | data formatting | bytes 2097152 | tf_op jit(solution)/shard_map/squeeze | solution.py:168
  429.1 18.8 %copy.381 = f32[1,256,8,16,8]{4,3,2,1,0:T(8,128)} copy(f32[1,256,8,16,8]{2,1,4,3,0:T(8,128)} %squeeze.8) | data formatting | bytes 2097152 | tf_op jit(solution)/shard_map/squeeze | solution.py:168
  447.9 11.2 %squeeze.9 = f32[1,256,8,16,8]{2,1,4,3,0:T(8,128)} reshape(f32[1,4,512,2,64]{2,1,4,3,0:T(4,128)S(1)} %get-tuple-element.66) | data formatting | bytes 2097152 | tf_op jit(solution)/shard_map/squeeze | solution.py:168
  459.1 18.8 %copy.383 = f32[1,256,8,16,8]{4,3,2,1,0:T(8,128)} copy(f32[1,256,8,16,8]{2,1,4,3,0:T(8,128)} %squeeze.9) | data formatting | bytes 2097152 | tf_op jit(solution)/shard_map/squeeze | solution.py:168
  477.9 34.1 %add_select_fusion = (f32[1,256,8,16,8]{4,3,2,1,0:T(8,128)}, f32[1,256,8,16,8]{4,3,2,1,0:T(8,128)}) fusion(f32[1,256,8,16,8]{4,3,2,1,0:T(8,128)} %mul.1050, f32[1,256,8,16,8]{4,3,2,1,0:T(8,128)} %copy.383, f32[1,256,8,16,8]{4,3,2,1,0:T(8,128)} %mul.1015, f32[1,256,8,16,8]{4,3,2,1,0:T(8,128)} %copy.381, s32[16]{0:T(128)S(1)} %broadcast_in_dim.9), kind=kLoop, calls=%fused_computation.4 | loop fusion | flops 2883584 | bytes 6291520 | tf_op jit(solution)/shard_map/mul | solution.py:168
  511.9 12.9 %maximum_reduce_fusion = f32[2,256,16]{2,1,0:T(8,128)S(1)} fusion(f32[1,256,8,16,8]{4,3,2,1,0:T(8,128)} %get-tuple-element.48, f32[1,256,8,16,8]{4,3,2,1,0:T(8,128)} %get-tuple-element.47), kind=kLoop, calls=%fused_computation.2 | loop fusion | flops 1040384 | bytes 2129920 | tf_op jit(solution)/shard_map/reduce_sum | solution.py:175
  525.0 7.7 %collective-permute-start.2 = (f32[2,256,1]{2,1,0:T(8,128)S(1)}, f32[2,256,1]{2,1,0:T(8,128)S(1)}, u32[]{:S(2)}, u32[]{:S(2)}) collective-permute-start(f32[2,256,1]{2,1,0:T(8,128)S(1)} %get-tuple-element.73), channel_id=1, source_target_pairs={{0,1},{1,2},{2,3},{3,4},{4,5},{5,6},{6,7},{7,8},{8,9},{9,10},{10,1... | collective-permute-start | bytes 6152 | tf_op jit(solution)/shard_map/ppermute | solution.py:28
  537.3 7.3 %collective-permute-done.3 = f32[2,256,1]{2,1,0:T(8,128)S(1)} collective-permute-done((f32[2,256,1]{2,1,0:T(8,128)S(1)}, f32[2,256,1]{2,1,0:T(8,128)S(1)}, u32[]{:S(2)}, u32[]{:S(2)}) %collective-permute-start.3) | collective-permute-done | bytes 2080 | tf_op jit(solution)/shard_map/ppermute | solution.py:29
  (233 shorter events, 237.3 us)
Async XLA Ops:
  6.5 41.0 %all-to-all-start = ((f32[2,256,1250]{2,0,1:T(2,128)}), f32[2,256,1250]{2,0,1:T(2,128)S(1)}, u32[]{:S(2)}, u32[]{:S(2)}) async-start(f32[2,256,1250]{2,0,1:T(2,128)} %copy.303), calls=%async_computation | async-start | bytes 5242880 | tf_op jit(solution)/shard_map/all_to_all | solution.py:127
  12.9 6.6 %copy-start.26 = (f32[2,20000]{1,0:T(2,128)S(1)}, f32[2,20000]{1,0:T(2,128)}, u32[]{:S(2)}) copy-start(f32[2,20000]{1,0:T(2,128)} %param.9) | copy-start | bytes 480004
  19.9 36.5 %copy-start.30 = (s32[256]{0:T(256)S(1)}, s32[256]{0:T(256)}, u32[]{:S(2)}) copy-start(s32[256]{0:T(256)} %param.13) | copy-start | bytes 3076
  19.9 37.9 %copy-start.27 = (f32[2,2048]{1,0:T(2,128)S(1)}, f32[2,2048]{1,0:T(2,128)}, u32[]{:S(2)}) copy-start(f32[2,2048]{1,0:T(2,128)} %param.10) | copy-start | bytes 49156
  19.9 38.8 %copy-start.28 = (s32[4,2]{0,1:T(2,128)S(1)}, s32[4,2]{0,1:T(2,128)}, u32[]{:S(2)}) copy-start(s32[4,2]{0,1:T(2,128)} %param.11) | copy-start | bytes 100
  19.9 38.8 %copy-start.29 = (s32[4,2]{0,1:T(2,128)S(1)}, s32[4,2]{0,1:T(2,128)}, u32[]{:S(2)}) copy-start(s32[4,2]{0,1:T(2,128)} %param.12) | copy-start | bytes 100
  47.5 41.2 %all-to-all-start.2 = ((f32[2,256,1250]{2,0,1:T(2,128)}), f32[2,256,1250]{2,0,1:T(2,128)}, u32[]{:S(2)}, u32[]{:S(2)}) async-start(f32[2,256,1250]{2,0,1:T(2,128)} %copy.339), calls=%async_computation.2 | async-start | bytes 5242880 | tf_op jit(solution)/shard_map/all_to_all | solution.py:128
  56.6 90.8 %copy-start.10 = (f32[200,100]{1,0:T(8,128)}, f32[200,100]{1,0:T(8,128)S(1)}, u32[]{:S(2)}) copy-start(f32[200,100]{1,0:T(8,128)S(1)} %reshape_squeeze.42) | copy-start | bytes 240004
  56.8 90.6 %copy-start.13 = (f32[200,100]{1,0:T(8,128)}, f32[200,100]{1,0:T(8,128)S(1)}, u32[]{:S(2)}) copy-start(f32[200,100]{1,0:T(8,128)S(1)} %reshape_squeeze.43) | copy-start | bytes 240004
  100.3 2.8 copy-start.22
  111.3 2.8 copy-start.21
  119.5 5.8 %copy-start.18 = (f32[100,3200]{0,1:S(1)}, f32[100,3200]{0,1}, u32[]{:S(2)}) copy-start(f32[100,3200]{0,1} %fusion.218) | copy-start | bytes 3840004
  122.4 2.9 copy-start.16
  122.4 2.9 copy-start.17
  147.5 25.3 %copy-start = (f32[16,100,200]{1,2,0:T(8,128)}, f32[16,100,200]{1,2,0:T(8,128)S(1)}, u32[]{:S(2)}) copy-start(f32[16,100,200]{1,2,0:T(8,128)S(1)} %convolution_subtract_fusion.1) | copy-start | bytes 3840004
  150.6 22.2 %copy-start.2 = (f32[16,100,200]{1,2,0:T(8,128)}, f32[16,100,200]{1,2,0:T(8,128)S(1)}, u32[]{:S(2)}) copy-start(f32[16,100,200]{1,2,0:T(8,128)S(1)} %convolution_add_fusion.1) | copy-start | bytes 3840004
  162.6 2.6 copy-start.11
  162.6 2.6 copy-start.14
  181.7 3.3 copy-start.20
  183.2 2.3 copy-start.3
  198.3 41.0 %all-to-all-start.1 = ((f32[2,1,16,128,128]{4,2,0,1,3:T(8,128)}), f32[2,1,16,128,128]{4,2,0,1,3:T(8,128)}, u32[]{:S(2)}, u32[]{:S(2)}) async-start(f32[2,1,16,128,128]{4,2,0,1,3:T(8,128)} %pad_maximum_fusion.1), calls=%async_computation.1 | async-start | bytes 4194304 | tf_op jit(solution)/shard_map/all_to_all | solution.py:142
  211.8 4.4 copy-start.12
  211.8 4.4 copy-start.15
  211.8 4.4 copy-start.19
  216.2 4.5 copy-start.4
  239.3 35.8 %all-to-all-start.3 = ((f32[2,1,16,128,128]{4,2,0,1,3:T(8,128)}), f32[2,1,16,128,128]{4,2,0,1,3:T(8,128)S(1)}, u32[]{:S(2)}, u32[]{:S(2)}) async-start(f32[2,1,16,128,128]{4,2,0,1,3:T(8,128)} %pad_maximum_fusion.2), calls=%async_computation.3 | async-start | bytes 4194304 | tf_op jit(solution)/shard_map/all_to_all | solution.py:145
  320.8 2.7 copy-start.8
  326.6 41.2 %collective-permute-start = (f32[2,2048,64]{1,2,0:T(8,128)}, f32[2,2048,64]{1,2,0:T(8,128)}, u32[]{:S(2)}, u32[]{:S(2)}) collective-permute-start(f32[2,2048,64]{1,2,0:T(8,128)} %copy.374), channel_id=1, source_target_pairs={{0,1},{1,2},{2,3},{3,4},{4,5},{5,6},{6,7},{7,8},{8,9},{9,10},{10,1... | collective-permute-start | bytes 3145736 | tf_op jit(solution)/shard_map/ppermute | solution.py:28
  335.8 35.2 %collective-permute-start.1 = (f32[2,2048,64]{1,2,0:T(8,128)}, f32[2,2048,64]{1,2,0:T(8,128)}, u32[]{:S(2)}, u32[]{:S(2)}) collective-permute-start(f32[2,2048,64]{1,2,0:T(8,128)} %copy.375), channel_id=1, source_target_pairs={{1,0},{2,1},{3,2},{4,3},{5,4},{6,5},{7,6},{8,7},{9,8},{10,9},{11,1... | collective-permute-start | bytes 3145736 | tf_op jit(solution)/shard_map/ppermute | solution.py:29
  371.0 3.3 copy-start.9
  525.0 12.3 %collective-permute-start.2 = (f32[2,256,1]{2,1,0:T(8,128)S(1)}, f32[2,256,1]{2,1,0:T(8,128)S(1)}, u32[]{:S(2)}, u32[]{:S(2)}) collective-permute-start(f32[2,256,1]{2,1,0:T(8,128)S(1)} %get-tuple-element.73), channel_id=1, source_target_pairs={{0,1},{1,2},{2,3},{3,4},{4,5},{5,6},{6,7},{7,8},{8,9},{9,10},{10,1... | collective-permute-start | bytes 6152 | tf_op jit(solution)/shard_map/ppermute | solution.py:28
  532.7 11.9 %collective-permute-start.3 = (f32[2,256,1]{2,1,0:T(8,128)S(1)}, f32[2,256,1]{2,1,0:T(8,128)S(1)}, u32[]{:S(2)}, u32[]{:S(2)}) collective-permute-start(f32[2,256,1]{2,1,0:T(8,128)S(1)} %get-tuple-element.74), channel_id=1, source_target_pairs={{1,0},{2,1},{3,2},{4,3},{5,4},{6,5},{7,6},{8,7},{9,8},{10,9},{11,1... | collective-permute-start | bytes 6152 | tf_op jit(solution)/shard_map/ppermute | solution.py:29
  (7 other events, 12.2 us)
where the time goes:
time: 557 us; the launch traced here: 547 us
  local copies, waits for them, and re-layouts  206 us (37%)
  matrix products  139 us (25%)
  other arithmetic  74.8 us (13%)
  waiting for transfers between devices  68.9 us (12%)
  starting transfers between devices  56.1 us (10%)
    squeeze x4, local copies, waits for them, and re-layouts, local(): cross_real = (master_real * moved[0] + master_imag * moved[1]) * valid_mask  60.7 us
    mul x1, other arithmetic, local(): cross_real = (master_real * moved[0] + master_imag * moved[1]) * valid_mask  34.1 us
    gather x24, local copies, waits for them, and re-layouts  32.4 us
    dot_general x14, matrix products, complex_einsum(): contract(pair_one[1], pair_two[0])  30.3 us
    dot_general x14, matrix products, complex_einsum(): contract(pair_one[1], pair_two[1])  30 us
    dot_general x14, matrix products, complex_einsum(): contract(pair_one[0], pair_two[1]) + contract(pair_one[1], pair_two[0])  28.7 us
    all_to_all x1, waiting for transfers between devices, local(): lax.all_to_all(master_raw, 'rg', split_axis=1, concat_axis=2, tiled=True)  27.6 us
    dot_general x14, matrix products, complex_einsum(): contract(pair_one[0], pair_two[0]) - contract(pair_one[1], pair_two[1])  26.9 us
  transfers between devices with their start and end apart: 8, of which 5 were waited for; matrix products, arithmetic and copies ran while one was open for 18% of the time, Pallas kernels for 0%

commit v1 on v0

v1 whole, which is shorter than its diff:
```python
import math

import jax
import jax.numpy as jnp
import numpy as np
from jax import lax
from jax.experimental import pallas as pl
from jax.experimental.pallas import tpu as pltpu
from jax.sharding import PartitionSpec as P

LINES = 2048
RANGE = 20000
RV = 16384
LOOK = 8
BA = 512
BR = 64
ASH = 32
RSH = 64
NBA = 4
ALL = ("az", "rg")
NP = 16
NQ = 10
NS = 125
RPAD = 1280
F32 = jnp.float32
BF16 = jnp.bfloat16


def _rot(v, angle):
    c, s = math.cos(angle), math.sin(angle)
    turns = angle / (math.pi / 4)
    eighth = round(turns)
    x, y = v
    if abs(turns - eighth) < 1e-9:
        e = eighth % 8
        if e == 0:
            return v
        if e == 2:
            return (-y, x)
        if e == 4:
            return (-x, -y)
        if e == 6:
            return (y, -x)
        h = math.sqrt(0.5)
        if e == 1:
            return ((x - y) * h, (x + y) * h)
        if e == 3:
            return (-(x + y) * h, (x - y) * h)
        if e == 5:
            return ((y - x) * h, -(x + y) * h)
        return ((x + y) * h, (y - x) * h)
    return (x * c - y * s, x * s + y * c)


def _add(a, b):
    return (a[0] + b[0], a[1] + b[1])


def _sub(a, b):
    return (a[0] - b[0], a[1] - b[1])


def _dft2(v, sign):
    return [_add(v[0], v[1]), _sub(v[0], v[1])]


def _dft4(v, sign):
    a, b = _add(v[0], v[2]), _sub(v[0], v[2])
    c, d = _add(v[1], v[3]), _sub(v[1], v[3])
    if sign < 0:
        return [_add(a, c), (b[0] + d[1], b[1] - d[0]), _sub(a, c), (b[0] - d[1], b[1] + d[0])]
    return [_add(a, c), (b[0] - d[1], b[1] + d[0]), _sub(a, c), (b[0] + d[1], b[1] - d[0])]


def _dft5(v, sign):
    c1, c2 = math.cos(2 * math.pi / 5), math.cos(4 * math.pi / 5)
    s1, s2 = sign * math.sin(2 * math.pi / 5), sign * math.sin(4 * math.pi / 5)
    a1, b1 = _add(v[1], v[4]), _sub(v[1], v[4])
    a2, b2 = _add(v[2], v[3]), _sub(v[2], v[3])
    x0 = v[0]
    y0 = (x0[0] + a1[0] + a2[0], x0[1] + a1[1] + a2[1])
    p1 = tuple(x0[i] + c1 * a1[i] + c2 * a2[i] for i in range(2))
    p2 = tuple(x0[i] + c2 * a1[i] + c1 * a2[i] for i in range(2))
    q1 = tuple(s1 * b1[i] + s2 * b2[i] for i in range(2))
    q2 = tuple(s2 * b1[i] - s1 * b2[i] for i in range(2))
    return [
        y0,
        (p1[0] - q1[1], p1[1] + q1[0]),
        (p2[0] - q2[1], p2[1] + q2[0]),
        (p2[0] + q2[1], p2[1] - q2[0]),
        (p1[0] + q1[1], p1[1] - q1[0]),
    ]


def _dft_two(v, n1, n2, first, second, sign):
    n = n1 * n2
    out = [None] * n
    mid = []
    for b in range(n2):
        col = first([v[n2 * a + b] for a in range(n1)], sign)
        mid.append([_rot(col[k], sign * 2 * math.pi * ((b * k) % n) / n) for k in range(n1)])
    for k1 in range(n1):
        row = second([mid[b][k1] for b in range(n2)], sign)
        for k2 in range(n2):
            out[k1 + n1 * k2] = row[k2]
    return out


def dft16(v, sign):
    return _dft_two(v, 4, 4, _dft4, _dft4, sign)


def dft10(v, sign):
    return _dft_two(v, 2, 5, _dft2, _dft5, sign)


def cmul(a, b):
    return (a[0] * b[0] - a[1] * b[1], a[0] * b[1] + a[1] * b[0])


def split(x):
    hi = x.astype(BF16)
    return hi, (x - hi.astype(F32)).astype(BF16)


def dot(a, b):
    return jnp.dot(a, b, preferred_element_type=F32)


def _np_split(x):
    x = np.asarray(x, np.float32)
    hi = x.astype(BF16)
    return hi, (x - hi.astype(np.float32)).astype(BF16)


def _tables():
    t = {}
    two = 2 * np.pi
    q = np.arange(RPAD)
    ang = -two * ((np.arange(NP)[:, None] * q[None, :]) % RANGE) / RANGE
    t["twa"] = np.stack([np.cos(ang), np.sin(ang)], 1).astype(np.float32)
    q2 = np.arange(128)
    keep = (q2 < NS)[None, :]
    ang = -two * ((np.arange(NQ)[:, None] * q2[None, :]) % 1250) / 1250
    t["twb"] = np.stack([np.cos(ang) * keep, np.sin(ang) * keep], 1).astype(np.float32)
    n = np.arange(NQ)[None, :, None] * NS + q2[None, None, :]
    ang = two * ((np.arange(NP)[:, None, None] * n) % RANGE) / RANGE
    t["twc"] = (
        (np.stack([np.cos(ang), np.sin(ang)], 2) / RANGE)
        .reshape(NP * NQ, 2, 128)
        .astype(np.float32)
    )
    ang = two * ((q2[:, None] * q2[None, :]) % NS) / NS
    both = keep & keep.T
    c, s = np.cos(ang) * both, np.sin(ang) * both
    t["fh"], t["fl"] = _np_split(np.block([[c, -s], [s, c]]))
    t["gh"], t["gl"] = _np_split(np.block([[c, s], [-s, c]]))
    k2 = np.arange(128)
    l2 = np.arange(128)
    ang = -two * ((l2[:, None] * k2[None, :]) % 128) / 128
    pr, pi = np.cos(ang), np.sin(ang)
    ang = np.broadcast_to(-two * l2[:, None] / LINES, (128, 128))
    wr, wi = np.cos(ang), np.sin(ang)
    t["p"] = np.stack([pr, pi]).astype(np.float32)
    t["w"] = np.stack([wr, wi]).astype(np.float32)
    kk = np.arange(256)
    part, line = (kk // 16) % 2, (kk // 32) * 16 + kk % 16
    sel = (part == 0)[:, None]
    t["q"] = np.stack(
        [np.where(sel, pr[line], -pi[line]), np.where(sel, -pi[line], -pr[line])]
    ).astype(np.float32)
    t["v"] = np.stack([wr[line], wi[line]]).astype(np.float32)
    lane = np.arange(128)
    band = np.zeros((128, 128), np.float32)
    for o in range(16):
        band[:, o] = np.abs(lane // LOOK - o) <= 1
    t["band"] = band
    edge = np.zeros((4, 8, 128), np.float32)
    for part in range(2):
        edge[part, part] = lane < LOOK
        edge[2 + part, part] = lane >= 128 - LOOK
    t["edge"] = edge
    return t


TABLES = _tables()


def _pre_kernel(x_ref, o_ref):
    for part in range(2):
        o_ref[0, part, :, 0:1152] = x_ref[part, :, 0:1152]
        tail = x_ref[part, :, 1152:1250]
        o_ref[0, part, :, 1152:1280] = jnp.concatenate([tail, jnp.zeros((16, 30), F32)], axis=1)


def pre(raw):
    return pl.pallas_call(
        _pre_kernel,
        grid=(NP,),
        in_specs=[pl.BlockSpec((2, 16, 1250), lambda i: (0, i, 0))],
        out_specs=pl.BlockSpec((1, 2, 16, RPAD), lambda i: (i, 0, 0, 0)),
        out_shape=jax.ShapeDtypeStruct((NP, 2, 16, RPAD), F32),
        cost_estimate=pl.CostEstimate(flops=10**8, bytes_accessed=5 * 10**6, transcendentals=0),
        name="pre",
    )(raw)


def _range_kernel(x_ref, twa_ref, twb_ref, hf_ref, fh_ref, fl_ref, gh_ref, gl_ref, twc_ref, o_ref, b_ref, d_ref):
    lane = lax.broadcasted_iota(jnp.int32, (16, 128), 1)

    def outer(j, carry):
        lanes = pl.ds(pl.multiple_of(j * 128, 128), 128)
        for g in range(2):
            rows = slice(8 * g, 8 * g + 8)
            v = [(x_ref[p, 0, rows, lanes], x_ref[p, 1, rows, lanes]) for p in range(NP)]
            v = dft16(v, -1)
            for k in range(NP):
                tw = (twa_ref[k, 0:1, lanes], twa_ref[k, 1:2, lanes])
                r, i = cmul(v[k], tw)
                b_ref[k, 0, rows, lanes] = r
                b_ref[k, 1, rows, lanes] = i
        return carry

    lax.fori_loop(0, RPAD // 128, outer, 0)

    def middle(kp, carry):
        chunks = []
        for q in range(NQ):
            pair = []
            for c in range(2):
                here = b_ref[kp, c, :, 128 * q : 128 * q + 128]
                if q:
                    prev = b_ref[kp, c, :, 128 * q - 128 : 128 * q]
                    here = jnp.where(
                        lane < 3 * q, pltpu.roll(prev, 3 * q, 1), pltpu.roll(here, 3 * q, 1)
                    )
                pair.append(here)
            chunks.append(tuple(pair))
        v = dft10(chunks, -1)
        rows = []
        for k in range(NQ):
            r, i = cmul(v[k], (twb_ref[k, 0:1, :], twb_ref[k, 1:2, :]))
            rows.append(jnp.concatenate([r, i], axis=1))
        hi, lo = split(jnp.concatenate(rows, axis=0))
        y = dot(hi, fh_ref[...]) + dot(lo, fh_ref[...]) + dot(hi, fl_ref[...])
        rows = []
        for k in range(NQ):
            val = (y[16 * k : 16 * k + 16, :128], y[16 * k : 16 * k + 16, 128:])
            r, i = cmul(val, (hf_ref[kp * NQ + k, 0:1, :], hf_ref[kp * NQ + k, 1:2, :]))
            rows.append(jnp.concatenate([r, i], axis=1))
        hi, lo = split(jnp.concatenate(rows, axis=0))
        y = dot(hi, gh_ref[...]) + dot(lo, gh_ref[...]) + dot(hi, gl_ref[...])
        v = []
        for k in range(NQ):
            val = (y[16 * k : 16 * k + 16, :128], y[16 * k : 16 * k + 16, 128:])
            v.append(cmul(val, (twb_ref[k, 0:1, :], -twb_ref[k, 1:2, :])))
        v = dft10(v, 1)
        for q in range(NQ):
            tw = (twc_ref[kp * NQ + q, 0:1, :], twc_ref[kp * NQ + q, 1:2, :])
            r, i = cmul(v[q], tw)
            d_ref[kp * NQ + q, 0] = r
            d_ref[kp * NQ + q, 1] = i
        return carry

    lax.fori_loop(0, NP, middle, 0)

    def inner(q, carry):
        for g in range(2):
            rows = slice(8 * g, 8 * g + 8)
            v = [(d_ref[k * NQ + q, 0, rows, :], d_ref[k * NQ + q, 1, rows, :]) for k in range(NP)]
            v = dft16(v, 1)
            for p in range(14):
                d_ref[p * NQ + q, 0, rows, :] = v[p][0]
                d_ref[p * NQ + q, 1, rows, :] = v[p][1]
        return carry

    lax.fori_loop(0, NQ, inner, 0)

    for d in range(128):
        n, a = divmod(128 * d, NS)
        for c in range(2):
            val = d_ref[n, c]
            if a:
                val = pltpu.roll(val, 128 - a, 1)
            start = NS - a
            while start < 128:
                n2 = (128 * d + start) // NS
                nxt = d_ref[n2, c]
                nxt = pltpu.roll(nxt, start % 128, 1)
                val = jnp.where(lane < start, val, nxt)
                start += NS
            o_ref[d, c] = val


def range_compress(x, hf):
    t = TABLES
    return pl.pallas_call(
        _range_kernel,
        out_shape=jax.ShapeDtypeStruct((128, 2, 16, 128), F32),
        scratch_shapes=[
            pltpu.VMEM((NP, 2, 16, RPAD), F32),
            pltpu.VMEM((NP * NQ, 2, 16, 128), F32),
        ],
        cost_estimate=pl.CostEstimate(flops=10**10, bytes_accessed=6 * 10**6, transcendentals=0),
        name="range",
    )(x, t["twa"], t["twb"], hf, t["fh"], t["fl"], t["gh"], t["gl"], t["twc"])


def _dot_t(a, b):
    return lax.dot_general(
        a, b, (((1,), (1,)), ((), ())), precision=lax.Precision.HIGHEST, preferred_element_type=F32
    )


def _prep_kernel(h_ref, p0_ref, w_ref, q0_ref, v_ref, ah_ref, al_ref, p_ref, q_ref):
    p_ref[...] = p0_ref[...]
    q_ref[...] = q0_ref[...]

    def body(k, carry):
        pr, pi = p_ref[0], p_ref[1]
        q1, q2 = q_ref[0], q_ref[1]
        hr, hi = h_ref[k, 0:1, :], h_ref[k, 1:2, :]
        vr, vi = cmul((pr, -pi), (hr, hi))
        top = _dot_t(vr, q1) + _dot_t(vi, q2)
        bottom = _dot_t(vi, q1) - _dot_t(vr, q2)
        high, low = split(top)
        ah_ref[k, 0:128, :] = high
        al_ref[k, 0:128, :] = low
        high, low = split(bottom)
        ah_ref[k, 128:256, :] = high
        al_ref[k, 128:256, :] = low
        pr, pi = cmul((pr, pi), (w_ref[0], w_ref[1]))
        p_ref[0] = pr
        p_ref[1] = pi
        wr, wi = v_ref[0], v_ref[1]
        q_ref[0] = q1 * wr + q2 * wi
        q_ref[1] = q2 * wr - q1 * wi
        return carry

    lax.fori_loop(0, 16, body, 0)


def prep(h):
    t = TABLES
    shape = jax.ShapeDtypeStruct((16, 256, 256), BF16)
    return pl.pallas_call(
        _prep_kernel,
        out_shape=(shape, shape),
        scratch_shapes=[pltpu.VMEM((2, 128, 128), F32), pltpu.VMEM((2, 256, 128), F32)],
        cost_estimate=pl.CostEstimate(flops=5 * 10**9, bytes_accessed=5 * 10**6, transcendentals=0),
        name="prep",
    )(h, t["p"], t["w"], t["q"], t["v"])


def _azimuth_front(x_ref, ah_ref, al_ref, e_ref):
    def first(s, carry):
        for g in range(2):
            rows = slice(8 * g, 8 * g + 8)
            v = [(x_ref[8 * a + s, 0, rows, :], x_ref[8 * a + s, 1, rows, :]) for a in range(16)]
            v = dft16(v, -1)
            for k in range(16):
                for c in range(2):
                    at = pl.multiple_of(s * 32 + c * 16 + g * 8, 8)
                    e_ref[k, pl.ds(at, 8), :] = v[k][c]
        return carry

    lax.fori_loop(0, 8, first, 0)

    def second(k, carry):
        hi, lo = split(e_ref[k])
        wide = dot(ah_ref[k], jnp.concatenate([hi, lo], axis=1))
        e_ref[k] = wide[:, :128] + wide[:, 128:] + dot(al_ref[k], hi)
        return carry

    lax.fori_loop(0, 16, second, 0)


def _azimuth_rows(e_ref, g):
    at = [pl.multiple_of(c * 128 + g * 8, 8) for c in range(2)]
    v = [(e_ref[k, pl.ds(at[0], 8), :], e_ref[k, pl.ds(at[1], 8), :]) for k in range(16)]
    return dft16(v, 1)


def _slave_kernel(x_ref, ah_ref, al_ref, o_ref, left_ref, right_ref, e_ref):
    _azimuth_front(x_ref, ah_ref, al_ref, e_ref)
    low = lax.broadcasted_iota(jnp.int32, (8, 128), 1) < 64

    def third(g, carry):
        v = _azimuth_rows(e_ref, g)
        for a in range(16):
            rows = pl.ds(pl.multiple_of(a * 128 + g * 8, 8), 8)
            r, i = v[a]
            o_ref[0, rows, :] = r
            o_ref[1, rows, :] = i
            left_ref[rows, :] = jnp.where(low, r, pltpu.roll(i, 64, 1))
            right_ref[rows, :] = jnp.where(low, pltpu.roll(r, 64, 1), i)
        return carry

    lax.fori_loop(0, 16, third, 0)


def slave_azimuth(x, ah, al):
    side = jax.ShapeDtypeStruct((LINES, 128), F32)
    return pl.pallas_call(
        _slave_kernel,
        out_shape=(jax.ShapeDtypeStruct((2, LINES, 128), F32), side, side),
        scratch_shapes=[pltpu.VMEM((16, 256, 128), F32)],
        cost_estimate=pl.CostEstimate(flops=5 * 10**9, bytes_accessed=10**7, transcendentals=0),
        name="slave_azimuth",
    )(x, ah, al)


def _resample_kernel(az_ref, rg_ref, s_ref, left_ref, right_ref, o_ref, w_ref):
    lane = lax.broadcasted_iota(jnp.int32, (64, 128), 1)
    low = lane < 64
    for i in range(4):
        w_ref[i, 0:ASH, :] = jnp.zeros((ASH, 128), F32)
        w_ref[i, ASH + LINES : 2 * ASH + LINES, :] = jnp.zeros((ASH, 128), F32)

    def fill(t, carry):
        rows = pl.ds(pl.multiple_of(t * 64, 64), 64)
        at = pl.ds(pl.multiple_of(t * 64 + ASH, 32), 64)
        sr = pltpu.roll(s_ref[0, rows, :], 64, 1)
        si = pltpu.roll(s_ref[1, rows, :], 64, 1)
        left, right = left_ref[rows, :], right_ref[rows, :]
        w_ref[0, at, :] = jnp.where(low, left, sr)
        w_ref[1, at, :] = jnp.where(low, pltpu.roll(left, 64, 1), si)
        w_ref[2, at, :] = jnp.where(low, sr, pltpu.roll(right, 64, 1))
        w_ref[3, at, :] = jnp.where(low, si, right)
        return carry

    lax.fori_loop(0, LINES // 64, fill, 0)

    def move(t, carry):
        block = t // 8
        parts = []
        for r in range(2):
            start = t * 64 + ASH + az_ref[block, r]
            shift = RSH + rg_ref[block, r]
            back = lax.rem(256 - shift, 128)
            rows = pl.ds(start, 64)
            near = lane + shift < 128
            parts.append(
                [
                    jnp.where(
                        near,
                        pltpu.roll(w_ref[c, rows, :], back, 1),
                        pltpu.roll(w_ref[2 + c, rows, :], back, 1),
                    )
                    for c in range(2)
                ]
            )
        rows = pl.ds(pl.multiple_of(t * 64, 64), 64)
        for c in range(2):
            o_ref[c, rows, :] = jnp.where(low, parts[0][c], parts[1][c])
        return carry

    lax.fori_loop(0, LINES // 64, move, 0)


def resample(az_shift, rg_shift, focused, left, right):
    return pl.pallas_call(
        _resample_kernel,
        in_specs=[pl.BlockSpec(memory_space=pltpu.SMEM)] * 2
        + [pl.BlockSpec(memory_space=pltpu.VMEM)] * 3,
        out_shape=jax.ShapeDtypeStruct((2, LINES, 128), F32),
        scratch_shapes=[pltpu.VMEM((4, LINES + 2 * ASH, 128), F32)],
        cost_estimate=pl.CostEstimate(flops=2 * 10**9, bytes_accessed=10**7, transcendentals=0),
        name="resample",
    )(az_shift, rg_shift, focused, left, right)


def _master_kernel(x_ref, ah_ref, al_ref, m_ref, n_ref, band_ref, edge_ref, box_ref, left_ref, right_ref, e_ref, c_ref):
    _azimuth_front(x_ref, ah_ref, al_ref, e_ref)
    line = lax.broadcasted_iota(jnp.int32, (8, 128), 0)
    count = n_ref[...]

    def third(g, carry):
        v = _azimuth_rows(e_ref, g)
        for a in range(16):
            at = pl.multiple_of(a * 128 + g * 8, 8)
            r, i = v[a]
            sr, si = m_ref[0, pl.ds(at, 8), :], m_ref[1, pl.ds(at, 8), :]
            keep = line + at < count
            c_ref[pl.ds(at, 8), :] = jnp.where(keep, r * sr + i * si, 0.0)
            c_ref[pl.ds(at + LINES, 8), :] = jnp.where(keep, i * sr - r * si, 0.0)
        return carry

    lax.fori_loop(0, 16, third, 0)
    total = c_ref[pl.ds(0, 512, stride=LOOK), :]
    for j in range(1, LOOK):
        total = total + c_ref[pl.ds(j, 512, stride=LOOK), :]
    parts = (total[:256], total[256:])
    for c in range(2):
        box_ref[c] = jnp.dot(
            parts[c], band_ref[...], precision=lax.Precision.HIGHEST, preferred_element_type=F32
        )
    left_ref[...] = _dot_t(edge_ref[0], parts[0]) + _dot_t(edge_ref[1], parts[1])
    right_ref[...] = _dot_t(edge_ref[2], parts[0]) + _dot_t(edge_ref[3], parts[1])


def master_looks(x, ah, al, moved, counts):
    t = TABLES
    side = jax.ShapeDtypeStruct((8, 256), F32)
    return pl.pallas_call(
        _master_kernel,
        out_shape=(jax.ShapeDtypeStruct((2, 256, 128), F32), side, side),
        scratch_shapes=[pltpu.VMEM((16, 256, 128), F32), pltpu.VMEM((2 * LINES, 128), F32)],
        cost_estimate=pl.CostEstimate(flops=5 * 10**9, bytes_accessed=10**7, transcendentals=0),
        name="master_looks",
    )(x, ah, al, moved, counts, t["band"], t["edge"])


def _final_kernel(box_ref, left_ref, right_ref, scale_ref, o_ref):
    row = lax.broadcasted_iota(jnp.int32, (256, 128), 0)
    sub = lax.broadcasted_iota(jnp.int32, (8, 128), 0)
    lane = lax.broadcasted_iota(jnp.int32, (8, 128), 1)
    for c in range(2):
        put = [
            jnp.where((sub == c) & (lane == at), 1.0, 0.0).astype(F32) for at in (0, 15)
        ]
        x = box_ref[c]
        for ref, onto in ((left_ref, put[0]), (right_ref, put[1])):
            x = x + lax.dot_general(
                ref[...],
                onto,
                (((0,), (0,)), ((), ())),
                precision=lax.Precision.HIGHEST,
                preferred_element_type=F32,
            )
        up = jnp.where(row == 0, 0.0, pltpu.roll(x, 1, 0))
        down = jnp.where(row == 255, 0.0, pltpu.roll(x, 255, 0))
        o_ref[c] = (x + up + down)[:, :16] * scale_ref[...]


def final(box, left, right, scale):
    return pl.pallas_call(
        _final_kernel,
        out_shape=jax.ShapeDtypeStruct((2, 256, 16), F32),
        name="final",
    )(box, left, right, scale)


def neighbours(first, second):
    devices = lax.axis_size(ALL)
    up = [(i, i + 1) for i in range(devices - 1)]
    down = [(j, i) for i, j in up]
    return lax.ppermute(first, ALL, up), lax.ppermute(second, ALL, down)


def local(master_raw, slave_raw, range_ref, az_ref, az_shift, rg_shift, valid_lines):
    hf = range_ref.reshape(2, NS, NQ, NP).transpose(3, 2, 0, 1).reshape(NP * NQ, 2, NS)
    hf = jnp.pad(hf, ((0, 0), (0, 0), (0, 3)))
    h = az_ref.reshape(2, 128, 16).transpose(2, 0, 1) * (1.0 / LINES)

    def lines_of(raw):
        return lax.all_to_all(pre(raw), "rg", 0, 0, tiled=True)

    def columns_of(ranged):
        return lax.all_to_all(ranged, ALL, 0, 0, tiled=True)

    slave = lines_of(slave_raw)
    master = lines_of(master_raw)
    slave = columns_of(range_compress(slave, hf))
    master = columns_of(range_compress(master, hf))
    ah, al = prep(h)
    focused, to_left, to_right = slave_azimuth(slave, ah, al)
    from_left, from_right = neighbours(to_right, to_left)
    moved = resample(az_shift, rg_shift, focused, from_left, from_right)

    flat = lax.axis_index(ALL)
    counts = lax.dynamic_slice(jnp.pad(valid_lines, 1), (flat * 2,), (4,))
    col_counts = jnp.repeat(counts[1:3], BR)[None, :]
    wide = jnp.concatenate([counts[:1], jnp.repeat(counts[1:3], BR // LOOK), counts[3:]])
    rows = LINES // LOOK
    groups = lax.broadcasted_iota(jnp.int32, (rows + 2, 18), 0) - 1
    pixels = jnp.clip(wide[None, :] - LOOK * groups, 0, LOOK) * LOOK
    pixels = jnp.where((groups >= 0) & (groups < rows), pixels, 0).astype(F32)
    box_pixels = sum(pixels[i : i + rows, j : j + 16] for i in range(3) for j in range(3))
    scale = 1.0 / jnp.sqrt(jnp.maximum(box_pixels, 1.0))

    box, edge_left, edge_right = master_looks(master, ah, al, moved, col_counts)
    left, right = neighbours(edge_right, edge_left)
    return final(box, left, right, scale)


def solution(mesh):
    return jax.shard_map(
        local,
        mesh=mesh,
        in_specs=(
            P(None, "az", "rg"),
            P(None, "az", "rg"),
            P(),
            P(),
            P(None, ALL),
            P(None, ALL),
            P(),
        ),
        out_specs=P(None, None, ALL),
        check_vma=False,
    )
```

time: 557 us -> 245 us (0.44); the launches traced: 547 us -> 244 us
  local copies, waits for them, and re-layouts: 206 us -> 23 us
  matrix products: 139 us -> 0 us
  Pallas kernels: 0 us -> 101 us
  other arithmetic: 74.8 us -> 2.48 us
  starting transfers between devices: 56.1 us -> 46.7 us
    dot_general x56 -> x0, matrix products: 116 us -> none  [the longest x14 30.3 us: complex_einsum(): contract(pair_one[1], pair_two[0])]
    pallas_call x0 -> x9, Pallas kernels: none -> 101 us  [the longest x2 33.5 us: range_compress(): pl.pallas_call(_range_kernel, out_shape=jax.ShapeDtypeStruct((128, 2, 16,...]
    squeeze x4 -> x0, local copies, waits for them, and re-layouts: 60.7 us -> none  [local(): cross_real = (master_real * moved[0] + master_imag * moved[1]) * valid_mask]
    gather x25 -> x0, local copies, waits for them, and re-layouts: 36.1 us -> none
    mul x2, other arithmetic: 34.1 us -> 0.01 us  [the longest x1 0.01 us: local(): h = az_ref.reshape(2, 128, 16).transpose(2, 0, 1) * (1.0 / LINES)]
    mul x6 -> x2, local copies, waits for them, and re-layouts: 26.6 us -> 0.78 us  [local(): h = az_ref.reshape(2, 128, 16).transpose(2, 0, 1) * (1.0 / LINES)]
    another operation x18 -> x1, local copies, waits for them, and re-layouts: 23.7 us -> 0.67 us  [local(): col_counts = jnp.repeat(counts[1:3], BR)[None, :]]
    unnamed x8 -> x0, matrix products: 22.9 us -> none
  transfers between devices with their start and end apart: 8 -> 8, of which waited for: 5 -> 6; matrix products, arithmetic and copies ran while one was open for 18% -> 6% of each run, Pallas kernels for 0% -> 32%
where the time goes in v1:
time: 245 us; the launch traced here: 244 us
  Pallas kernels  101 us (41%)
  waiting for transfers between devices  70.4 us (29%)
  starting transfers between devices  46.7 us (19%)
  local copies, waits for them, and re-layouts  23 us (9%)
  other arithmetic  2.48 us (1%)
    pallas_call x2, Pallas kernels, range_compress(): pl.pallas_call(_range_kernel, out_shape=jax.ShapeDtypeStruct((128, 2, 16,...  33.5 us
    all_to_all x2, waiting for transfers between devices, lines_of(): return lax.all_to_all(pre(raw), 'rg', 0, 0, tiled=True)  33.2 us
    ppermute x4, waiting for transfers between devices, neighbours(): return (lax.ppermute(first, ALL, up), lax.ppermute(second, ALL, down))  28.7 us
    all_to_all x2, starting transfers between devices, columns_of(): return lax.all_to_all(ranged, ALL, 0, 0, tiled=True)  21 us
    pallas_call x2, Pallas kernels, pre(): pl.pallas_call(_pre_kernel, grid=(NP,), in_specs=[pl.BlockSpec((2, 16, 12...  19.4 us
    unnamed x26, local copies, waits for them, and re-layouts  16.7 us
    all_to_all x2, starting transfers between devices, lines_of(): return lax.all_to_all(pre(raw), 'rg', 0, 0, tiled=True)  15.1 us
    pallas_call x1, Pallas kernels, prep(): pl.pallas_call(_prep_kernel, out_shape=(shape, shape), scratch_shapes=[pl...  13.3 us
  transfers between devices with their start and end apart: 8, of which 6 were waited for; matrix products, arithmetic and copies ran while one was open for 6% of the time, Pallas kernels for 32%

profile of v1, /device:TPU:103, one launch (start us, length us, event | category | flops | bytes accessed | tf_op | source)
XLA Modules:
  0.0 243.7 jit_solution(6247053190241391752)
XLA Ops:
  0.0 5.2 %copy.30.x_ref = f32[2,256,1250]{2,1,0:T(8,128)} copy(f32[2,256,1250]{1,0,2:T(2,128)} %param.21) | data formatting | bytes 5120000 | tf_op args[1]
  5.2 9.7 %pre.3 = f32[16,2,16,1280]{3,2,1,0:T(8,128)} custom-call(f32[2,256,1250]{2,1,0:T(8,128)} %copy.30.x_ref), custom_call_target="tpu_custom_call" | custom-call | flops 100000000 | bytes 5000000 | tf_op jit(solution)/shard_map/pre/pallas_call | solution.py:197
  14.9 6.3 %all-to-all-start.2 = ((f32[16,2,16,1280]{3,2,1,0:T(8,128)}), f32[16,2,16,1280]{3,2,1,0:T(8,128)S(1)}, u32[]{:S(2)}, u32[]{:S(2)}) async-start(f32[16,2,16,1280]{3,2,1,0:T(8,128)} %pre.3), calls=%async_computation.2 | async-start | bytes 5242880 | tf_op jit(solution)/shard_map/all_to_all | solution.py:557
  21.3 5.2 %copy.27.x_ref = f32[2,256,1250]{2,1,0:T(8,128)} copy(f32[2,256,1250]{1,0,2:T(2,128)} %param.20) | data formatting | bytes 5120000 | tf_op args[0]
  26.5 9.7 %pre.2 = f32[16,2,16,1280]{3,2,1,0:T(8,128)} custom-call(f32[2,256,1250]{2,1,0:T(8,128)} %copy.27.x_ref), custom_call_target="tpu_custom_call" | custom-call | flops 100000000 | bytes 5000000 | tf_op jit(solution)/shard_map/pre/pallas_call | solution.py:197
  36.1 19.8 %all-to-all-done.2.x_ref = f32[16,2,16,1280]{3,2,1,0:T(8,128)S(1)} async-done(((f32[16,2,16,1280]{3,2,1,0:T(8,128)}), f32[16,2,16,1280]{3,2,1,0:T(8,128)S(1)}, u32[]{:S(2)}, u32[]{:S(2)}) %all-to-all-start.2) | async-done | bytes 2621472 | tf_op jit(solution)/shard_map/all_to_all | solution.py:557
  55.9 1.5 copy-done
  57.4 8.8 %all-to-all-start = ((f32[16,2,16,1280]{3,2,1,0:T(8,128)}), f32[16,2,16,1280]{3,2,1,0:T(8,128)}, u32[]{:S(2)}, u32[]{:S(2)}) async-start(f32[16,2,16,1280]{3,2,1,0:T(8,128)} %pre.2), calls=%async_computation | async-start | bytes 5242880 | tf_op jit(solution)/shard_map/all_to_all | solution.py:557
  67.0 0.7 copy.28
  68.5 16.8 %range.3 = f32[128,2,16,128]{3,2,1,0:T(8,128)} custom-call(f32[16,2,16,1280]{3,2,1,0:T(8,128)} %copy-done, f32[16,2,1280]{2,1,0:T(2,128)} %constant.58.clone.twa_ref, f32[10,2,128]{2,1,0:T(2,128)} %constant.59.clone.twb_ref, f32[160,2,128]{2,1,0:T(2,128)} %pad.8.hf_ref, bf16[256,256]{1,0:T(8,128)(2,1)} %constant.60.clone.fh_ref, ...), custom_call_target="tpu_custom_call" | custom-call | flops 10000000000 | bytes 6000000 | tf_op jit(solution)/shard_map/range/pallas_call | solution.py:297
  85.2 13.4 %all-to-all-done.x_ref = f32[16,2,16,1280]{3,2,1,0:T(8,128)} async-done(((f32[16,2,16,1280]{3,2,1,0:T(8,128)}), f32[16,2,16,1280]{3,2,1,0:T(8,128)}, u32[]{:S(2)}, u32[]{:S(2)}) %all-to-all-start) | async-done | bytes 2621472 | tf_op jit(solution)/shard_map/all_to_all | solution.py:557
  98.6 12.6 %all-to-all-start.3 = ((f32[128,2,16,128]{3,2,1,0:T(8,128)}), f32[128,2,16,128]{3,2,1,0:T(8,128)S(1)}, u32[]{:S(2)}, u32[]{:S(2)}) async-start(f32[128,2,16,128]{3,2,1,0:T(8,128)} %range.3), calls=%async_computation.3 | async-start | bytes 4194304 | tf_op jit(solution)/shard_map/all_to_all | solution.py:560
  112.0 16.8 %range.2 = f32[128,2,16,128]{3,2,1,0:T(8,128)} custom-call(f32[16,2,16,1280]{3,2,1,0:T(8,128)} %all-to-all-done.x_ref, f32[16,2,1280]{2,1,0:T(2,128)} %constant.58.clone.twa_ref, f32[10,2,128]{2,1,0:T(2,128)} %constant.59.clone.twb_ref, f32[160,2,128]{2,1,0:T(2,128)} %pad.8.hf_ref, bf16[256,256]{1,0:T(8,128)(2,1)} %constant.60.clone.fh_ref, ...), custom_call_target="tpu_custom_call" | custom-call | flops 10000000000 | bytes 6000000 | tf_op jit(solution)/shard_map/range/pallas_call | solution.py:297
  128.8 8.4 %all-to-all-done.3.x_ref = f32[128,2,16,128]{3,2,1,0:T(8,128)S(1)} async-done(((f32[128,2,16,128]{3,2,1,0:T(8,128)}), f32[128,2,16,128]{3,2,1,0:T(8,128)S(1)}, u32[]{:S(2)}, u32[]{:S(2)}) %all-to-all-start.3) | async-done | bytes 2097184 | tf_op jit(solution)/shard_map/all_to_all | solution.py:560
  137.2 1.3 copy-done.2
  138.6 8.4 %all-to-all-start.1 = ((f32[128,2,16,128]{3,2,1,0:T(8,128)}), f32[128,2,16,128]{3,2,1,0:T(8,128)S(1)}, u32[]{:S(2)}, u32[]{:S(2)}) async-start(f32[128,2,16,128]{3,2,1,0:T(8,128)} %range.2), calls=%async_computation.1 | async-start | bytes 4194304 | tf_op jit(solution)/shard_map/all_to_all | solution.py:560
  147.0 13.3 %prep.1 = (bf16[16,256,256]{2,1,0:T(8,128)(2,1)}, bf16[16,256,256]{2,1,0:T(8,128)(2,1)}) custom-call(f32[16,2,128]{2,1,0:T(2,128)} %bitcast.5, f32[2,128,128]{2,1,0:T(8,128)} %constant.65.clone.p0_ref, f32[2,128,128]{2,1,0:T(8,128)} %constant.66.clone.w_ref, f32[2,256,128]{2,1,0:T(8,128)} %constant.67.clone.q0_ref, f32[2,256,128]{2,1,0:T(8,128)} %constant.68.clone.v_ref), custom_call_target="tpu_custom_call" | custom-call | flops 5000000000 | bytes 5000000 | tf_op jit(solution)/shard_map/prep/pallas_call | solution.py:346
  160.3 11.0 %slave_azimuth.1 = (f32[2,2048,128]{2,1,0:T(8,128)}, f32[2048,128]{1,0:T(8,128)}, f32[2048,128]{1,0:T(8,128)}) custom-call(f32[128,2,16,128]{3,2,1,0:T(8,128)} %copy-done.2, bf16[16,256,256]{2,1,0:T(8,128)(2,1)} %get-tuple-element.13.ah_ref, bf16[16,256,256]{2,1,0:T(8,128)(2,1)} %get-tuple-element.14.al_ref), custom_call_target="tpu_custom_call" | custom-call | flops 5000000000 | bytes 10000000 | tf_op jit(solution)/shard_map/slave_azimuth/pallas_call | solution.py:404
  171.3 2.6 %collective-permute-start = (f32[2048,128]{1,0:T(8,128)}, f32[2048,128]{1,0:T(8,128)S(1)}, u32[]{:S(2)}, u32[]{:S(2)}) collective-permute-start(f32[2048,128]{1,0:T(8,128)} %get-tuple-element.16), channel_id=1, source_target_pairs={{0,1},{1,2},{2,3},{3,4},{4,5},{5,6},{6,7},{7,8},{8,9},{9,10},{10,1... | collective-permute-start | bytes 3145736 | tf_op jit(solution)/shard_map/ppermute | solution.py:548
  173.9 2.7 %collective-permute-start.1 = (f32[2048,128]{1,0:T(8,128)}, f32[2048,128]{1,0:T(8,128)}, u32[]{:S(2)}, u32[]{:S(2)}) collective-permute-start(f32[2048,128]{1,0:T(8,128)} %get-tuple-element.17), channel_id=1, source_target_pairs={{1,0},{2,1},{3,2},{4,3},{5,4},{6,5},{7,6},{8,7},{9,8},{10,9},{11,1... | collective-permute-start | bytes 3145736 | tf_op jit(solution)/shard_map/ppermute | solution.py:548
  179.7 1.4 pad_add_fusion
  181.2 16.6 %collective-permute-done.left_ref = f32[2048,128]{1,0:T(8,128)S(1)} collective-permute-done((f32[2048,128]{1,0:T(8,128)}, f32[2048,128]{1,0:T(8,128)S(1)}, u32[]{:S(2)}, u32[]{:S(2)}) %collective-permute-start) | collective-permute-done | bytes 1048608 | tf_op jit(solution)/shard_map/ppermute | solution.py:548
  197.8 7.1 %collective-permute-done.1.right_ref = f32[2048,128]{1,0:T(8,128)} collective-permute-done((f32[2048,128]{1,0:T(8,128)}, f32[2048,128]{1,0:T(8,128)}, u32[]{:S(2)}, u32[]{:S(2)}) %collective-permute-start.1) | collective-permute-done | bytes 1048608 | tf_op jit(solution)/shard_map/ppermute | solution.py:548
  204.9 11.3 %resample.1.m_ref = f32[2,2048,128]{2,1,0:T(8,128)} custom-call(s32[4,2]{1,0:T(4,128)} %copy.31.az_ref, s32[4,2]{1,0:T(4,128)} %copy.32.rg_ref, f32[2,2048,128]{2,1,0:T(8,128)} %get-tuple-element.15.s_ref, f32[2048,128]{1,0:T(8,128)} %copy-done.10, f32[2048,128]{1,0:T(8,128)} %collective-permute-done.1.right_ref), custom_call_target="tpu_custom_call" | custom-call | flops 2000000000 | bytes 10000000 | tf_op jit(solution)/shard_map/resample/pallas_call | solution.py:462
  216.2 1.4 copy-done.1
  217.6 10.2 %master_looks.1 = (f32[2,256,128]{2,1,0:T(8,128)}, f32[8,256]{1,0:T(8,128)}, f32[8,256]{1,0:T(8,128)}) custom-call(f32[128,2,16,128]{3,2,1,0:T(8,128)} %copy-done.1, bf16[16,256,256]{2,1,0:T(8,128)(2,1)} %get-tuple-element.13.ah_ref, bf16[16,256,256]{2,1,0:T(8,128)(2,1)} %get-tuple-element.14.al_ref, f32[2,2048,128]{2,1,0:T(8,128)} %resample.1.m_ref, ...), custom_call_target="tpu_custom_call" | custom-call | flops 5000000000 | bytes 10000000 | tf_op jit(solution)/shard_map/master_looks/pallas_call | solution.py:505
  227.8 1.9 collective-permute-start.2
  229.7 3.4 %collective-permute-start.3 = (f32[8,256]{1,0:T(8,128)}, f32[8,256]{1,0:T(8,128)S(1)}, u32[]{:S(2)}, u32[]{:S(2)}) collective-permute-start(f32[8,256]{1,0:T(8,128)} %get-tuple-element.20), channel_id=1, source_target_pairs={{1,0},{2,1},{3,2},{4,3},{5,4},{6,5},{7,6},{8,7},{9,8},{10,9},{11,1... | collective-permute-start | bytes 24584 | tf_op jit(solution)/shard_map/ppermute | solution.py:548
  233.1 0.9 fusion.1.scale_ref
  234.0 5.1 %collective-permute-done.3.right_ref = f32[8,256]{1,0:T(8,128)S(1)} collective-permute-done((f32[8,256]{1,0:T(8,128)}, f32[8,256]{1,0:T(8,128)S(1)}, u32[]{:S(2)}, u32[]{:S(2)}) %collective-permute-start.3) | collective-permute-done | bytes 8224 | tf_op jit(solution)/shard_map/ppermute | solution.py:548
  239.7 2.4 final.1
  242.1 1.7 copy.33
  (38 shorter events, 6.1 us)
Async XLA Ops:
  14.9 41.0 %all-to-all-start.2 = ((f32[16,2,16,1280]{3,2,1,0:T(8,128)}), f32[16,2,16,1280]{3,2,1,0:T(8,128)S(1)}, u32[]{:S(2)}, u32[]{:S(2)}) async-start(f32[16,2,16,1280]{3,2,1,0:T(8,128)} %pre.3), calls=%async_computation.2 | async-start | bytes 5242880 | tf_op jit(solution)/shard_map/all_to_all | solution.py:557
  36.1 30.1 %copy-start.3 = (f32[2,20000]{1,0:T(2,128)S(1)}, f32[2,20000]{1,0:T(2,128)}, u32[]{:S(2)}) copy-start(f32[2,20000]{1,0:T(2,128)} %param.22) | copy-start | bytes 480004
  55.9 1.5 copy-start
  57.4 41.2 %all-to-all-start = ((f32[16,2,16,1280]{3,2,1,0:T(8,128)}), f32[16,2,16,1280]{3,2,1,0:T(8,128)}, u32[]{:S(2)}, u32[]{:S(2)}) async-start(f32[16,2,16,1280]{3,2,1,0:T(8,128)} %pre.2), calls=%async_computation | async-start | bytes 5242880 | tf_op jit(solution)/shard_map/all_to_all | solution.py:557
  85.2 26.0 %copy-start.4 = (f32[2,2048]{1,0:T(2,128)S(1)}, f32[2,2048]{1,0:T(2,128)}, u32[]{:S(2)}) copy-start(f32[2,2048]{1,0:T(2,128)} %param.23) | copy-start | bytes 49156
  98.6 38.6 %all-to-all-start.3 = ((f32[128,2,16,128]{3,2,1,0:T(8,128)}), f32[128,2,16,128]{3,2,1,0:T(8,128)S(1)}, u32[]{:S(2)}, u32[]{:S(2)}) async-start(f32[128,2,16,128]{3,2,1,0:T(8,128)} %range.3), calls=%async_computation.3 | async-start | bytes 4194304 | tf_op jit(solution)/shard_map/all_to_all | solution.py:560
  137.2 1.3 copy-start.2
  138.6 77.6 %all-to-all-start.1 = ((f32[128,2,16,128]{3,2,1,0:T(8,128)}), f32[128,2,16,128]{3,2,1,0:T(8,128)S(1)}, u32[]{:S(2)}, u32[]{:S(2)}) async-start(f32[128,2,16,128]{3,2,1,0:T(8,128)} %range.2), calls=%async_computation.1 | async-start | bytes 4194304 | tf_op jit(solution)/shard_map/all_to_all | solution.py:560
  160.3 16.3 %copy-start.7 = (s32[4,2]{0,1:T(2,128)S(1)}, s32[4,2]{0,1:T(2,128)}, u32[]{:S(2)}) copy-start(s32[4,2]{0,1:T(2,128)} %param.24) | copy-start | bytes 100
  160.3 17.0 %copy-start.8 = (s32[4,2]{0,1:T(2,128)S(1)}, s32[4,2]{0,1:T(2,128)}, u32[]{:S(2)}) copy-start(s32[4,2]{0,1:T(2,128)} %param.25) | copy-start | bytes 100
  160.3 17.7 %copy-start.9 = (s32[256]{0:T(256)S(1)}, s32[256]{0:T(256)}, u32[]{:S(2)}) copy-start(s32[256]{0:T(256)} %param.26) | copy-start | bytes 3076
  171.3 26.5 %collective-permute-start = (f32[2048,128]{1,0:T(8,128)}, f32[2048,128]{1,0:T(8,128)S(1)}, u32[]{:S(2)}, u32[]{:S(2)}) collective-permute-start(f32[2048,128]{1,0:T(8,128)} %get-tuple-element.16), channel_id=1, source_target_pairs={{0,1},{1,2},{2,3},{3,4},{4,5},{5,6},{6,7},{7,8},{8,9},{9,10},{10,1... | collective-permute-start | bytes 3145736 | tf_op jit(solution)/shard_map/ppermute | solution.py:548
  173.9 31.0 %collective-permute-start.1 = (f32[2048,128]{1,0:T(8,128)}, f32[2048,128]{1,0:T(8,128)}, u32[]{:S(2)}, u32[]{:S(2)}) collective-permute-start(f32[2048,128]{1,0:T(8,128)} %get-tuple-element.17), channel_id=1, source_target_pairs={{1,0},{2,1},{3,2},{4,3},{5,4},{6,5},{7,6},{8,7},{9,8},{10,9},{11,1... | collective-permute-start | bytes 3145736 | tf_op jit(solution)/shard_map/ppermute | solution.py:548
  197.8 7.1 %copy-start.10 = (f32[2048,128]{1,0:T(8,128)}, f32[2048,128]{1,0:T(8,128)S(1)}, u32[]{:S(2)}) copy-start(f32[2048,128]{1,0:T(8,128)S(1)} %collective-permute-done.left_ref) | copy-start | bytes 3145732
  216.2 1.4 copy-start.1
  227.8 6.2 %collective-permute-start.2 = (f32[8,256]{1,0:T(8,128)}, f32[8,256]{1,0:T(8,128)S(1)}, u32[]{:S(2)}, u32[]{:S(2)}) collective-permute-start(f32[8,256]{1,0:T(8,128)} %get-tuple-element.19), channel_id=1, source_target_pairs={{0,1},{1,2},{2,3},{3,4},{4,5},{5,6},{6,7},{7,8},{8,9},{9,10},{10,1... | collective-permute-start | bytes 24584 | tf_op jit(solution)/shard_map/ppermute | solution.py:548
  229.7 9.4 %collective-permute-start.3 = (f32[8,256]{1,0:T(8,128)}, f32[8,256]{1,0:T(8,128)S(1)}, u32[]{:S(2)}, u32[]{:S(2)}) collective-permute-start(f32[8,256]{1,0:T(8,128)} %get-tuple-element.20), channel_id=1, source_target_pairs={{1,0},{2,1},{3,2},{4,3},{5,4},{6,5},{7,6},{8,7},{9,8},{10,9},{11,1... | collective-permute-start | bytes 24584 | tf_op jit(solution)/shard_map/ppermute | solution.py:548
  234.0 5.1 %copy-start.5 = (f32[8,256]{1,0:T(8,128)}, f32[8,256]{1,0:T(8,128)S(1)}, u32[]{:S(2)}) copy-start(f32[8,256]{1,0:T(8,128)S(1)} %collective-permute-done.2.left_ref) | copy-start | bytes 24580
  239.1 0.6 copy-start.6

commit v2 on v1

--- a/solution.py
+++ b/solution.py
@@ -127,6 +127,12 @@
     return jnp.dot(a, b, preferred_element_type=F32)
 
 
+def worker(block):
+    chip, core = divmod(block, 2)
+    y, rest = divmod(chip, 16)
+    return (y * 2 + core) * 16 + rest
+
+
 def _np_split(x):
     x = np.asarray(x, np.float32)
     hi = x.astype(BF16)
@@ -136,20 +142,13 @@
 def _tables():
     t = {}
     two = 2 * np.pi
-    q = np.arange(RPAD)
-    ang = -two * ((np.arange(NP)[:, None] * q[None, :]) % RANGE) / RANGE
-    t["twa"] = np.stack([np.cos(ang), np.sin(ang)], 1).astype(np.float32)
     q2 = np.arange(128)
     keep = (q2 < NS)[None, :]
     ang = -two * ((np.arange(NQ)[:, None] * q2[None, :]) % 1250) / 1250
     t["twb"] = np.stack([np.cos(ang) * keep, np.sin(ang) * keep], 1).astype(np.float32)
     n = np.arange(NQ)[None, :, None] * NS + q2[None, None, :]
     ang = two * ((np.arange(NP)[:, None, None] * n) % RANGE) / RANGE
-    t["twc"] = (
-        (np.stack([np.cos(ang), np.sin(ang)], 2) / RANGE)
-        .reshape(NP * NQ, 2, 128)
-        .astype(np.float32)
-    )
+    t["twc"] = np.stack([np.cos(ang), np.sin(ang)], 2).reshape(NP * NQ, 2, 128).astype(np.float32)
     ang = two * ((q2[:, None] * q2[None, :]) % NS) / NS
     both = keep & keep.T
     c, s = np.cos(ang) * both, np.sin(ang) * both
@@ -171,15 +170,12 @@
     ).astype(np.float32)
     t["v"] = np.stack([wr[line], wi[line]]).astype(np.float32)
     lane = np.arange(128)
-    band = np.zeros((128, 128), np.float32)
+    pick = np.zeros((24, 128), np.float32)
     for o in range(16):
-        band[:, o] = np.abs(lane // LOOK - o) <= 1
-    t["band"] = band
-    edge = np.zeros((4, 8, 128), np.float32)
-    for part in range(2):
-        edge[part, part] = lane < LOOK
-        edge[2 + part, part] = lane >= 128 - LOOK
-    t["edge"] = edge
+        pick[o] = np.abs(lane // LOOK - o) <= 1
+    pick[16] = lane < LOOK
+    pick[17] = lane >= 128 - LOOK
+    t["pick"] = pick
     return t
 
 
@@ -187,56 +183,49 @@
 
 
 def _pre_kernel(x_ref, o_ref):
-    for part in range(2):
-        o_ref[0, part, :, 0:1152] = x_ref[part, :, 0:1152]
-        tail = x_ref[part, :, 1152:1250]
-        o_ref[0, part, :, 1152:1280] = jnp.concatenate([tail, jnp.zeros((16, 30), F32)], axis=1)
+    for q in range(2):
+        for half in range(2):
+            for c in range(2):
+                v = x_ref[pl.ds(500 * q + 2 * half + c, NS, stride=4), :]
+                v = jnp.concatenate([v, jnp.zeros((128 - NS, 128), F32)], axis=0).T
+                for k in range(8):
+                    o_ref[8 * half + k, q, c] = v[16 * k : 16 * k + 16]
 
 
 def pre(raw):
+    rows = raw.transpose(2, 0, 1).reshape(1250, 2, 2, 128).transpose(0, 2, 1, 3).reshape(5000, 128)
     return pl.pallas_call(
         _pre_kernel,
-        grid=(NP,),
-        in_specs=[pl.BlockSpec((2, 16, 1250), lambda i: (0, i, 0))],
-        out_specs=pl.BlockSpec((1, 2, 16, RPAD), lambda i: (i, 0, 0, 0)),
-        out_shape=jax.ShapeDtypeStruct((NP, 2, 16, RPAD), F32),
+        grid=(5,),
+        in_specs=[pl.BlockSpec((1000, 128), lambda i: (i, 0))],
+        out_specs=pl.BlockSpec((NP, 2, 2, 16, 128), lambda i: (0, i, 0, 0, 0)),
+        out_shape=jax.ShapeDtypeStruct((NP, NQ, 2, 16, 128), F32),
         cost_estimate=pl.CostEstimate(flops=10**8, bytes_accessed=5 * 10**6, transcendentals=0),
+        compiler_params=pltpu.CompilerParams(vmem_limit_bytes=8 << 20),
         name="pre",
-    )(raw)
-
-
-def _range_kernel(x_ref, twa_ref, twb_ref, hf_ref, fh_ref, fl_ref, gh_ref, gl_ref, twc_ref, o_ref, b_ref, d_ref):
+    )(rows)
+
+
+def _range_kernel(x_ref, twb_ref, hf_ref, fh_ref, fl_ref, gh_ref, gl_ref, twc_ref, o_ref, d_ref):
     lane = lax.broadcasted_iota(jnp.int32, (16, 128), 1)
 
-    def outer(j, carry):
-        lanes = pl.ds(pl.multiple_of(j * 128, 128), 128)
+    def outer(q, carry):
         for g in range(2):
             rows = slice(8 * g, 8 * g + 8)
-            v = [(x_ref[p, 0, rows, lanes], x_ref[p, 1, rows, lanes]) for p in range(NP)]
+            v = [(x_ref[p, q, 0, rows, :], x_ref[p, q, 1, rows, :]) for p in range(NP)]
             v = dft16(v, -1)
             for k in range(NP):
-                tw = (twa_ref[k, 0:1, lanes], twa_ref[k, 1:2, lanes])
-                r, i = cmul(v[k], tw)
-                b_ref[k, 0, rows, lanes] = r
-                b_ref[k, 1, rows, lanes] = i
-        return carry
-
-    lax.fori_loop(0, RPAD // 128, outer, 0)
+                at = k * NQ + q
+                r, i = cmul(v[k], (twc_ref[at, 0:1, :], -twc_ref[at, 1:2, :]))
+                d_ref[at, 0, rows, :] = r
+                d_ref[at, 1, rows, :] = i
+        return carry
+
+    lax.fori_loop(0, NQ, outer, 0)
 
     def middle(kp, carry):
-        chunks = []
-        for q in range(NQ):
-            pair = []
-            for c in range(2):
-                here = b_ref[kp, c, :, 128 * q : 128 * q + 128]
-                if q:
-                    prev = b_ref[kp, c, :, 128 * q - 128 : 128 * q]
-                    here = jnp.where(
-                        lane < 3 * q, pltpu.roll(prev, 3 * q, 1), pltpu.roll(here, 3 * q, 1)
-                    )
-                pair.append(here)
-            chunks.append(tuple(pair))
-        v = dft10(chunks, -1)
+        v = [(d_ref[kp * NQ + q, 0], d_ref[kp * NQ + q, 1]) for q in range(NQ)]
+        v = dft10(v, -1)
         rows = []
         for k in range(NQ):
             r, i = cmul(v[k], (twb_ref[k, 0:1, :], twb_ref[k, 1:2, :]))
@@ -256,13 +245,13 @@
             v.append(cmul(val, (twb_ref[k, 0:1, :], -twb_ref[k, 1:2, :])))
         v = dft10(v, 1)
         for q in range(NQ):
-            tw = (twc_ref[kp * NQ + q, 0:1, :], twc_ref[kp * NQ + q, 1:2, :])
-            r, i = cmul(v[q], tw)
-            d_ref[kp * NQ + q, 0] = r
-            d_ref[kp * NQ + q, 1] = i
-        return carry
-
-    lax.fori_loop(0, NP, middle, 0)
+            at = kp * NQ + q
+            r, i = cmul(v[q], (twc_ref[at, 0:1, :], twc_ref[at, 1:2, :]))
+            d_ref[at, 0] = r
+            d_ref[at, 1] = i
+        return carry
+
+    lax.fori_loop(0, NP, middle, 0, unroll=2)
 
     def inner(q, carry):
         for g in range(2):
@@ -289,7 +278,7 @@
                 nxt = pltpu.roll(nxt, start % 128, 1)
                 val = jnp.where(lane < start, val, nxt)
                 start += NS
-            o_ref[d, c] = val
+            o_ref[worker(d), c] = val
 
 
 def range_compress(x, hf):
@@ -297,13 +286,11 @@
     return pl.pallas_call(
         _range_kernel,
         out_shape=jax.ShapeDtypeStruct((128, 2, 16, 128), F32),
-        scratch_shapes=[
-            pltpu.VMEM((NP, 2, 16, RPAD), F32),
-            pltpu.VMEM((NP * NQ, 2, 16, 128), F32),
-        ],
+        scratch_shapes=[pltpu.VMEM((NP * NQ, 2, 16, 128), F32)],
         cost_estimate=pl.CostEstimate(flops=10**10, bytes_accessed=6 * 10**6, transcendentals=0),
+        compiler_params=pltpu.CompilerParams(vmem_limit_bytes=24 << 20),
         name="range",
-    )(x, t["twa"], t["twb"], hf, t["fh"], t["fl"], t["gh"], t["gl"], t["twc"])
+    )(x, t["twb"], hf, t["fh"], t["fl"], t["gh"], t["gl"], t["twc"])
 
 
 def _dot_t(a, b):
@@ -348,6 +335,7 @@
         out_shape=(shape, shape),
         scratch_shapes=[pltpu.VMEM((2, 128, 128), F32), pltpu.VMEM((2, 256, 128), F32)],
         cost_estimate=pl.CostEstimate(flops=5 * 10**9, bytes_accessed=5 * 10**6, transcendentals=0),
+        compiler_params=pltpu.CompilerParams(vmem_limit_bytes=16 << 20),
         name="prep",
     )(h, t["p"], t["w"], t["q"], t["v"])
 
@@ -372,7 +360,7 @@
         e_ref[k] = wide[:, :128] + wide[:, 128:] + dot(al_ref[k], hi)
         return carry
 
-    lax.fori_loop(0, 16, second, 0)
+    lax.fori_loop(0, 16, second, 0, unroll=4)
 
 
 def _azimuth_rows(e_ref, g):
@@ -384,11 +372,15 @@
 def _slave_kernel(x_ref, ah_ref, al_ref, o_ref, left_ref, right_ref, e_ref):
     _azimuth_front(x_ref, ah_ref, al_ref, e_ref)
     low = lax.broadcasted_iota(jnp.int32, (8, 128), 1) < 64
+    zero = jnp.zeros((ASH, 128), F32)
+    for ref in (o_ref.at[0], o_ref.at[1], left_ref, right_ref):
+        ref[0:ASH, :] = zero
+        ref[ASH + LINES :, :] = zero
 
     def third(g, carry):
         v = _azimuth_rows(e_ref, g)
         for a in range(16):
-            rows = pl.ds(pl.multiple_of(a * 128 + g * 8, 8), 8)
+            rows = pl.ds(pl.multiple_of(a * 128 + g * 8 + ASH, 8), 8)
             r, i = v[a]
             o_ref[0, rows, :] = r
             o_ref[1, rows, :] = i
@@ -400,52 +392,38 @@
 
 
 def slave_azimuth(x, ah, al):
-    side = jax.ShapeDtypeStruct((LINES, 128), F32)
+    side = jax.ShapeDtypeStruct((LINES + 2 * ASH, 128), F32)
     return pl.pallas_call(
         _slave_kernel,
-        out_shape=(jax.ShapeDtypeStruct((2, LINES, 128), F32), side, side),
+        out_shape=(jax.ShapeDtypeStruct((2, LINES + 2 * ASH, 128), F32), side, side),
         scratch_shapes=[pltpu.VMEM((16, 256, 128), F32)],
         cost_estimate=pl.CostEstimate(flops=5 * 10**9, bytes_accessed=10**7, transcendentals=0),
+        compiler_params=pltpu.CompilerParams(vmem_limit_bytes=24 << 20),
         name="slave_azimuth",
     )(x, ah, al)
 
 
-def _resample_kernel(az_ref, rg_ref, s_ref, left_ref, right_ref, o_ref, w_ref):
+def _resample_kernel(az_ref, rg_ref, s_ref, left_ref, right_ref, o_ref):
     lane = lax.broadcasted_iota(jnp.int32, (64, 128), 1)
     low = lane < 64
-    for i in range(4):
-        w_ref[i, 0:ASH, :] = jnp.zeros((ASH, 128), F32)
-        w_ref[i, ASH + LINES : 2 * ASH + LINES, :] = jnp.zeros((ASH, 128), F32)
-
-    def fill(t, carry):
-        rows = pl.ds(pl.multiple_of(t * 64, 64), 64)
-        at = pl.ds(pl.multiple_of(t * 64 + ASH, 32), 64)
-        sr = pltpu.roll(s_ref[0, rows, :], 64, 1)
-        si = pltpu.roll(s_ref[1, rows, :], 64, 1)
-        left, right = left_ref[rows, :], right_ref[rows, :]
-        w_ref[0, at, :] = jnp.where(low, left, sr)
-        w_ref[1, at, :] = jnp.where(low, pltpu.roll(left, 64, 1), si)
-        w_ref[2, at, :] = jnp.where(low, sr, pltpu.roll(right, 64, 1))
-        w_ref[3, at, :] = jnp.where(low, si, right)
-        return carry
-
-    lax.fori_loop(0, LINES // 64, fill, 0)
 
     def move(t, carry):
         block = t // 8
         parts = []
-        for r in range(2):
-            start = t * 64 + ASH + az_ref[block, r]
-            shift = RSH + rg_ref[block, r]
-            back = lax.rem(256 - shift, 128)
-            rows = pl.ds(start, 64)
-            near = lane + shift < 128
+        for r, side_ref in ((0, left_ref), (1, right_ref)):
+            shift = rg_ref[block, r]
+            rows = pl.ds(t * 64 + ASH + az_ref[block, r], 64)
+            whole = lax.rem(256 - shift, 128)
+            half = lax.rem(192 - shift, 128)
+            near = lane + shift >= 0 if r == 0 else lane + shift < 128
+            side = side_ref[rows, :]
+            turns = (half, whole) if r == 0 else (whole, half)
             parts.append(
                 [
                     jnp.where(
                         near,
-                        pltpu.roll(w_ref[c, rows, :], back, 1),
-                        pltpu.roll(w_ref[2 + c, rows, :], back, 1),
+                        pltpu.roll(s_ref[c, rows, :], whole, 1),
+                        pltpu.roll(side, turns[c], 1),
                     )
                     for c in range(2)
                 ]
@@ -455,7 +433,7 @@
             o_ref[c, rows, :] = jnp.where(low, parts[0][c], parts[1][c])
         return carry
 
-    lax.fori_loop(0, LINES // 64, move, 0)
+    lax.fori_loop(0, LINES // 64, move, 0, unroll=2)
 
 
 def resample(az_shift, rg_shift, focused, left, right):
@@ -464,13 +442,13 @@
         in_specs=[pl.BlockSpec(memory_space=pltpu.SMEM)] * 2
         + [pl.BlockSpec(memory_space=pltpu.VMEM)] * 3,
         out_shape=jax.ShapeDtypeStruct((2, LINES, 128), F32),
-        scratch_shapes=[pltpu.VMEM((4, LINES + 2 * ASH, 128), F32)],
         cost_estimate=pl.CostEstimate(flops=2 * 10**9, bytes_accessed=10**7, transcendentals=0),
+        compiler_params=pltpu.CompilerParams(vmem_limit_bytes=16 << 20),
         name="resample",
     )(az_shift, rg_shift, focused, left, right)
 
 
-def _master_kernel(x_ref, ah_ref, al_ref, m_ref, n_ref, band_ref, edge_ref, box_ref, left_ref, right_ref, e_ref, c_ref):
+def _master_kernel(x_ref, ah_ref, al_ref, m_ref, n_ref, pick_ref, box_ref, side_ref, e_ref, c_ref):
     _azimuth_front(x_ref, ah_ref, al_ref, e_ref)
     line = lax.broadcasted_iota(jnp.int32, (8, 128), 0)
     count = n_ref[...]
@@ -490,67 +468,63 @@
     total = c_ref[pl.ds(0, 512, stride=LOOK), :]
     for j in range(1, LOOK):
         total = total + c_ref[pl.ds(j, 512, stride=LOOK), :]
-    parts = (total[:256], total[256:])
-    for c in range(2):
-        box_ref[c] = jnp.dot(
-            parts[c], band_ref[...], precision=lax.Precision.HIGHEST, preferred_element_type=F32
-        )
-    left_ref[...] = _dot_t(edge_ref[0], parts[0]) + _dot_t(edge_ref[1], parts[1])
-    right_ref[...] = _dot_t(edge_ref[2], parts[0]) + _dot_t(edge_ref[3], parts[1])
+    y = _dot_t(pick_ref[...], total)
+    cell = lax.broadcasted_iota(jnp.int32, (24, 512), 1) % 256
+    y = (
+        y
+        + jnp.where(cell == 0, 0.0, pltpu.roll(y, 1, 1))
+        + jnp.where(cell == 255, 0.0, pltpu.roll(y, 511, 1))
+    )
+    box_ref[...] = y[:16]
+    side_ref[...] = y[16:]
 
 
 def master_looks(x, ah, al, moved, counts):
-    t = TABLES
-    side = jax.ShapeDtypeStruct((8, 256), F32)
     return pl.pallas_call(
         _master_kernel,
-        out_shape=(jax.ShapeDtypeStruct((2, 256, 128), F32), side, side),
+        out_shape=(
+            jax.ShapeDtypeStruct((16, 512), F32),
+            jax.ShapeDtypeStruct((8, 512), F32),
+        ),
         scratch_shapes=[pltpu.VMEM((16, 256, 128), F32), pltpu.VMEM((2 * LINES, 128), F32)],
         cost_estimate=pl.CostEstimate(flops=5 * 10**9, bytes_accessed=10**7, transcendentals=0),
+        compiler_params=pltpu.CompilerParams(vmem_limit_bytes=24 << 20),
         name="master_looks",
-    )(x, ah, al, moved, counts, t["band"], t["edge"])
+    )(x, ah, al, moved, counts, TABLES["pick"])
 
 
 def _final_kernel(box_ref, left_ref, right_ref, scale_ref, o_ref):
-    row = lax.broadcasted_iota(jnp.int32, (256, 128), 0)
-    sub = lax.broadcasted_iota(jnp.int32, (8, 128), 0)
-    lane = lax.broadcasted_iota(jnp.int32, (8, 128), 1)
+    row = lax.broadcasted_iota(jnp.int32, (16, 256), 0)
     for c in range(2):
-        put = [
-            jnp.where((sub == c) & (lane == at), 1.0, 0.0).astype(F32) for at in (0, 15)
-        ]
-        x = box_ref[c]
-        for ref, onto in ((left_ref, put[0]), (right_ref, put[1])):
-            x = x + lax.dot_general(
-                ref[...],
-                onto,
-                (((0,), (0,)), ((), ())),
-                precision=lax.Precision.HIGHEST,
-                preferred_element_type=F32,
-            )
-        up = jnp.where(row == 0, 0.0, pltpu.roll(x, 1, 0))
-        down = jnp.where(row == 255, 0.0, pltpu.roll(x, 255, 0))
-        o_ref[c] = (x + up + down)[:, :16] * scale_ref[...]
+        at = slice(256 * c, 256 * c + 256)
+        x = box_ref[:, at]
+        x = x + jnp.where(row == 0, left_ref[1:2, at], 0.0)
+        x = x + jnp.where(row == 15, right_ref[0:1, at], 0.0)
+        o_ref[c] = x * scale_ref[...]
 
 
 def final(box, left, right, scale):
     return pl.pallas_call(
         _final_kernel,
-        out_shape=jax.ShapeDtypeStruct((2, 256, 16), F32),
+        out_shape=jax.ShapeDtypeStruct((2, 16, 256), F32),
+        compiler_params=pltpu.CompilerParams(vmem_limit_bytes=4 << 20),
         name="final",
     )(box, left, right, scale)
 
 
-def neighbours(first, second):
-    devices = lax.axis_size(ALL)
-    up = [(i, i + 1) for i in range(devices - 1)]
+def to_worker(x):
+    return lax.ppermute(x, ALL, [(b, worker(b)) for b in range(128)])
+
+
+def halo(to_right, to_left):
+    up = [(worker(b), worker(b + 1)) for b in range(127)]
     down = [(j, i) for i, j in up]
-    return lax.ppermute(first, ALL, up), lax.ppermute(second, ALL, down)
+    return lax.ppermute(to_right, ALL, up), lax.ppermute(to_left, ALL, down)
 
 
 def local(master_raw, slave_raw, range_ref, az_ref, az_shift, rg_shift, valid_lines):
     hf = range_ref.reshape(2, NS, NQ, NP).transpose(3, 2, 0, 1).reshape(NP * NQ, 2, NS)
-    hf = jnp.pad(hf, ((0, 0), (0, 0), (0, 3)))
+    hf = jnp.pad(hf * (1.0 / RANGE), ((0, 0), (0, 0), (0, 3)))
     h = az_ref.reshape(2, 128, 16).transpose(2, 0, 1) * (1.0 / LINES)
 
     def lines_of(raw):
@@ -559,29 +533,38 @@
     def columns_of(ranged):
         return lax.all_to_all(ranged, ALL, 0, 0, tiled=True)
 
+    flat = lax.axis_index(ALL)
+    counts = lax.dynamic_slice(jnp.pad(valid_lines, 1), (flat * 2,), (4,))
+    wide = jnp.concatenate([counts[:1], jnp.repeat(counts[1:3], BR // LOOK), counts[3:]])
+    rows = LINES // LOOK
+    groups = lax.broadcasted_iota(jnp.int32, (18, rows + 2), 1) - 1
+    pixels = jnp.clip(wide[:, None] - LOOK * groups, 0, LOOK) * LOOK
+    pixels = jnp.where((groups >= 0) & (groups < rows), pixels, 0).astype(F32)
+    box_pixels = sum(pixels[j : j + 16, i : i + rows] for i in range(3) for j in range(3))
+    scale = 1.0 / jnp.sqrt(jnp.maximum(box_pixels, 1.0))
+    core = lax.axis_index("az") % 2
+    block = ((lax.axis_index("az") // 2) * 16 + lax.axis_index("rg")) * 2 + core
+    own = lax.dynamic_slice(valid_lines, (block * 2,), (2,))
+    col_counts = jnp.repeat(own, BR)[None, :]
+    shifts = to_worker(jnp.stack([az_shift, rg_shift]))
+
     slave = lines_of(slave_raw)
     master = lines_of(master_raw)
+    ah, al = prep(h)
+    slave, ah, al, hf, shifts, scale, col_counts = lax.optimization_barrier(
+        (slave, ah, al, hf, shifts, scale, col_counts)
+    )
     slave = columns_of(range_compress(slave, hf))
     master = columns_of(range_compress(master, hf))
-    ah, al = prep(h)
     focused, to_left, to_right = slave_azimuth(slave, ah, al)
-    from_left, from_right = neighbours(to_right, to_left)
-    moved = resample(az_shift, rg_shift, focused, from_left, from_right)
-
-    flat = lax.axis_index(ALL)
-    counts = lax.dynamic_slice(jnp.pad(valid_lines, 1), (flat * 2,), (4,))
-    col_counts = jnp.repeat(counts[1:3], BR)[None, :]
-    wide = jnp.concatenate([counts[:1], jnp.repeat(counts[1:3], BR // LOOK), counts[3:]])
-    rows = LINES // LOOK
-    groups = lax.broadcasted_iota(jnp.int32, (rows + 2, 18), 0) - 1
-    pixels = jnp.clip(wide[None, :] - LOOK * groups, 0, LOOK) * LOOK
-    pixels = jnp.where((groups >= 0) & (groups < rows), pixels, 0).astype(F32)
-    box_pixels = sum(pixels[i : i + rows, j : j + 16] for i in range(3) for j in range(3))
-    scale = 1.0 / jnp.sqrt(jnp.maximum(box_pixels, 1.0))
-
-    box, edge_left, edge_right = master_looks(master, ah, al, moved, col_counts)
-    left, right = neighbours(edge_right, edge_left)
-    return final(box, left, right, scale)
+    from_left, from_right = halo(to_right, to_left)
+    moved = resample(shifts[0], shifts[1], focused, from_left, from_right)
+
+    box, side = master_looks(master, ah, al, moved, col_counts)
+    box = lax.ppermute(box, ALL, [(worker(b), b) for b in range(128)])
+    left = lax.ppermute(side, ALL, [(worker(b), b + 1) for b in range(127)])
+    right = lax.ppermute(side, ALL, [(worker(b + 1), b) for b in range(127)])
+    return final(box, left, right, scale).transpose(0, 2, 1)
 
 
 def solution(mesh):

time: 245 us -> 212 us (0.87)
  Pallas kernels: 101 us -> 49.3 us
  local copies, waits for them, and re-layouts: 23 us -> 34.7 us
  starting transfers between devices: 46.7 us -> 52.3 us
    pallas_call x5, Pallas kernels: 42.9 us -> 19.3 us  [the longest x1 7.24 us: slave_azimuth(): pl.pallas_call(_slave_kernel, out_shape=(jax.ShapeDtypeStruct((2, LINES +...]
    pallas_call x2, Pallas kernels: 33.5 us -> 16.1 us  [range_compress(): pl.pallas_call(_range_kernel, out_shape=jax.ShapeDtypeStruct((128, 2, 16,...]
    unnamed x26 -> x82, local copies, waits for them, and re-layouts: 16.7 us -> 28.2 us
    all_to_all x2, waiting for transfers between devices: 8.44 us -> 16.2 us  [columns_of(): return lax.all_to_all(ranged, ALL, 0, 0, tiled=True)]
    pallas_call x1, Pallas kernels: 11.3 us -> 3.92 us  [resample(): pl.pallas_call(_resample_kernel, in_specs=[pl.BlockSpec(memory_space=pltp...]
    mul x0 -> x2, local copies, waits for them, and re-layouts: none -> 4.91 us  [local(): hf = jnp.pad(hf * (1.0 / RANGE), ((0, 0), (0, 0), (0, 3)))]
    ppermute x4 -> x6, starting transfers between devices: 10.5 us -> 15.2 us  [the longest x1 7.48 us: local(): left = lax.ppermute(side, ALL, [(worker(b), b + 1) for b in range(127)])]
    pallas_call x1, Pallas kernels: 13.3 us -> 10 us  [prep(): pl.pallas_call(_prep_kernel, out_shape=(shape, shape), scratch_shapes=[pl...]
  transfers between devices with their start and end apart: 8 -> 10, of which waited for: 6 -> 6; matrix products, arithmetic and copies ran while one was open for 6% -> 4% of each run, Pallas kernels for 32% -> 19%
where the time goes in v2:
time: 212 us; the launch traced here: 210 us
  waiting for transfers between devices  72 us (34%)
  starting transfers between devices  52.3 us (25%)
  Pallas kernels  49.3 us (23%)
  local copies, waits for them, and re-layouts  34.7 us (16%)
    all_to_all x2, waiting for transfers between devices, lines_of(): return lax.all_to_all(pre(raw), 'rg', 0, 0, tiled=True)  30 us
    unnamed x82, local copies, waits for them, and re-layouts  28.2 us
    all_to_all x2, starting transfers between devices, columns_of(): return lax.all_to_all(ranged, ALL, 0, 0, tiled=True)  22.5 us
    ppermute x2, waiting for transfers between devices, halo(): return (lax.ppermute(to_right, ALL, up), lax.ppermute(to_left, ALL, down))  18.5 us
    all_to_all x2, waiting for transfers between devices, columns_of(): return lax.all_to_all(ranged, ALL, 0, 0, tiled=True)  16.2 us
    pallas_call x2, Pallas kernels, range_compress(): pl.pallas_call(_range_kernel, out_shape=jax.ShapeDtypeStruct((128, 2, 16,...  16.1 us
    all_to_all x2, starting transfers between devices, lines_of(): return lax.all_to_all(pre(raw), 'rg', 0, 0, tiled=True)  14.6 us
    pallas_call x1, Pallas kernels, prep(): pl.pallas_call(_prep_kernel, out_shape=(shape, shape), scratch_shapes=[pl...  10 us
  transfers between devices with their start and end apart: 10, of which 6 were waited for; matrix products, arithmetic and copies ran while one was open for 4% of the time, Pallas kernels for 19%

profile of v2, /device:TPU:103, one launch (start us, length us, event | category | flops | bytes accessed | tf_op | source)
XLA Modules:
  0.0 210.5 jit_solution(5038232296548528844)
XLA Ops:
  0.0 1.7 copy-done.2
  1.7 3.0 %pre.3 = f32[16,10,2,16,128]{4,3,2,1,0:T(8,128)} custom-call(f32[5000,128]{1,0:T(8,128)S(1)} %bitcast.24), custom_call_target="tpu_custom_call" | custom-call | flops 100000000 | bytes 5000000 | tf_op jit(solution)/shard_map/pre/pallas_call | solution.py:197
  4.7 6.5 %all-to-all-start.1 = ((f32[16,10,2,16,128]{4,3,2,1,0:T(8,128)}), f32[16,10,2,16,128]{4,3,2,1,0:T(8,128)S(1)}, u32[]{:S(2)}, u32[]{:S(2)}) async-start(f32[16,10,2,16,128]{4,3,2,1,0:T(8,128)} %pre.3), calls=%async_computation.1 | async-start | bytes 5242880 | tf_op jit(solution)/shard_map/all_to_all | solution.py:531
  11.9 1.7 copy-done.3
  13.6 3.0 %pre.2 = f32[16,10,2,16,128]{4,3,2,1,0:T(8,128)} custom-call(f32[5000,128]{1,0:T(8,128)S(1)} %bitcast.25), custom_call_target="tpu_custom_call" | custom-call | flops 100000000 | bytes 5000000 | tf_op jit(solution)/shard_map/pre/pallas_call | solution.py:197
  16.7 29.2 %all-to-all-done.1.x_ref = f32[16,10,2,16,128]{4,3,2,1,0:T(8,128)S(1)} async-done(((f32[16,10,2,16,128]{4,3,2,1,0:T(8,128)}), f32[16,10,2,16,128]{4,3,2,1,0:T(8,128)S(1)}, u32[]{:S(2)}, u32[]{:S(2)}) %all-to-all-start.1) | async-done | bytes 2621472 | tf_op jit(solution)/shard_map/all_to_all | solution.py:531
  45.9 1.5 copy-done
  47.4 8.1 %all-to-all-start = ((f32[16,10,2,16,128]{4,3,2,1,0:T(8,128)}), f32[16,10,2,16,128]{4,3,2,1,0:T(8,128)S(1)}, u32[]{:S(2)}, u32[]{:S(2)}) async-start(f32[16,10,2,16,128]{4,3,2,1,0:T(8,128)} %pre.2), calls=%async_computation | async-start | bytes 5242880 | tf_op jit(solution)/shard_map/all_to_all | solution.py:531
  56.3 2.1 mul.53
  58.4 2.8 %copy.27 = f32[16,10,2,125]{3,2,1,0:T(2,128)} copy(f32[16,10,2,125]{0,1,3,2:T(8,128)} %bitcast.27) | data formatting | bytes 320000 | tf_op jit(solution)/shard_map/mul | solution.py:527
  64.5 10.0 %prep.1 = (bf16[16,256,256]{2,1,0:T(8,128)(2,1)S(1)}, bf16[16,256,256]{2,1,0:T(8,128)(2,1)S(1)}) custom-call(f32[16,2,128]{2,1,0:T(2,128)S(1)} %bitcast.26, f32[2,128,128]{2,1,0:T(8,128)S(1)} %copy-done.21, f32[2,128,128]{2,1,0:T(8,128)S(1)} %copy-done.22, f32[2,256,128]{2,1,0:T(8,128)S(1)} %copy-done.10, f32[2,256,128]{2,1,0:T(8,128)S(1)} %copy-done.11), custom_call_target="tpu_custom_call" | custom-call | flops 5000000000 | bytes 5000000 | tf_op jit(solution)/shard_map/prep/pallas_call | solution.py:333
  77.4 8.1 %range.3 = f32[128,2,16,128]{3,2,1,0:T(8,128)S(1)} custom-call(f32[16,10,2,16,128]{4,3,2,1,0:T(8,128)S(1)} %copy-done.1, f32[10,2,128]{2,1,0:T(2,128)S(1)} %copy-done.24, f32[160,2,128]{2,1,0:T(2,128)S(1)} %pad.8.hf_ref, bf16[256,256]{1,0:T(8,128)(2,1)S(1)} %copy-done.13, bf16[256,256]{1,0:T(8,128)(2,1)S(1)} %copy-done.15, bf16[256,256]{1,0:T(8,128)(2,1)S(1)} %copy-done.17, ...), custom_call_target="tpu_custom_call" | custom-call | flops 10000000000 | bytes 6000000 | tf_op jit(solution)/shard_map/range/pallas_call | solution.py:286
  85.5 1.4 copy-done.5
  87.7 13.1 %all-to-all-start.3 = ((f32[128,2,16,128]{3,2,1,0:T(8,128)}), f32[128,2,16,128]{3,2,1,0:T(8,128)}, u32[]{:S(2)}, u32[]{:S(2)}) async-start(f32[128,2,16,128]{3,2,1,0:T(8,128)} %copy-done.5), calls=%async_computation.3 | async-start | bytes 4194304 | tf_op jit(solution)/shard_map/all_to_all | solution.py:534
  100.9 8.1 %range.2 = f32[128,2,16,128]{3,2,1,0:T(8,128)S(1)} custom-call(f32[16,10,2,16,128]{4,3,2,1,0:T(8,128)S(1)} %all-to-all-done.x_ref, f32[10,2,128]{2,1,0:T(2,128)S(1)} %copy-done.24, f32[160,2,128]{2,1,0:T(2,128)S(1)} %pad.8.hf_ref, bf16[256,256]{1,0:T(8,128)(2,1)S(1)} %copy-done.14, bf16[256,256]{1,0:T(8,128)(2,1)S(1)} %copy-done.16, ...), custom_call_target="tpu_custom_call" | custom-call | flops 10000000000 | bytes 6000000 | tf_op jit(solution)/shard_map/range/pallas_call | solution.py:286
  110.3 16.2 %all-to-all-done.3.x_ref = f32[128,2,16,128]{3,2,1,0:T(8,128)} async-done(((f32[128,2,16,128]{3,2,1,0:T(8,128)}), f32[128,2,16,128]{3,2,1,0:T(8,128)}, u32[]{:S(2)}, u32[]{:S(2)}) %all-to-all-start.3) | async-done | bytes 2097184 | tf_op jit(solution)/shard_map/all_to_all | solution.py:534
  126.5 9.5 %all-to-all-start.2 = ((f32[128,2,16,128]{3,2,1,0:T(8,128)}), f32[128,2,16,128]{3,2,1,0:T(8,128)}, u32[]{:S(2)}, u32[]{:S(2)}) async-start(f32[128,2,16,128]{3,2,1,0:T(8,128)} %copy-done.4), calls=%async_computation.2 | async-start | bytes 4194304 | tf_op jit(solution)/shard_map/all_to_all | solution.py:534
  136.0 1.6 copy-done.30
  137.5 1.6 copy-done.33
  139.1 7.2 %slave_azimuth.1 = (f32[2,2112,128]{2,1,0:T(8,128)S(1)}, f32[2112,128]{1,0:T(8,128)}, f32[2112,128]{1,0:T(8,128)}) custom-call(f32[128,2,16,128]{3,2,1,0:T(8,128)} %all-to-all-done.3.x_ref, bf16[16,256,256]{2,1,0:T(8,128)(2,1)S(1)} %copy-done.30, bf16[16,256,256]{2,1,0:T(8,128)(2,1)S(1)} %copy-done.33), custom_call_target="tpu_custom_call" | custom-call | flops 5000000000 | bytes 10000000 | tf_op jit(solution)/shard_map/slave_azimuth/pallas_call | solution.py:396
  147.7 2.6 %collective-permute-start.1 = (f32[2112,128]{1,0:T(8,128)}, f32[2112,128]{1,0:T(8,128)S(1)}, u32[]{:S(2)}, u32[]{:S(2)}) collective-permute-start(f32[2112,128]{1,0:T(8,128)} %get-tuple-element.27), channel_id=1, source_target_pairs={{0,16},{16,1},{1,17},{17,2},{2,18},{18,3},{3,19},{19,4},{4,20},{20... | collective-permute-start | bytes 3244040 | tf_op jit(solution)/shard_map/ppermute | solution.py:522
  150.3 1.9 collective-permute-start.2
  152.4 17.3 %collective-permute-done.1.left_ref = f32[2112,128]{1,0:T(8,128)S(1)} collective-permute-done((f32[2112,128]{1,0:T(8,128)}, f32[2112,128]{1,0:T(8,128)S(1)}, u32[]{:S(2)}, u32[]{:S(2)}) %collective-permute-start.1) | collective-permute-done | bytes 1081376 | tf_op jit(solution)/shard_map/ppermute | solution.py:522
  175.4 1.6 copy-done.26
  177.0 3.9 %resample.1.m_ref = f32[2,2048,128]{2,1,0:T(8,128)S(1)} custom-call(s32[4,2]{1,0:T(4,128)S(1)} %copy.28.az_ref, s32[4,2]{1,0:T(4,128)S(1)} %copy.29.rg_ref, f32[2,2112,128]{2,1,0:T(8,128)S(1)} %copy-done.26, f32[2112,128]{1,0:T(8,128)S(1)} %copy-done.7, f32[2112,128]{1,0:T(8,128)S(1)} %copy-done.9), custom_call_target="tpu_custom_call" | custom-call | flops 2000000000 | bytes 10000000 | tf_op jit(solution)/shard_map/resample/pallas_call | solution.py:440
  182.2 1.6 copy-done.28
  183.8 1.6 copy-done.31
  185.4 1.6 copy-done.34
  187.0 5.4 %master_looks.1 = (f32[16,512]{1,0:T(8,128)S(1)}, f32[8,512]{1,0:T(8,128)S(1)}) custom-call(f32[128,2,16,128]{3,2,1,0:T(8,128)} %all-to-all-done.2.x_ref, bf16[16,256,256]{2,1,0:T(8,128)(2,1)S(1)} %copy-done.31, bf16[16,256,256]{2,1,0:T(8,128)(2,1)S(1)} %copy-done.34, f32[2,2048,128]{2,1,0:T(8,128)S(1)} %copy-done.28, ...), custom_call_target="tpu_custom_call" | custom-call | flops 5000000000 | bytes 10000000 | tf_op jit(solution)/shard_map/master_looks/pallas_call | solution.py:483
  193.1 7.5 %collective-permute-start.4 = (f32[8,512]{1,0:T(8,128)S(1)}, f32[8,512]{1,0:T(8,128)S(1)}, u32[]{:S(2)}, u32[]{:S(2)}) collective-permute-start(f32[8,512]{1,0:T(8,128)S(1)} %get-tuple-element.31), channel_id=1, source_target_pairs={{0,1},{16,2},{1,3},{17,4},{2,5},{18,6},{3,7},{19,8},{4,9},{20,10},... | collective-permute-start | bytes 49160 | tf_op jit(solution)/shard_map/ppermute | solution.py:565
  200.6 1.9 collective-permute-start.5
  202.5 7.3 %collective-permute-done.5.right_ref = f32[8,512]{1,0:T(8,128)S(1)} collective-permute-done((f32[8,512]{1,0:T(8,128)S(1)}, f32[8,512]{1,0:T(8,128)S(1)}, u32[]{:S(2)}, u32[]{:S(2)}) %collective-permute-start.5) | collective-permute-done | bytes 16416 | tf_op jit(solution)/shard_map/ppermute | solution.py:566
  (103 shorter events, 19.5 us)
Async XLA Ops:
  4.7 6.5 %copy-start.39 = (s32[4,2]{0,1:T(2,128)S(1)}, s32[4,2]{0,1:T(2,128)}, u32[]{:S(2)}) copy-start(s32[4,2]{0,1:T(2,128)} %param.23) | copy-start | bytes 100
  4.7 6.5 %copy-start.40 = (s32[4,2]{0,1:T(2,128)S(1)}, s32[4,2]{0,1:T(2,128)}, u32[]{:S(2)}) copy-start(s32[4,2]{0,1:T(2,128)} %param.22) | copy-start | bytes 100
  4.7 41.2 %all-to-all-start.1 = ((f32[16,10,2,16,128]{4,3,2,1,0:T(8,128)}), f32[16,10,2,16,128]{4,3,2,1,0:T(8,128)S(1)}, u32[]{:S(2)}, u32[]{:S(2)}) async-start(f32[16,10,2,16,128]{4,3,2,1,0:T(8,128)} %pre.3), calls=%async_computation.1 | async-start | bytes 5242880 | tf_op jit(solution)/shard_map/all_to_all | solution.py:531
  11.2 66.1 %collective-permute-start = (s32[2,4,2]{1,2,0:T(2,128)S(1)}, s32[2,4,2]{1,2,0:T(2,128)S(1)}, u32[]{:S(2)}, u32[]{:S(2)}) collective-permute-start(s32[2,4,2]{1,2,0:T(2,128)S(1)} %pad_add_fusion), channel_id=1, source_target_pairs={{0,0},{1,16},{2,1},{3,17},{4,2},{5,18},{6,3},{7,19},{8,4},{9,20},{... | collective-permute-start | bytes 200 | tf_op jit(solution)/shard_map/ppermute | solution.py:516
  11.9 1.7 copy-start.3
  13.6 3.0 %copy-start.36 = (f32[2,20000]{1,0:T(2,128)S(1)}, f32[2,20000]{1,0:T(2,128)}, u32[]{:S(2)}) copy-start(f32[2,20000]{1,0:T(2,128)} %param.20) | copy-start | bytes 480004
  16.7 38.8 %copy-start.37 = (f32[2,2048]{1,0:T(2,128)S(1)}, f32[2,2048]{1,0:T(2,128)}, u32[]{:S(2)}) copy-start(f32[2,2048]{1,0:T(2,128)} %param.21) | copy-start | bytes 49156
  16.7 38.9 %copy-start.38 = (s32[256]{0:T(256)S(1)}, s32[256]{0:T(256)}, u32[]{:S(2)}) copy-start(s32[256]{0:T(256)} %param.24) | copy-start | bytes 3076
  47.4 40.3 %all-to-all-start = ((f32[16,10,2,16,128]{4,3,2,1,0:T(8,128)}), f32[16,10,2,16,128]{4,3,2,1,0:T(8,128)S(1)}, u32[]{:S(2)}, u32[]{:S(2)}) async-start(f32[16,10,2,16,128]{4,3,2,1,0:T(8,128)} %pre.2), calls=%async_computation | async-start | bytes 5242880 | tf_op jit(solution)/shard_map/all_to_all | solution.py:531
  56.3 7.2 %copy-start.10 = (f32[2,256,128]{2,1,0:T(8,128)S(1)}, f32[2,256,128]{2,1,0:T(8,128)}, u32[]{:S(2)}) copy-start(f32[2,256,128]{2,1,0:T(8,128)} %constant.79.clone.q0_ref) | copy-start | bytes 786436
  56.3 7.2 %copy-start.11 = (f32[2,256,128]{2,1,0:T(8,128)S(1)}, f32[2,256,128]{2,1,0:T(8,128)}, u32[]{:S(2)}) copy-start(f32[2,256,128]{2,1,0:T(8,128)} %constant.80.clone.v_ref) | copy-start | bytes 786436
  56.3 7.2 %copy-start.21 = (f32[2,128,128]{2,1,0:T(8,128)S(1)}, f32[2,128,128]{2,1,0:T(8,128)}, u32[]{:S(2)}) copy-start(f32[2,128,128]{2,1,0:T(8,128)} %constant.77.clone.p0_ref) | copy-start | bytes 393220
  64.4 12.8 %copy-start.35 = (f32[16,10,2,125]{3,2,1,0:T(2,128)S(1)}, f32[16,10,2,125]{3,2,1,0:T(2,128)}, u32[]{:S(2)}) copy-start(f32[16,10,2,125]{3,2,1,0:T(2,128)} %copy.27) | copy-start | bytes 480004
  64.4 12.9 %copy-start.1 = (f32[16,10,2,16,128]{4,3,2,1,0:T(8,128)S(1)}, f32[16,10,2,16,128]{4,3,2,1,0:T(8,128)}, u32[]{:S(2)}) copy-start(f32[16,10,2,16,128]{4,3,2,1,0:T(8,128)} %copy-done) | copy-start | bytes 7864324
  64.4 12.9 %copy-start.12 = (f32[160,2,128]{2,1,0:T(2,128)S(1)}, f32[160,2,128]{2,1,0:T(2,128)}, u32[]{:S(2)}) copy-start(f32[160,2,128]{2,1,0:T(2,128)} %constant.86.clone.twc_ref) | copy-start | bytes 491524
  64.4 12.9 %copy-start.13 = (bf16[256,256]{1,0:T(8,128)(2,1)S(1)}, bf16[256,256]{1,0:T(8,128)(2,1)}, u32[]{:S(2)}) copy-start(bf16[256,256]{1,0:T(8,128)(2,1)} %constant.82.clone.fh_ref) | copy-start | bytes 393220
  64.4 12.9 %copy-start.15 = (bf16[256,256]{1,0:T(8,128)(2,1)S(1)}, bf16[256,256]{1,0:T(8,128)(2,1)}, u32[]{:S(2)}) copy-start(bf16[256,256]{1,0:T(8,128)(2,1)} %constant.83.clone.fl_ref) | copy-start | bytes 393220
  64.4 12.9 %copy-start.17 = (bf16[256,256]{1,0:T(8,128)(2,1)S(1)}, bf16[256,256]{1,0:T(8,128)(2,1)}, u32[]{:S(2)}) copy-start(bf16[256,256]{1,0:T(8,128)(2,1)} %constant.84.clone.gh_ref) | copy-start | bytes 393220
  64.5 12.9 %copy-start.19 = (bf16[256,256]{1,0:T(8,128)(2,1)S(1)}, bf16[256,256]{1,0:T(8,128)(2,1)}, u32[]{:S(2)}) copy-start(bf16[256,256]{1,0:T(8,128)(2,1)} %constant.85.clone.gl_ref) | copy-start | bytes 393220
  64.5 12.9 %copy-start.24 = (f32[10,2,128]{2,1,0:T(2,128)S(1)}, f32[10,2,128]{2,1,0:T(2,128)}, u32[]{:S(2)}) copy-start(f32[10,2,128]{2,1,0:T(2,128)} %constant.81.clone.twb_ref) | copy-start | bytes 30724
  86.9 14.0 %copy-start.14 = (bf16[256,256]{1,0:T(8,128)(2,1)S(1)}, bf16[256,256]{1,0:T(8,128)(2,1)}, u32[]{:S(2)}) copy-start(bf16[256,256]{1,0:T(8,128)(2,1)} %constant.82.clone.fh_ref) | copy-start | bytes 393220
  86.9 14.0 %copy-start.16 = (bf16[256,256]{1,0:T(8,128)(2,1)S(1)}, bf16[256,256]{1,0:T(8,128)(2,1)}, u32[]{:S(2)}) copy-start(bf16[256,256]{1,0:T(8,128)(2,1)} %constant.83.clone.fl_ref) | copy-start | bytes 393220
  86.9 14.0 %copy-start.18 = (bf16[256,256]{1,0:T(8,128)(2,1)S(1)}, bf16[256,256]{1,0:T(8,128)(2,1)}, u32[]{:S(2)}) copy-start(bf16[256,256]{1,0:T(8,128)(2,1)} %constant.84.clone.gh_ref) | copy-start | bytes 393220
  86.9 14.0 %copy-start.20 = (bf16[256,256]{1,0:T(8,128)(2,1)S(1)}, bf16[256,256]{1,0:T(8,128)(2,1)}, u32[]{:S(2)}) copy-start(bf16[256,256]{1,0:T(8,128)(2,1)} %constant.85.clone.gl_ref) | copy-start | bytes 393220
  87.7 38.7 %all-to-all-start.3 = ((f32[128,2,16,128]{3,2,1,0:T(8,128)}), f32[128,2,16,128]{3,2,1,0:T(8,128)}, u32[]{:S(2)}, u32[]{:S(2)}) async-start(f32[128,2,16,128]{3,2,1,0:T(8,128)} %copy-done.5), calls=%async_computation.3 | async-start | bytes 4194304 | tf_op jit(solution)/shard_map/all_to_all | solution.py:534
  126.5 55.8 %all-to-all-start.2 = ((f32[128,2,16,128]{3,2,1,0:T(8,128)}), f32[128,2,16,128]{3,2,1,0:T(8,128)}, u32[]{:S(2)}, u32[]{:S(2)}) async-start(f32[128,2,16,128]{3,2,1,0:T(8,128)} %copy-done.4), calls=%async_computation.2 | async-start | bytes 4194304 | tf_op jit(solution)/shard_map/all_to_all | solution.py:534
  147.7 22.0 %collective-permute-start.1 = (f32[2112,128]{1,0:T(8,128)}, f32[2112,128]{1,0:T(8,128)S(1)}, u32[]{:S(2)}, u32[]{:S(2)}) collective-permute-start(f32[2112,128]{1,0:T(8,128)} %get-tuple-element.27), channel_id=1, source_target_pairs={{0,16},{16,1},{1,17},{17,2},{2,18},{18,3},{3,19},{19,4},{4,20},{20... | collective-permute-start | bytes 3244040 | tf_op jit(solution)/shard_map/ppermute | solution.py:522
  150.3 21.6 %collective-permute-start.2 = (f32[2112,128]{1,0:T(8,128)}, f32[2112,128]{1,0:T(8,128)S(1)}, u32[]{:S(2)}, u32[]{:S(2)}) collective-permute-start(f32[2112,128]{1,0:T(8,128)} %get-tuple-element.28), channel_id=1, source_target_pairs={{16,0},{1,16},{17,1},{2,17},{18,2},{3,18},{19,3},{4,19},{20,4},{5,... | collective-permute-start | bytes 3244040 | tf_op jit(solution)/shard_map/ppermute | solution.py:522
  177.0 5.3 %copy-start.23 = (f32[24,128]{1,0:T(8,128)S(1)}, f32[24,128]{1,0:T(8,128)}, u32[]{:S(2)}) copy-start(f32[24,128]{1,0:T(8,128)} %constant.87.clone.pick_ref) | copy-start | bytes 36868
  192.4 17.4 %collective-permute-start.3 = (f32[16,512]{1,0:T(8,128)S(1)}, f32[16,512]{1,0:T(8,128)S(1)}, u32[]{:S(2)}, u32[]{:S(2)}) collective-permute-start(f32[16,512]{1,0:T(8,128)S(1)} %get-tuple-element.30), channel_id=1, source_target_pairs={{0,0},{16,1},{1,2},{17,3},{2,4},{18,5},{3,6},{19,7},{4,8},{20,9},{... | collective-permute-start | bytes 98312 | tf_op jit(solution)/shard_map/ppermute | solution.py:564
  193.1 9.4 %collective-permute-start.4 = (f32[8,512]{1,0:T(8,128)S(1)}, f32[8,512]{1,0:T(8,128)S(1)}, u32[]{:S(2)}, u32[]{:S(2)}) collective-permute-start(f32[8,512]{1,0:T(8,128)S(1)} %get-tuple-element.31), channel_id=1, source_target_pairs={{0,1},{16,2},{1,3},{17,4},{2,5},{18,6},{3,7},{19,8},{4,9},{20,10},... | collective-permute-start | bytes 49160 | tf_op jit(solution)/shard_map/ppermute | solution.py:565
  200.6 9.3 %collective-permute-start.5 = (f32[8,512]{1,0:T(8,128)S(1)}, f32[8,512]{1,0:T(8,128)S(1)}, u32[]{:S(2)}, u32[]{:S(2)}) collective-permute-start(f32[8,512]{1,0:T(8,128)S(1)} %get-tuple-element.31), channel_id=1, source_target_pairs={{16,0},{1,1},{17,2},{2,3},{18,4},{3,5},{19,6},{4,7},{20,8},{5,9},{... | collective-permute-start | bytes 49160 | tf_op jit(solution)/shard_map/ppermute | solution.py:566
  (19 other events, 26.4 us)

commit v3 on v2

--- a/solution.py
+++ b/solution.py
@@ -1,4 +1,5 @@
 import math
+from functools import partial
 
 import jax
 import jax.numpy as jnp
@@ -182,34 +183,53 @@
 TABLES = _tables()
 
 
-def _pre_kernel(x_ref, o_ref):
-    for q in range(2):
-        for half in range(2):
-            for c in range(2):
-                v = x_ref[pl.ds(500 * q + 2 * half + c, NS, stride=4), :]
-                v = jnp.concatenate([v, jnp.zeros((128 - NS, 128), F32)], axis=0).T
-                for k in range(8):
-                    o_ref[8 * half + k, q, c] = v[16 * k : 16 * k + 16]
-
-
-def pre(raw):
-    rows = raw.transpose(2, 0, 1).reshape(1250, 2, 2, 128).transpose(0, 2, 1, 3).reshape(5000, 128)
+HBM = pl.BlockSpec(memory_space=pltpu.HBM)
+VMEM = pl.BlockSpec(memory_space=pltpu.VMEM)
+SMEM = pl.BlockSpec(memory_space=pltpu.SMEM)
+
+
+def limit(mib):
+    return pltpu.CompilerParams(vmem_limit_bytes=mib << 20)
+
+
+def _pre_kernel(first_ref, second_ref, o_ref):
+    for image, x_ref in enumerate((first_ref, second_ref)):
+        for q in range(2):
+            for half in range(2):
+                for c in range(2):
+                    v = x_ref[pl.ds(500 * q + 2 * half + c, NS, stride=4), :]
+                    v = jnp.concatenate([v, jnp.zeros((128 - NS, 128), F32)], axis=0).T
+                    for k in range(8):
+                        o_ref[8 * half + k, image, q, c] = v[16 * k : 16 * k + 16]
+
+
+def pre(first, second):
+    def rows(raw):
+        raw = raw.transpose(2, 0, 1).reshape(1250, 2, 2, 128)
+        return raw.transpose(0, 2, 1, 3).reshape(5000, 128)
+
     return pl.pallas_call(
         _pre_kernel,
         grid=(5,),
-        in_specs=[pl.BlockSpec((1000, 128), lambda i: (i, 0))],
-        out_specs=pl.BlockSpec((NP, 2, 2, 16, 128), lambda i: (0, i, 0, 0, 0)),
-        out_shape=jax.ShapeDtypeStruct((NP, NQ, 2, 16, 128), F32),
-        cost_estimate=pl.CostEstimate(flops=10**8, bytes_accessed=5 * 10**6, transcendentals=0),
-        compiler_params=pltpu.CompilerParams(vmem_limit_bytes=8 << 20),
+        in_specs=[pl.BlockSpec((1000, 128), lambda i: (i, 0))] * 2,
+        out_specs=pl.BlockSpec((NP, 2, 2, 2, 16, 128), lambda i: (0, 0, i, 0, 0, 0)),
+        out_shape=jax.ShapeDtypeStruct((NP, 2, NQ, 2, 16, 128), F32),
+        cost_estimate=pl.CostEstimate(flops=10**8, bytes_accessed=10**7, transcendentals=0),
         name="pre",
-    )(rows)
-
-
-def _range_kernel(x_ref, twb_ref, hf_ref, fh_ref, fl_ref, gh_ref, gl_ref, twc_ref, o_ref, d_ref):
+    )(rows(first), rows(second))
+
+
+def _range_kernel(image, x_hbm, twb_ref, hf_ref, fh_ref, fl_ref, gh_ref, gl_ref, twc_ref, o_hbm, d_ref, x_ref, o_ref, in_sem, out_sem):
     lane = lax.broadcasted_iota(jnp.int32, (16, 128), 1)
 
+    def load(q):
+        return pltpu.make_async_copy(x_hbm.at[:, image, q], x_ref.at[:, q], in_sem.at[q])
+
+    for q in range(NQ):
+        load(q).start()
+
     def outer(q, carry):
+        load(q).wait()
         for g in range(2):
             rows = slice(8 * g, 8 * g + 8)
             v = [(x_ref[p, q, 0, rows, :], x_ref[p, q, 1, rows, :]) for p in range(NP)]
@@ -265,6 +285,10 @@
 
     lax.fori_loop(0, NQ, inner, 0)
 
+    def store(part):
+        at = pl.ds(32 * part, 32)
+        return pltpu.make_async_copy(o_ref.at[at], o_hbm.at[at], out_sem.at[part])
+
     for d in range(128):
         n, a = divmod(128 * d, NS)
         for c in range(2):
@@ -279,16 +303,27 @@
                 val = jnp.where(lane < start, val, nxt)
                 start += NS
             o_ref[worker(d), c] = val
-
-
-def range_compress(x, hf):
+        if d % 32 == 31:
+            store(d // 32).start()
+    for part in range(4):
+        store(part).wait()
+
+
+def range_compress(x, image, hf):
     t = TABLES
     return pl.pallas_call(
-        _range_kernel,
+        partial(_range_kernel, image),
+        in_specs=[HBM] + [VMEM] * 7,
+        out_specs=HBM,
         out_shape=jax.ShapeDtypeStruct((128, 2, 16, 128), F32),
-        scratch_shapes=[pltpu.VMEM((NP * NQ, 2, 16, 128), F32)],
+        scratch_shapes=[
+            pltpu.VMEM((NP * NQ, 2, 16, 128), F32),
+            pltpu.VMEM((NP, NQ, 2, 16, 128), F32),
+            pltpu.VMEM((128, 2, 16, 128), F32),
+            pltpu.SemaphoreType.DMA((NQ,)),
+            pltpu.SemaphoreType.DMA((4,)),
+        ],
         cost_estimate=pl.CostEstimate(flops=10**10, bytes_accessed=6 * 10**6, transcendentals=0),
-        compiler_params=pltpu.CompilerParams(vmem_limit_bytes=24 << 20),
         name="range",
     )(x, t["twb"], hf, t["fh"], t["fl"], t["gh"], t["gl"], t["twc"])
 
@@ -335,16 +370,22 @@
         out_shape=(shape, shape),
         scratch_shapes=[pltpu.VMEM((2, 128, 128), F32), pltpu.VMEM((2, 256, 128), F32)],
         cost_estimate=pl.CostEstimate(flops=5 * 10**9, bytes_accessed=5 * 10**6, transcendentals=0),
-        compiler_params=pltpu.CompilerParams(vmem_limit_bytes=16 << 20),
         name="prep",
     )(h, t["p"], t["w"], t["q"], t["v"])
 
 
-def _azimuth_front(x_ref, ah_ref, al_ref, e_ref):
+def _azimuth_front(x_ref, ah_hbm, al_hbm, e_ref, ah_ref, al_ref, sem):
+    matrices = [
+        pltpu.make_async_copy(ah_hbm, ah_ref, sem.at[0]),
+        pltpu.make_async_copy(al_hbm, al_ref, sem.at[1]),
+    ]
+    for copy in matrices:
+        copy.start()
+
     def first(s, carry):
         for g in range(2):
             rows = slice(8 * g, 8 * g + 8)
-            v = [(x_ref[8 * a + s, 0, rows, :], x_ref[8 * a + s, 1, rows, :]) for a in range(16)]
+            v = [(x_ref[a, s, 0, rows, :], x_ref[a, s, 1, rows, :]) for a in range(16)]
             v = dft16(v, -1)
             for k in range(16):
                 for c in range(2):
@@ -353,6 +394,8 @@
         return carry
 
     lax.fori_loop(0, 8, first, 0)
+    for copy in matrices:
+        copy.wait()
 
     def second(k, carry):
         hi, lo = split(e_ref[k])
@@ -363,14 +406,22 @@
     lax.fori_loop(0, 16, second, 0, unroll=4)
 
 
+AZIMUTH_SCRATCH = [
+    pltpu.VMEM((16, 256, 128), F32),
+    pltpu.VMEM((16, 256, 256), BF16),
+    pltpu.VMEM((16, 256, 256), BF16),
+    pltpu.SemaphoreType.DMA((4,)),
+]
+
+
 def _azimuth_rows(e_ref, g):
     at = [pl.multiple_of(c * 128 + g * 8, 8) for c in range(2)]
     v = [(e_ref[k, pl.ds(at[0], 8), :], e_ref[k, pl.ds(at[1], 8), :]) for k in range(16)]
     return dft16(v, 1)
 
 
-def _slave_kernel(x_ref, ah_ref, al_ref, o_ref, left_ref, right_ref, e_ref):
-    _azimuth_front(x_ref, ah_ref, al_ref, e_ref)
+def _slave_kernel(x_ref, ah_hbm, al_hbm, o_hbm, left_ref, right_ref, o_ref, e_ref, *scratch):
+    _azimuth_front(x_ref, ah_hbm, al_hbm, e_ref, *scratch)
     low = lax.broadcasted_iota(jnp.int32, (8, 128), 1) < 64
     zero = jnp.zeros((ASH, 128), F32)
     for ref in (o_ref.at[0], o_ref.at[1], left_ref, right_ref):
@@ -389,6 +440,9 @@
         return carry
 
     lax.fori_loop(0, 16, third, 0)
+    out = pltpu.make_async_copy(o_ref, o_hbm, scratch[-1].at[2])
+    out.start()
+    out.wait()
 
 
 def slave_azimuth(x, ah, al):
@@ -396,60 +450,85 @@
     return pl.pallas_call(
         _slave_kernel,
         out_shape=(jax.ShapeDtypeStruct((2, LINES + 2 * ASH, 128), F32), side, side),
-        scratch_shapes=[pltpu.VMEM((16, 256, 128), F32)],
+        in_specs=[VMEM, HBM, HBM],
+        out_specs=(HBM, VMEM, VMEM),
+        scratch_shapes=[pltpu.VMEM((2, LINES + 2 * ASH, 128), F32)] + AZIMUTH_SCRATCH,
+        compiler_params=limit(52),
         cost_estimate=pl.CostEstimate(flops=5 * 10**9, bytes_accessed=10**7, transcendentals=0),
-        compiler_params=pltpu.CompilerParams(vmem_limit_bytes=24 << 20),
         name="slave_azimuth",
-    )(x, ah, al)
-
-
-def _resample_kernel(az_ref, rg_ref, s_ref, left_ref, right_ref, o_ref):
+    )(x.reshape(16, 8, 2, 16, 128), ah, al)
+
+
+def _resample_kernel(az_ref, rg_ref, s_hbm, left_ref, right_ref, o_hbm, s_ref, o_ref, sem):
     lane = lax.broadcasted_iota(jnp.int32, (64, 128), 1)
     low = lane < 64
 
-    def move(t, carry):
-        block = t // 8
-        parts = []
-        for r, side_ref in ((0, left_ref), (1, right_ref)):
-            shift = rg_ref[block, r]
-            rows = pl.ds(t * 64 + ASH + az_ref[block, r], 64)
-            whole = lax.rem(256 - shift, 128)
-            half = lax.rem(192 - shift, 128)
-            near = lane + shift >= 0 if r == 0 else lane + shift < 128
-            side = side_ref[rows, :]
-            turns = (half, whole) if r == 0 else (whole, half)
-            parts.append(
-                [
-                    jnp.where(
-                        near,
-                        pltpu.roll(s_ref[c, rows, :], whole, 1),
-                        pltpu.roll(side, turns[c], 1),
-                    )
-                    for c in range(2)
-                ]
-            )
-        rows = pl.ds(pl.multiple_of(t * 64, 64), 64)
-        for c in range(2):
-            o_ref[c, rows, :] = jnp.where(low, parts[0][c], parts[1][c])
-        return carry
-
-    lax.fori_loop(0, LINES // 64, move, 0, unroll=2)
+    def load(block):
+        rows = pl.ds(0, BA + 2 * ASH) if block == 0 else pl.ds(block * BA + 2 * ASH, BA)
+        return pltpu.make_async_copy(s_hbm.at[:, rows], s_ref.at[:, rows], sem.at[block])
+
+    def store(block):
+        rows = pl.ds(block * BA, BA)
+        return pltpu.make_async_copy(o_ref.at[:, rows], o_hbm.at[:, rows], sem.at[4 + block])
+
+    for block in range(NBA):
+        load(block).start()
+    for block in range(NBA):
+        load(block).wait()
+
+        def move(t, carry):
+            parts = []
+            for r, side_ref in ((0, left_ref), (1, right_ref)):
+                shift = rg_ref[block, r]
+                rows = pl.ds(block * BA + t * 64 + ASH + az_ref[block, r], 64)
+                whole = lax.rem(256 - shift, 128)
+                half = lax.rem(192 - shift, 128)
+                near = lane + shift >= 0 if r == 0 else lane + shift < 128
+                side = side_ref[rows, :]
+                turns = (half, whole) if r == 0 else (whole, half)
+                parts.append(
+                    [
+                        jnp.where(
+                            near,
+                            pltpu.roll(s_ref[c, rows, :], whole, 1),
+                            pltpu.roll(side, turns[c], 1),
+                        )
+                        for c in range(2)
+                    ]
+                )
+            rows = pl.ds(pl.multiple_of(block * BA + t * 64, 64), 64)
+            for c in range(2):
+                o_ref[c, rows, :] = jnp.where(low, parts[0][c], parts[1][c])
+            return carry
+
+        lax.fori_loop(0, BA // 64, move, 0, unroll=2)
+        store(block).start()
+    for block in range(NBA):
+        store(block).wait()
 
 
 def resample(az_shift, rg_shift, focused, left, right):
     return pl.pallas_call(
         _resample_kernel,
-        in_specs=[pl.BlockSpec(memory_space=pltpu.SMEM)] * 2
-        + [pl.BlockSpec(memory_space=pltpu.VMEM)] * 3,
+        in_specs=[SMEM, SMEM, HBM, VMEM, VMEM],
+        out_specs=HBM,
         out_shape=jax.ShapeDtypeStruct((2, LINES, 128), F32),
+        scratch_shapes=[
+            pltpu.VMEM((2, LINES + 2 * ASH, 128), F32),
+            pltpu.VMEM((2, LINES, 128), F32),
+            pltpu.SemaphoreType.DMA((8,)),
+        ],
         cost_estimate=pl.CostEstimate(flops=2 * 10**9, bytes_accessed=10**7, transcendentals=0),
-        compiler_params=pltpu.CompilerParams(vmem_limit_bytes=16 << 20),
+        compiler_params=limit(61),
         name="resample",
     )(az_shift, rg_shift, focused, left, right)
 
 
-def _master_kernel(x_ref, ah_ref, al_ref, m_ref, n_ref, pick_ref, box_ref, side_ref, e_ref, c_ref):
-    _azimuth_front(x_ref, ah_ref, al_ref, e_ref)
+def _master_kernel(x_ref, ah_hbm, al_hbm, m_hbm, n_ref, pick_ref, box_ref, side_ref, c_ref, m_ref, e_ref, *scratch):
+    moved = pltpu.make_async_copy(m_hbm, m_ref, scratch[-1].at[2])
+    moved.start()
+    _azimuth_front(x_ref, ah_hbm, al_hbm, e_ref, *scratch)
+    moved.wait()
     line = lax.broadcasted_iota(jnp.int32, (8, 128), 0)
     count = n_ref[...]
 
@@ -486,11 +565,13 @@
             jax.ShapeDtypeStruct((16, 512), F32),
             jax.ShapeDtypeStruct((8, 512), F32),
         ),
-        scratch_shapes=[pltpu.VMEM((16, 256, 128), F32), pltpu.VMEM((2 * LINES, 128), F32)],
+        in_specs=[VMEM, HBM, HBM, HBM, VMEM, VMEM],
+        compiler_params=limit(52),
+        scratch_shapes=[pltpu.VMEM((2 * LINES, 128), F32), pltpu.VMEM((2, LINES, 128), F32)]
+        + AZIMUTH_SCRATCH,
         cost_estimate=pl.CostEstimate(flops=5 * 10**9, bytes_accessed=10**7, transcendentals=0),
-        compiler_params=pltpu.CompilerParams(vmem_limit_bytes=24 << 20),
         name="master_looks",
-    )(x, ah, al, moved, counts, TABLES["pick"])
+    )(x.reshape(16, 8, 2, 16, 128), ah, al, moved, counts, TABLES["pick"])
 
 
 def _final_kernel(box_ref, left_ref, right_ref, scale_ref, o_ref):
@@ -507,7 +588,7 @@
     return pl.pallas_call(
         _final_kernel,
         out_shape=jax.ShapeDtypeStruct((2, 16, 256), F32),
-        compiler_params=pltpu.CompilerParams(vmem_limit_bytes=4 << 20),
+        compiler_params=limit(4),
         name="final",
     )(box, left, right, scale)
 
@@ -526,9 +607,6 @@
     hf = range_ref.reshape(2, NS, NQ, NP).transpose(3, 2, 0, 1).reshape(NP * NQ, 2, NS)
     hf = jnp.pad(hf * (1.0 / RANGE), ((0, 0), (0, 0), (0, 3)))
     h = az_ref.reshape(2, 128, 16).transpose(2, 0, 1) * (1.0 / LINES)
-
-    def lines_of(raw):
-        return lax.all_to_all(pre(raw), "rg", 0, 0, tiled=True)
 
     def columns_of(ranged):
         return lax.all_to_all(ranged, ALL, 0, 0, tiled=True)
@@ -548,14 +626,13 @@
     col_counts = jnp.repeat(own, BR)[None, :]
     shifts = to_worker(jnp.stack([az_shift, rg_shift]))
 
-    slave = lines_of(slave_raw)
-    master = lines_of(master_raw)
+    lines = lax.all_to_all(pre(slave_raw, master_raw), "rg", 0, 0, tiled=True)
     ah, al = prep(h)
-    slave, ah, al, hf, shifts, scale, col_counts = lax.optimization_barrier(
-        (slave, ah, al, hf, shifts, scale, col_counts)
+    lines, ah, al, hf, shifts, scale, col_counts = lax.optimization_barrier(
+        (lines, ah, al, hf, shifts, scale, col_counts)
     )
-    slave = columns_of(range_compress(slave, hf))
-    master = columns_of(range_compress(master, hf))
+    slave = columns_of(range_compress(lines, 0, hf))
+    master = columns_of(range_compress(lines, 1, hf))
     focused, to_left, to_right = slave_azimuth(slave, ah, al)
     from_left, from_right = halo(to_right, to_left)
     moved = resample(shifts[0], shifts[1], focused, from_left, from_right)

time: 212 us -> 218 us (1.028)
  local copies, waits for them, and re-layouts: 34.7 us -> 6.77 us
  waiting for transfers between devices: 72 us -> 97.6 us
  Pallas kernels: 49.3 us -> 67.8 us
  starting transfers between devices: 52.3 us -> 42.6 us
    unnamed x82 -> x14, local copies, waits for them, and re-layouts: 28.2 us -> 1.33 us
    all_to_all x2 -> x1, waiting for transfers between devices: 30 us -> 55.6 us  [local(): lines = lax.all_to_all(pre(slave_raw, master_raw), 'rg', 0, 0, tiled=True)]
    pallas_call x3, Pallas kernels: 20 us -> 29.1 us  [the longest x2 22.3 us: range_compress(): pl.pallas_call(partial(_range_kernel, image), in_specs=[HBM] + [VMEM] * 7...]
    all_to_all x2 -> x1, starting transfers between devices: 14.6 us -> 6.49 us  [local(): lines = lax.all_to_all(pre(slave_raw, master_raw), 'rg', 0, 0, tiled=True)]
    mul x2, local copies, waits for them, and re-layouts: 4.91 us -> 1.47 us  [local(): hf = jnp.pad(hf * (1.0 / RANGE), ((0, 0), (0, 0), (0, 3)))]
    pallas_call x1, Pallas kernels: 10 us -> 13.2 us  [prep(): pl.pallas_call(_prep_kernel, out_shape=(shape, shape), scratch_shapes=[pl...]
    pallas_call x1, Pallas kernels: 7.24 us -> 9.96 us  [slave_azimuth(): pl.pallas_call(_slave_kernel, out_shape=(jax.ShapeDtypeStruct((2, LINES +...]
    pallas_call x1, Pallas kernels: 5.42 us -> 7.85 us  [master_looks(): pl.pallas_call(_master_kernel, out_shape=(jax.ShapeDtypeStruct((16, 512),...]
  transfers between devices with their start and end apart: 10 -> 9, of which waited for: 6 -> 5; matrix products, arithmetic and copies ran while one was open for 4% -> 3% of each run, Pallas kernels for 19% -> 19%
where the time goes in v3:
time: 218 us; the launch traced here: 217 us
  waiting for transfers between devices  97.6 us (45%)
  Pallas kernels  67.8 us (31%)
  starting transfers between devices  42.6 us (20%)
  local copies, waits for them, and re-layouts  6.77 us (3%)
    all_to_all x1, waiting for transfers between devices, local(): lines = lax.all_to_all(pre(slave_raw, master_raw), 'rg', 0, 0, tiled=True)  55.6 us
    pallas_call x2, Pallas kernels, range_compress(): pl.pallas_call(partial(_range_kernel, image), in_specs=[HBM] + [VMEM] * 7...  22.3 us
    all_to_all x2, starting transfers between devices, columns_of(): return lax.all_to_all(ranged, ALL, 0, 0, tiled=True)  21.6 us
    ppermute x2, waiting for transfers between devices, halo(): return (lax.ppermute(to_right, ALL, up), lax.ppermute(to_left, ALL, down))  19.8 us
    all_to_all x2, waiting for transfers between devices, columns_of(): return lax.all_to_all(ranged, ALL, 0, 0, tiled=True)  14.8 us
    pallas_call x1, Pallas kernels, prep(): pl.pallas_call(_prep_kernel, out_shape=(shape, shape), scratch_shapes=[pl...  13.2 us
    pallas_call x1, Pallas kernels, slave_azimuth(): pl.pallas_call(_slave_kernel, out_shape=(jax.ShapeDtypeStruct((2, LINES +...  9.96 us
    pallas_call x1, Pallas kernels, master_looks(): pl.pallas_call(_master_kernel, out_shape=(jax.ShapeDtypeStruct((16, 512),...  7.85 us
  transfers between devices with their start and end apart: 9, of which 5 were waited for; matrix products, arithmetic and copies ran while one was open for 3% of the time, Pallas kernels for 19%

profile of v3, /device:TPU:103, one launch (start us, length us, event | category | flops | bytes accessed | tf_op | source)
XLA Modules:
  0.0 216.6 jit_solution(11203427838592389393)
XLA Ops:
  0.0 7.0 %pre.1 = f32[16,2,10,2,16,128]{5,4,3,2,1,0:T(8,128)} custom-call(f32[5000,128]{1,0:T(8,128)} %bitcast.27, f32[5000,128]{1,0:T(8,128)} %bitcast.28), custom_call_target="tpu_custom_call" | custom-call | flops 100000000 | bytes 10000000 | tf_op jit(solution)/shard_map/pre/pallas_call | solution.py:211
  7.1 6.5 %all-to-all-start = ((f32[16,2,10,2,16,128]{5,4,3,2,1,0:T(8,128)}), f32[16,2,10,2,16,128]{5,4,3,2,1,0:T(8,128)}, u32[]{:S(2)}, u32[]{:S(2)}) async-start(f32[16,2,10,2,16,128]{5,4,3,2,1,0:T(8,128)} %pre.1), calls=%async_computation | async-start | bytes 10485760 | tf_op jit(solution)/shard_map/all_to_all | solution.py:629
  13.6 0.7 collective-permute-start
  14.3 0.1 mul.49
  14.4 0.7 copy.26
  15.2 0.7 mul.53
  15.9 0.7 copy.27
  17.2 0.6 fusion.6
  17.8 1.3 pad_add_fusion.1
  19.3 13.2 %prep.1 = (bf16[16,256,256]{2,1,0:T(8,128)(2,1)}, bf16[16,256,256]{2,1,0:T(8,128)(2,1)}) custom-call(f32[16,2,128]{2,1,0:T(2,128)} %bitcast.31, f32[2,128,128]{2,1,0:T(8,128)} %constant.77.clone.p0_ref, f32[2,128,128]{2,1,0:T(8,128)} %constant.78.clone.w_ref, f32[2,256,128]{2,1,0:T(8,128)} %constant.79.clone.q0_ref, f32[2,256,128]{2,1,0:T(8,128)} %constant.80.clone.v_ref), custom_call_target="tpu_custom_call" | custom-call | flops 5000000000 | bytes 5000000 | tf_op jit(solution)/shard_map/prep/pallas_call | solution.py:368
  32.5 0.7 pad.8.hf_ref
  33.2 55.6 %all-to-all-done.x_hbm = f32[16,2,10,2,16,128]{5,4,3,2,1,0:T(8,128)} async-done(((f32[16,2,10,2,16,128]{5,4,3,2,1,0:T(8,128)}), f32[16,2,10,2,16,128]{5,4,3,2,1,0:T(8,128)}, u32[]{:S(2)}, u32[]{:S(2)}) %all-to-all-start) | async-done | bytes 5242912 | tf_op jit(solution)/shard_map/all_to_all | solution.py:629
  88.9 11.1 %range.3 = f32[128,2,16,128]{3,2,1,0:T(8,128)} custom-call(f32[16,2,10,2,16,128]{5,4,3,2,1,0:T(8,128)} %all-to-all-done.x_hbm, f32[10,2,128]{2,1,0:T(2,128)} %constant.81.clone.twb_ref, f32[160,2,128]{2,1,0:T(2,128)} %pad.8.hf_ref, bf16[256,256]{1,0:T(8,128)(2,1)} %constant.82.clone.fh_ref, bf16[256,256]{1,0:T(8,128)(2,1)} %constant.83.clone.fl_ref, ...), custom_call_target="tpu_custom_call" | custom-call | flops 10000000000 | bytes 6000000 | tf_op jit(solution)/shard_map/range/pallas_call | solution.py:314
  100.0 12.1 %all-to-all-start.2 = ((f32[128,2,16,128]{3,2,1,0:T(8,128)}), f32[128,2,16,128]{3,2,1,0:T(8,128)S(1)}, u32[]{:S(2)}, u32[]{:S(2)}) async-start(f32[128,2,16,128]{3,2,1,0:T(8,128)} %range.3), calls=%async_computation.2 | async-start | bytes 4194304 | tf_op jit(solution)/shard_map/all_to_all | solution.py:612
  112.1 11.2 %range.2 = f32[128,2,16,128]{3,2,1,0:T(8,128)} custom-call(f32[16,2,10,2,16,128]{5,4,3,2,1,0:T(8,128)} %all-to-all-done.x_hbm, f32[10,2,128]{2,1,0:T(2,128)} %constant.81.clone.twb_ref, f32[160,2,128]{2,1,0:T(2,128)} %pad.8.hf_ref, bf16[256,256]{1,0:T(8,128)(2,1)} %constant.82.clone.fh_ref, bf16[256,256]{1,0:T(8,128)(2,1)} %constant.83.clone.fl_ref, ...), custom_call_target="tpu_custom_call" | custom-call | flops 10000000000 | bytes 6000000 | tf_op jit(solution)/shard_map/range/pallas_call | solution.py:314
  123.3 14.8 %all-to-all-done.2 = f32[128,2,16,128]{3,2,1,0:T(8,128)S(1)} async-done(((f32[128,2,16,128]{3,2,1,0:T(8,128)}), f32[128,2,16,128]{3,2,1,0:T(8,128)S(1)}, u32[]{:S(2)}, u32[]{:S(2)}) %all-to-all-start.2) | async-done | bytes 2097184 | tf_op jit(solution)/shard_map/all_to_all | solution.py:612
  138.1 1.3 copy-done.1
  139.4 9.5 %all-to-all-start.1 = ((f32[128,2,16,128]{3,2,1,0:T(8,128)}), f32[128,2,16,128]{3,2,1,0:T(8,128)}, u32[]{:S(2)}, u32[]{:S(2)}) async-start(f32[128,2,16,128]{3,2,1,0:T(8,128)} %range.2), calls=%async_computation.1 | async-start | bytes 4194304 | tf_op jit(solution)/shard_map/all_to_all | solution.py:612
  148.9 10.0 %slave_azimuth.1 = (f32[2,2112,128]{2,1,0:T(8,128)}, f32[2112,128]{1,0:T(8,128)S(1)}, f32[2112,128]{1,0:T(8,128)}) custom-call(f32[16,8,2,16,128]{4,3,2,1,0:T(8,128)} %bitcast.29, bf16[16,256,256]{2,1,0:T(8,128)(2,1)} %get-tuple-element.23.ah_hbm, bf16[16,256,256]{2,1,0:T(8,128)(2,1)} %get-tuple-element.24.al_hbm), custom_call_target="tpu_custom_call" | custom-call | flops 5000000000 | bytes 10000000 | tf_op jit(solution)/shard_map/slave_azimuth/pallas_call | solution.py:450
  158.9 2.6 %collective-permute-start.1 = (f32[2112,128]{1,0:T(8,128)}, f32[2112,128]{1,0:T(8,128)}, u32[]{:S(2)}, u32[]{:S(2)}) collective-permute-start(f32[2112,128]{1,0:T(8,128)} %get-tuple-element.27), channel_id=1, source_target_pairs={{0,16},{16,1},{1,17},{17,2},{2,18},{18,3},{3,19},{19,4},{4,20},{20... | collective-permute-start | bytes 3244040 | tf_op jit(solution)/shard_map/ppermute | solution.py:603
  161.4 1.9 collective-permute-start.2
  163.4 0.7 copy.28.az_ref
  164.0 0.7 copy.29.rg_ref
  164.7 18.0 %collective-permute-done.1.left_ref = f32[2112,128]{1,0:T(8,128)} collective-permute-done((f32[2112,128]{1,0:T(8,128)}, f32[2112,128]{1,0:T(8,128)}, u32[]{:S(2)}, u32[]{:S(2)}) %collective-permute-start.1) | collective-permute-done | bytes 1081376 | tf_op jit(solution)/shard_map/ppermute | solution.py:603
  182.7 1.9 collective-permute-done.2.right_ref
  184.6 6.8 %resample.1.m_hbm = f32[2,2048,128]{2,1,0:T(8,128)} custom-call(s32[4,2]{1,0:T(4,128)} %copy.28.az_ref, s32[4,2]{1,0:T(4,128)} %copy.29.rg_ref, f32[2,2112,128]{2,1,0:T(8,128)} %get-tuple-element.26.s_hbm, f32[2112,128]{1,0:T(8,128)} %collective-permute-done.1.left_ref, f32[2112,128]{1,0:T(8,128)} %collective-permute-done.2.right_ref), custom_call_target="tpu_custom_call" | custom-call | flops 2000000000 | bytes 10000000 | tf_op jit(solution)/shard_map/resample/pallas_call | solution.py:511
  191.4 7.8 %master_looks.1 = (f32[16,512]{1,0:T(8,128)S(1)}, f32[8,512]{1,0:T(8,128)S(1)}) custom-call(f32[16,8,2,16,128]{4,3,2,1,0:T(8,128)} %bitcast.13.x_ref, bf16[16,256,256]{2,1,0:T(8,128)(2,1)} %get-tuple-element.23.ah_hbm, bf16[16,256,256]{2,1,0:T(8,128)(2,1)} %get-tuple-element.24.al_hbm, f32[2,2048,128]{2,1,0:T(8,128)} %resample.1.m_hbm, ...), custom_call_target="tpu_custom_call" | custom-call | flops 5000000000 | bytes 10000000 | tf_op jit(solution)/shard_map/master_looks/pallas_call | solution.py:562
  199.2 0.7 collective-permute-start.3
  199.9 6.8 %collective-permute-start.4 = (f32[8,512]{1,0:T(8,128)S(1)}, f32[8,512]{1,0:T(8,128)S(1)}, u32[]{:S(2)}, u32[]{:S(2)}) collective-permute-start(f32[8,512]{1,0:T(8,128)S(1)} %get-tuple-element.31), channel_id=1, source_target_pairs={{0,1},{16,2},{1,3},{17,4},{2,5},{18,6},{3,7},{19,8},{4,9},{20,10},... | collective-permute-start | bytes 49160 | tf_op jit(solution)/shard_map/ppermute | solution.py:642
  206.7 1.9 collective-permute-start.5
  208.7 7.3 %collective-permute-done.5.right_ref = f32[8,512]{1,0:T(8,128)S(1)} collective-permute-done((f32[8,512]{1,0:T(8,128)S(1)}, f32[8,512]{1,0:T(8,128)S(1)}, u32[]{:S(2)}, u32[]{:S(2)}) %collective-permute-start.5) | collective-permute-done | bytes 16416 | tf_op jit(solution)/shard_map/ppermute | solution.py:643
  216.0 0.6 final.1
  (32 shorter events, 0.9 us)
Async XLA Ops:
  7.0 6.5 %copy-start.5 = (s32[4,2]{0,1:T(2,128)S(1)}, s32[4,2]{0,1:T(2,128)}, u32[]{:S(2)}) copy-start(s32[4,2]{0,1:T(2,128)} %param.23) | copy-start | bytes 100
  7.0 6.5 %copy-start.6 = (s32[4,2]{0,1:T(2,128)S(1)}, s32[4,2]{0,1:T(2,128)}, u32[]{:S(2)}) copy-start(s32[4,2]{0,1:T(2,128)} %param.22) | copy-start | bytes 100
  7.0 7.2 %copy-start.3 = (f32[2,2048]{1,0:T(2,128)S(1)}, f32[2,2048]{1,0:T(2,128)}, u32[]{:S(2)}) copy-start(f32[2,2048]{1,0:T(2,128)} %param.21) | copy-start | bytes 49156
  7.0 8.0 %copy-start.2 = (f32[2,20000]{1,0:T(2,128)S(1)}, f32[2,20000]{1,0:T(2,128)}, u32[]{:S(2)}) copy-start(f32[2,20000]{1,0:T(2,128)} %param.20) | copy-start | bytes 480004
  7.1 81.8 %all-to-all-start = ((f32[16,2,10,2,16,128]{5,4,3,2,1,0:T(8,128)}), f32[16,2,10,2,16,128]{5,4,3,2,1,0:T(8,128)}, u32[]{:S(2)}, u32[]{:S(2)}) async-start(f32[16,2,10,2,16,128]{5,4,3,2,1,0:T(8,128)} %pre.1), calls=%async_computation | async-start | bytes 10485760 | tf_op jit(solution)/shard_map/all_to_all | solution.py:629
  13.6 19.7 %collective-permute-start = (s32[2,4,2]{1,2,0:T(2,128)S(1)}, s32[2,4,2]{1,2,0:T(2,128)S(1)}, u32[]{:S(2)}, u32[]{:S(2)}) collective-permute-start(s32[2,4,2]{1,2,0:T(2,128)S(1)} %pad_add_fusion), channel_id=1, source_target_pairs={{0,0},{1,16},{2,1},{3,17},{4,2},{5,18},{6,3},{7,19},{8,4},{9,20},{... | collective-permute-start | bytes 200 | tf_op jit(solution)/shard_map/ppermute | solution.py:597
  15.2 1.5 copy-start.4
  100.0 38.1 %all-to-all-start.2 = ((f32[128,2,16,128]{3,2,1,0:T(8,128)}), f32[128,2,16,128]{3,2,1,0:T(8,128)S(1)}, u32[]{:S(2)}, u32[]{:S(2)}) async-start(f32[128,2,16,128]{3,2,1,0:T(8,128)} %range.3), calls=%async_computation.2 | async-start | bytes 4194304 | tf_op jit(solution)/shard_map/all_to_all | solution.py:612
  138.1 1.3 copy-start.1
  139.4 51.9 %all-to-all-start.1 = ((f32[128,2,16,128]{3,2,1,0:T(8,128)}), f32[128,2,16,128]{3,2,1,0:T(8,128)}, u32[]{:S(2)}, u32[]{:S(2)}) async-start(f32[128,2,16,128]{3,2,1,0:T(8,128)} %range.2), calls=%async_computation.1 | async-start | bytes 4194304 | tf_op jit(solution)/shard_map/all_to_all | solution.py:612
  158.9 23.8 %collective-permute-start.1 = (f32[2112,128]{1,0:T(8,128)}, f32[2112,128]{1,0:T(8,128)}, u32[]{:S(2)}, u32[]{:S(2)}) collective-permute-start(f32[2112,128]{1,0:T(8,128)} %get-tuple-element.27), channel_id=1, source_target_pairs={{0,16},{16,1},{1,17},{17,2},{2,18},{18,3},{3,19},{19,4},{4,20},{20... | collective-permute-start | bytes 3244040 | tf_op jit(solution)/shard_map/ppermute | solution.py:603
  161.4 23.1 %collective-permute-start.2 = (f32[2112,128]{1,0:T(8,128)S(1)}, f32[2112,128]{1,0:T(8,128)}, u32[]{:S(2)}, u32[]{:S(2)}) collective-permute-start(f32[2112,128]{1,0:T(8,128)S(1)} %get-tuple-element.28), channel_id=1, source_target_pairs={{16,0},{1,16},{17,1},{2,17},{18,2},{3,18},{19,3},{4,19},{20,4},{5,... | collective-permute-start | bytes 3244040 | tf_op jit(solution)/shard_map/ppermute | solution.py:603
  184.6 6.8 %copy-start = (f32[24,128]{1,0:T(8,128)S(1)}, f32[24,128]{1,0:T(8,128)}, u32[]{:S(2)}) copy-start(f32[24,128]{1,0:T(8,128)} %constant.87.clone.pick_ref) | copy-start | bytes 36868
  199.2 16.8 %collective-permute-start.3 = (f32[16,512]{1,0:T(8,128)S(1)}, f32[16,512]{1,0:T(8,128)S(1)}, u32[]{:S(2)}, u32[]{:S(2)}) collective-permute-start(f32[16,512]{1,0:T(8,128)S(1)} %get-tuple-element.30), channel_id=1, source_target_pairs={{0,0},{16,1},{1,2},{17,3},{2,4},{18,5},{3,6},{19,7},{4,8},{20,9},{... | collective-permute-start | bytes 98312 | tf_op jit(solution)/shard_map/ppermute | solution.py:641
  199.9 8.8 %collective-permute-start.4 = (f32[8,512]{1,0:T(8,128)S(1)}, f32[8,512]{1,0:T(8,128)S(1)}, u32[]{:S(2)}, u32[]{:S(2)}) collective-permute-start(f32[8,512]{1,0:T(8,128)S(1)} %get-tuple-element.31), channel_id=1, source_target_pairs={{0,1},{16,2},{1,3},{17,4},{2,5},{18,6},{3,7},{19,8},{4,9},{20,10},... | collective-permute-start | bytes 49160 | tf_op jit(solution)/shard_map/ppermute | solution.py:642
  206.7 9.3 %collective-permute-start.5 = (f32[8,512]{1,0:T(8,128)S(1)}, f32[8,512]{1,0:T(8,128)S(1)}, u32[]{:S(2)}, u32[]{:S(2)}) collective-permute-start(f32[8,512]{1,0:T(8,128)S(1)} %get-tuple-element.31), channel_id=1, source_target_pairs={{16,0},{1,1},{17,2},{2,3},{18,4},{3,5},{19,6},{4,7},{20,8},{5,9},{... | collective-permute-start | bytes 49160 | tf_op jit(solution)/shard_map/ppermute | solution.py:643

commit v4 on v3

--- a/solution.py
+++ b/solution.py
@@ -1,5 +1,4 @@
 import math
-from functools import partial
 
 import jax
 import jax.numpy as jnp
@@ -9,22 +8,30 @@
 from jax.experimental.pallas import tpu as pltpu
 from jax.sharding import PartitionSpec as P
 
+
 LINES = 2048
 RANGE = 20000
-RV = 16384
 LOOK = 8
 BA = 512
 BR = 64
 ASH = 32
-RSH = 64
 NBA = 4
 ALL = ("az", "rg")
 NP = 16
 NQ = 10
 NS = 125
-RPAD = 1280
 F32 = jnp.float32
 BF16 = jnp.bfloat16
+
+
+SHIFTS = sorted(
+    ((dx, dz) for dx in range(4) for dz in range(4)),
+    key=lambda s: -(min(s[0], 4 - s[0]) + min(s[1], 4 - s[1])),
+)
+
+
+def shifted(r, shift):
+    return ((r // 4 + shift[1]) % 4) * 4 + (r % 4 + shift[0]) % 4
 
 
 def _rot(v, angle):
@@ -192,44 +199,63 @@
     return pltpu.CompilerParams(vmem_limit_bytes=mib << 20)
 
 
-def _pre_kernel(first_ref, second_ref, o_ref):
-    for image, x_ref in enumerate((first_ref, second_ref)):
-        for q in range(2):
-            for half in range(2):
-                for c in range(2):
-                    v = x_ref[pl.ds(500 * q + 2 * half + c, NS, stride=4), :]
-                    v = jnp.concatenate([v, jnp.zeros((128 - NS, 128), F32)], axis=0).T
-                    for k in range(8):
-                        o_ref[8 * half + k, image, q, c] = v[16 * k : 16 * k + 16]
-
-
-def pre(first, second):
-    def rows(raw):
-        raw = raw.transpose(2, 0, 1).reshape(1250, 2, 2, 128)
-        return raw.transpose(0, 2, 1, 3).reshape(5000, 128)
-
+def _line_tile(x_ref, q, half, c):
+    v = x_ref[pl.ds(500 * q + 2 * half + c, NS, stride=4), :]
+    return jnp.concatenate([v, jnp.zeros((128 - NS, 128), F32)], axis=0).T
+
+
+def _pre_kernel(x_ref, o_ref):
+    for q in range(2):
+        for half in range(2):
+            for c in range(2):
+                v = _line_tile(x_ref, q, half, c)
+                for k in range(8):
+                    o_ref[8 * half + k, q, c] = v[16 * k : 16 * k + 16]
+
+
+def _pre_shift_kernel(me_ref, x_ref, *refs):
+    outs, t_ref = refs[:-1], refs[-1]
+    _pre_kernel(x_ref, t_ref)
+    me = me_ref[0]
+    for shift, o_ref in zip(SHIFTS, outs):
+        o_ref[...] = t_ref[shifted(me, shift)]
+
+
+def _raw_rows(raw):
+    raw = raw.transpose(2, 0, 1).reshape(1250, 2, 2, 128)
+    return raw.transpose(0, 2, 1, 3).reshape(5000, 128)
+
+
+def pre(raw):
     return pl.pallas_call(
         _pre_kernel,
         grid=(5,),
-        in_specs=[pl.BlockSpec((1000, 128), lambda i: (i, 0))] * 2,
-        out_specs=pl.BlockSpec((NP, 2, 2, 2, 16, 128), lambda i: (0, 0, i, 0, 0, 0)),
-        out_shape=jax.ShapeDtypeStruct((NP, 2, NQ, 2, 16, 128), F32),
+        in_specs=[pl.BlockSpec((1000, 128), lambda i: (i, 0))],
+        out_specs=pl.BlockSpec((NP, 2, 2, 16, 128), lambda i: (0, i, 0, 0, 0)),
+        out_shape=jax.ShapeDtypeStruct((NP, NQ, 2, 16, 128), F32),
         cost_estimate=pl.CostEstimate(flops=10**8, bytes_accessed=10**7, transcendentals=0),
         name="pre",
-    )(rows(first), rows(second))
-
-
-def _range_kernel(image, x_hbm, twb_ref, hf_ref, fh_ref, fl_ref, gh_ref, gl_ref, twc_ref, o_hbm, d_ref, x_ref, o_ref, in_sem, out_sem):
+    )(_raw_rows(raw))
+
+
+def pre_shifts(me, raw):
+    return pl.pallas_call(
+        _pre_shift_kernel,
+        grid=(5,),
+        in_specs=[SMEM, pl.BlockSpec((1000, 128), lambda i: (i, 0))],
+        out_specs=[pl.BlockSpec((2, 2, 16, 128), lambda i: (i, 0, 0, 0))] * NP,
+        out_shape=[jax.ShapeDtypeStruct((NQ, 2, 16, 128), F32)] * NP,
+        scratch_shapes=[pltpu.VMEM((NP, 2, 2, 16, 128), F32)],
+        cost_estimate=pl.CostEstimate(flops=10**8, bytes_accessed=10**7, transcendentals=0),
+        name="pre_shifts",
+    )(me, _raw_rows(raw))
+
+
+def _range_body(ready, twb_ref, hf_ref, fh_ref, fl_ref, gh_ref, gl_ref, twc_ref, o_hbm, d_ref, x_ref, o_ref, out_sem):
     lane = lax.broadcasted_iota(jnp.int32, (16, 128), 1)
 
-    def load(q):
-        return pltpu.make_async_copy(x_hbm.at[:, image, q], x_ref.at[:, q], in_sem.at[q])
-
-    for q in range(NQ):
-        load(q).start()
-
     def outer(q, carry):
-        load(q).wait()
+        ready(q)
         for g in range(2):
             rows = slice(8 * g, 8 * g + 8)
             v = [(x_ref[p, q, 0, rows, :], x_ref[p, q, 1, rows, :]) for p in range(NP)]
@@ -309,23 +335,50 @@
         store(part).wait()
 
 
-def range_compress(x, image, hf):
+def _range_kernel(x_hbm, *refs):
+    in_sem, x_ref = refs[-1], refs[-4]
+
+    def load(q):
+        return pltpu.make_async_copy(x_hbm.at[:, q], x_ref.at[:, q], in_sem.at[q])
+
+    for q in range(NQ):
+        load(q).start()
+    _range_body(lambda q: load(q).wait(), *refs[:-1])
+
+
+def _range_shift_kernel(me_ref, *refs):
+    parts, refs = refs[:NP], refs[NP:]
+    in_sem, x_ref = refs[-1], refs[-4]
+    me = me_ref[0]
+    loads = [
+        pltpu.make_async_copy(
+            part, x_ref.at[shifted(me, (4 - shift[0], 4 - shift[1]))], in_sem.at[k]
+        )
+        for k, (shift, part) in enumerate(zip(SHIFTS, parts))
+    ]
+    for load in loads:
+        load.start()
+    for load in loads:
+        load.wait()
+    _range_body(lambda q: None, *refs[:-1])
+
+
+def range_compress(kernel, specs, operands, hf):
     t = TABLES
     return pl.pallas_call(
-        partial(_range_kernel, image),
-        in_specs=[HBM] + [VMEM] * 7,
+        kernel,
+        in_specs=specs + [VMEM] * 7,
         out_specs=HBM,
         out_shape=jax.ShapeDtypeStruct((128, 2, 16, 128), F32),
         scratch_shapes=[
             pltpu.VMEM((NP * NQ, 2, 16, 128), F32),
             pltpu.VMEM((NP, NQ, 2, 16, 128), F32),
             pltpu.VMEM((128, 2, 16, 128), F32),
-            pltpu.SemaphoreType.DMA((NQ,)),
             pltpu.SemaphoreType.DMA((4,)),
+            pltpu.SemaphoreType.DMA((NP,)),
         ],
         cost_estimate=pl.CostEstimate(flops=10**10, bytes_accessed=6 * 10**6, transcendentals=0),
-        name="range",
-    )(x, t["twb"], hf, t["fh"], t["fl"], t["gh"], t["gl"], t["twc"])
+    )(*operands, t["twb"], hf, t["fh"], t["fl"], t["gh"], t["gl"], t["twc"])
 
 
 def _dot_t(a, b):
@@ -626,13 +679,22 @@
     col_counts = jnp.repeat(own, BR)[None, :]
     shifts = to_worker(jnp.stack([az_shift, rg_shift]))
 
-    lines = lax.all_to_all(pre(slave_raw, master_raw), "rg", 0, 0, tiled=True)
+    slave = pre(slave_raw)
+    slave = lax.all_to_all(slave, "rg", 0, 0, tiled=True)
+    me = lax.axis_index("rg").astype(jnp.int32)[None]
+    pieces = pre_shifts(me, master_raw)
+    master = [
+        lax.ppermute(piece, "rg", [(r, shifted(r, shift)) for r in range(NP)])
+        if any(shift)
+        else piece
+        for shift, piece in zip(SHIFTS, pieces)
+    ]
+    slave, hf, scale, col_counts = lax.optimization_barrier((slave, hf, scale, col_counts))
+    slave = range_compress(_range_kernel, [HBM], [slave], hf)
+    slave = columns_of(slave)
     ah, al = prep(h)
-    lines, ah, al, hf, shifts, scale, col_counts = lax.optimization_barrier(
-        (lines, ah, al, hf, shifts, scale, col_counts)
-    )
-    slave = columns_of(range_compress(lines, 0, hf))
-    master = columns_of(range_compress(lines, 1, hf))
+    master = range_compress(_range_shift_kernel, [SMEM] + [HBM] * NP, [me, *master], hf)
+    master = columns_of(master)
     focused, to_left, to_right = slave_azimuth(slave, ah, al)
     from_left, from_right = halo(to_right, to_left)
     moved = resample(shifts[0], shifts[1], focused, from_left, from_right)

time: 218 us -> 238 us (1.092); the launches traced: 217 us -> 234 us
  starting transfers between devices: 42.6 us -> 58.4 us
  waiting for transfers between devices: 97.6 us -> 92.9 us
  Pallas kernels: 67.8 us -> 72.1 us
    ppermute x0 -> x15, waiting for transfers between devices: none -> 39.1 us  [local(): lax.ppermute(piece, 'rg', [(r, shifted(r, shift)) for r in range(NP)])]
    all_to_all x1, waiting for transfers between devices: 55.6 us -> 29.6 us  [local(): slave = lax.all_to_all(slave, 'rg', 0, 0, tiled=True)]
    ppermute x0 -> x15, starting transfers between devices: none -> 18.7 us  [local(): lax.ppermute(piece, 'rg', [(r, shifted(r, shift)) for r in range(NP)])]
    all_to_all x2, waiting for transfers between devices: 14.8 us -> 0.01 us  [columns_of(): return lax.all_to_all(ranged, ALL, 0, 0, tiled=True)]
    pallas_call x2 -> x3, Pallas kernels: 22.3 us -> 28.5 us  [the longest x2 23.3 us: range_compress(): pl.pallas_call(kernel, in_specs=specs + [VMEM] * 7, out_specs=HBM, out_sh...]
    ppermute x1, starting transfers between devices: 6.83 us -> 1.92 us  [local(): left = lax.ppermute(side, ALL, [(worker(b), b + 1) for b in range(127)])]
    ppermute x2, waiting for transfers between devices: 19.8 us -> 16.7 us  [halo(): return (lax.ppermute(to_right, ALL, up), lax.ppermute(to_left, ALL, down))]
  transfers between devices with their start and end apart: 9 -> 24, of which waited for: 5 -> 10; matrix products, arithmetic and copies ran while one was open for 3% -> 3% of each run, Pallas kernels for 19% -> 20%
where the time goes in v4:
time: 238 us; the launch traced here: 234 us
  waiting for transfers between devices  92.9 us (39%)
  Pallas kernels  72.1 us (30%)
  starting transfers between devices  58.4 us (25%)
  local copies, waits for them, and re-layouts  8.54 us (4%)
    ppermute x15, waiting for transfers between devices, local(): lax.ppermute(piece, 'rg', [(r, shifted(r, shift)) for r in range(NP)])  39.1 us
    all_to_all x1, waiting for transfers between devices, local(): slave = lax.all_to_all(slave, 'rg', 0, 0, tiled=True)  29.6 us
    all_to_all x2, starting transfers between devices, columns_of(): return lax.all_to_all(ranged, ALL, 0, 0, tiled=True)  23.5 us
    pallas_call x2, Pallas kernels, range_compress(): pl.pallas_call(kernel, in_specs=specs + [VMEM] * 7, out_specs=HBM, out_sh...  23.3 us
    ppermute x15, starting transfers between devices, local(): lax.ppermute(piece, 'rg', [(r, shifted(r, shift)) for r in range(NP)])  18.7 us
    ppermute x2, waiting for transfers between devices, halo(): return (lax.ppermute(to_right, ALL, up), lax.ppermute(to_left, ALL, down))  16.7 us
    pallas_call x1, Pallas kernels, prep(): pl.pallas_call(_prep_kernel, out_shape=(shape, shape), scratch_shapes=[pl...  13.3 us
    pallas_call x1, Pallas kernels, slave_azimuth(): pl.pallas_call(_slave_kernel, out_shape=(jax.ShapeDtypeStruct((2, LINES +...  9.96 us
  transfers between devices with their start and end apart: 24, of which 10 were waited for; matrix products, arithmetic and copies ran while one was open for 3% of the time, Pallas kernels for 20%

profile of v4, /device:TPU:103, one launch (start us, length us, event | category | flops | bytes accessed | tf_op | source)
XLA Modules:
  0.0 234.0 jit_solution(9258240636524406646)
XLA Ops:
  0.0 5.2 %pre.1 = f32[16,10,2,16,128]{4,3,2,1,0:T(8,128)} custom-call(f32[5000,128]{1,0:T(8,128)} %bitcast.28), custom_call_target="tpu_custom_call" | custom-call | flops 100000000 | bytes 10000000 | tf_op jit(solution)/shard_map/pre/pallas_call | solution.py:230
  5.2 6.5 %all-to-all-start = ((f32[16,10,2,16,128]{4,3,2,1,0:T(8,128)}), f32[16,10,2,16,128]{4,3,2,1,0:T(8,128)}, u32[]{:S(2)}, u32[]{:S(2)}) async-start(f32[16,10,2,16,128]{4,3,2,1,0:T(8,128)} %pre.1), calls=%async_computation | async-start | bytes 5242880 | tf_op jit(solution)/shard_map/all_to_all | solution.py:683
  15.2 1.4 pad_add_fusion.1
  16.8 29.6 %all-to-all-done.x_hbm = f32[16,10,2,16,128]{4,3,2,1,0:T(8,128)} async-done(((f32[16,10,2,16,128]{4,3,2,1,0:T(8,128)}), f32[16,10,2,16,128]{4,3,2,1,0:T(8,128)}, u32[]{:S(2)}, u32[]{:S(2)}) %all-to-all-start) | async-done | bytes 2621472 | tf_op jit(solution)/shard_map/all_to_all | solution.py:683
  46.4 11.2 %shard_map.173 = f32[128,2,16,128]{3,2,1,0:T(8,128)} custom-call(f32[16,10,2,16,128]{4,3,2,1,0:T(8,128)} %all-to-all-done.x_hbm, f32[10,2,128]{2,1,0:T(2,128)} %constant.77.clone.refs_16_.refs_0_, f32[160,2,128]{2,1,0:T(2,128)} %pad.8.refs_17_.refs_1_, bf16[256,256]{1,0:T(8,128)(2,1)} %constant.78.clone.refs_18_.refs_2_, ...), custom_call_target="tpu_custom_call" | custom-call | flops 10000000000 | bytes 6000000 | tf_op jit(solution)/shard_map/pallas_call | solution.py:368
  57.6 12.6 %all-to-all-start.2 = ((f32[128,2,16,128]{3,2,1,0:T(8,128)}), f32[128,2,16,128]{3,2,1,0:T(8,128)S(1)}, u32[]{:S(2)}, u32[]{:S(2)}) async-start(f32[128,2,16,128]{3,2,1,0:T(8,128)} %shard_map.173), calls=%async_computation.2 | async-start | bytes 4194304 | tf_op jit(solution)/shard_map/all_to_all | solution.py:665
  70.3 5.1 %pre_shifts.1 = (f32[10,2,16,128]{3,2,1,0:T(8,128)}, f32[10,2,16,128]{3,2,1,0:T(8,128)}, f32[10,2,16,128]{3,2,1,0:T(8,128)}, f32[10,2,16,128]{3,2,1,0:T(8,128)},...) custom-call(s32[1]{0:T(128)} %bitcast.me_ref, ...), custom_call_target="tpu_custom_call" | custom-call | flops 100000000 | bytes 10000000 | tf_op jit(solution)/shard_map/pre_shifts/pallas_call | solution.py:242
  75.4 1.6 collective-permute-start
  77.0 3.8 %collective-permute-start.1 = (f32[10,2,16,128]{3,2,1,0:T(8,128)}, f32[10,2,16,128]{3,2,1,0:T(8,128)S(1)}, u32[]{:S(2)}, u32[]{:S(2)}) collective-permute-start(f32[10,2,16,128]{3,2,1,0:T(8,128)} %get-tuple-element.33), channel_id=1, source_target_pairs={{0,9},{1,10},{2,11},{3,8},{4,13},{5,14},{6,15},{7,12},{8,1},{9,2},... | collective-permute-start | bytes 491528 | tf_op jit(solution)/shard_map/ppermute | solution.py:687
  80.9 2.1 collective-permute-start.11
  82.9 18.4 %collective-permute-done.refs_0_ = f32[10,2,16,128]{3,2,1,0:T(8,128)S(1)} collective-permute-done((f32[10,2,16,128]{3,2,1,0:T(8,128)}, f32[10,2,16,128]{3,2,1,0:T(8,128)S(1)}, u32[]{:S(2)}, u32[]{:S(2)}) %collective-permute-start) | collective-permute-done | bytes 163872 | tf_op jit(solution)/shard_map/ppermute | solution.py:687
  101.9 5.0 %collective-permute-done.1.refs_1_ = f32[10,2,16,128]{3,2,1,0:T(8,128)S(1)} collective-permute-done((f32[10,2,16,128]{3,2,1,0:T(8,128)}, f32[10,2,16,128]{3,2,1,0:T(8,128)S(1)}, u32[]{:S(2)}, u32[]{:S(2)}) %collective-permute-start.1) | collective-permute-done | bytes 163872 | tf_op jit(solution)/shard_map/ppermute | solution.py:687
  107.0 3.8 %collective-permute-start.3 = (f32[10,2,16,128]{3,2,1,0:T(8,128)}, f32[10,2,16,128]{3,2,1,0:T(8,128)S(1)}, u32[]{:S(2)}, u32[]{:S(2)}) collective-permute-start(f32[10,2,16,128]{3,2,1,0:T(8,128)} %get-tuple-element.35), channel_id=1, source_target_pairs={{0,14},{1,15},{2,12},{3,13},{4,2},{5,3},{6,0},{7,1},{8,6},{9,7},{1... | collective-permute-start | bytes 491528 | tf_op jit(solution)/shard_map/ppermute | solution.py:687
  113.4 6.8 %collective-permute-done.14.refs_14_ = f32[10,2,16,128]{3,2,1,0:T(8,128)S(1)} collective-permute-done((f32[10,2,16,128]{3,2,1,0:T(8,128)}, f32[10,2,16,128]{3,2,1,0:T(8,128)S(1)}, u32[]{:S(2)}, u32[]{:S(2)}) %collective-permute-start.14) | collective-permute-done | bytes 163872 | tf_op jit(solution)/shard_map/ppermute | solution.py:687
  120.3 4.0 %collective-permute-start.8 = (f32[10,2,16,128]{3,2,1,0:T(8,128)}, f32[10,2,16,128]{3,2,1,0:T(8,128)}, u32[]{:S(2)}, u32[]{:S(2)}) collective-permute-start(f32[10,2,16,128]{3,2,1,0:T(8,128)} %get-tuple-element.40), channel_id=1, source_target_pairs={{0,2},{1,3},{2,0},{3,1},{4,6},{5,7},{6,4},{7,5},{8,10},{9,11},{10,... | collective-permute-start | bytes 491528 | tf_op jit(solution)/shard_map/ppermute | solution.py:687
  124.3 2.9 %collective-permute-done.4.refs_4_ = f32[10,2,16,128]{3,2,1,0:T(8,128)S(1)} collective-permute-done((f32[10,2,16,128]{3,2,1,0:T(8,128)}, f32[10,2,16,128]{3,2,1,0:T(8,128)S(1)}, u32[]{:S(2)}, u32[]{:S(2)}) %collective-permute-start.4) | collective-permute-done | bytes 163872 | tf_op jit(solution)/shard_map/ppermute | solution.py:687
  128.7 1.5 collective-permute-done.7.refs_7_
  130.3 4.6 %collective-permute-done.9.refs_9_ = f32[10,2,16,128]{3,2,1,0:T(8,128)} collective-permute-done((f32[10,2,16,128]{3,2,1,0:T(8,128)}, f32[10,2,16,128]{3,2,1,0:T(8,128)}, u32[]{:S(2)}, u32[]{:S(2)}) %collective-permute-start.9) | collective-permute-done | bytes 163872 | tf_op jit(solution)/shard_map/ppermute | solution.py:687
  134.9 12.1 %shard_map.172 = f32[128,2,16,128]{3,2,1,0:T(8,128)} custom-call(s32[1]{0:T(128)} %bitcast.me_ref, f32[10,2,16,128]{3,2,1,0:T(8,128)} %copy-done.9, f32[10,2,16,128]{3,2,1,0:T(8,128)} %copy-done.10, f32[10,2,16,128]{3,2,1,0:T(8,128)} %copy-done.16, f32[10,2,16,128]{3,2,1,0:T(8,128)} %copy-done.17, f32[10,2,16,128]{3,2,1,0:T(8,128)} %copy-done.18, ...), custom_call_target="tpu_custom_call" | custom-call | flops 10000000000 | bytes 6000000 | tf_op jit(solution)/shard_map/pallas_call | solution.py:368
  147.0 1.3 copy-done.1
  148.3 10.9 %all-to-all-start.1 = ((f32[128,2,16,128]{3,2,1,0:T(8,128)}), f32[128,2,16,128]{3,2,1,0:T(8,128)}, u32[]{:S(2)}, u32[]{:S(2)}) async-start(f32[128,2,16,128]{3,2,1,0:T(8,128)} %shard_map.172), calls=%async_computation.1 | async-start | bytes 4194304 | tf_op jit(solution)/shard_map/all_to_all | solution.py:665
  159.2 13.3 %prep.1 = (bf16[16,256,256]{2,1,0:T(8,128)(2,1)}, bf16[16,256,256]{2,1,0:T(8,128)(2,1)}) custom-call(f32[16,2,128]{2,1,0:T(2,128)} %bitcast.32, f32[2,128,128]{2,1,0:T(8,128)} %constant.83.clone.p0_ref, f32[2,128,128]{2,1,0:T(8,128)} %constant.84.clone.w_ref, f32[2,256,128]{2,1,0:T(8,128)} %constant.85.clone.q0_ref, f32[2,256,128]{2,1,0:T(8,128)} %constant.86.clone.v_ref), custom_call_target="tpu_custom_call" | custom-call | flops 5000000000 | bytes 5000000 | tf_op jit(solution)/shard_map/prep/pallas_call | solution.py:421
  172.5 10.0 %slave_azimuth.1 = (f32[2,2112,128]{2,1,0:T(8,128)}, f32[2112,128]{1,0:T(8,128)S(1)}, f32[2112,128]{1,0:T(8,128)}) custom-call(f32[16,8,2,16,128]{4,3,2,1,0:T(8,128)} %bitcast.30, bf16[16,256,256]{2,1,0:T(8,128)(2,1)} %get-tuple-element.49.ah_hbm, bf16[16,256,256]{2,1,0:T(8,128)(2,1)} %get-tuple-element.50.al_hbm), custom_call_target="tpu_custom_call" | custom-call | flops 5000000000 | bytes 10000000 | tf_op jit(solution)/shard_map/slave_azimuth/pallas_call | solution.py:503
  182.5 2.7 %collective-permute-start.16 = (f32[2112,128]{1,0:T(8,128)}, f32[2112,128]{1,0:T(8,128)S(1)}, u32[]{:S(2)}, u32[]{:S(2)}) collective-permute-start(f32[2112,128]{1,0:T(8,128)} %get-tuple-element.53), channel_id=1, source_target_pairs={{0,16},{16,1},{1,17},{17,2},{2,18},{18,3},{3,19},{19,4},{4,20},{20... | collective-permute-start | bytes 3244040 | tf_op jit(solution)/shard_map/ppermute | solution.py:656
  185.1 1.9 collective-permute-start.17
  189.1 8.4 %collective-permute-done.16.left_ref = f32[2112,128]{1,0:T(8,128)S(1)} collective-permute-done((f32[2112,128]{1,0:T(8,128)}, f32[2112,128]{1,0:T(8,128)S(1)}, u32[]{:S(2)}, u32[]{:S(2)}) %collective-permute-start.16) | collective-permute-done | bytes 1081376 | tf_op jit(solution)/shard_map/ppermute | solution.py:656
  197.5 8.3 %collective-permute-done.17.right_ref = f32[2112,128]{1,0:T(8,128)S(1)} collective-permute-done((f32[2112,128]{1,0:T(8,128)S(1)}, f32[2112,128]{1,0:T(8,128)S(1)}, u32[]{:S(2)}, u32[]{:S(2)}) %collective-permute-start.17) | collective-permute-done | bytes 1081376 | tf_op jit(solution)/shard_map/ppermute | solution.py:656
  206.8 6.8 %resample.1.m_hbm = f32[2,2048,128]{2,1,0:T(8,128)} custom-call(s32[4,2]{1,0:T(4,128)} %copy.28.az_ref, s32[4,2]{1,0:T(4,128)} %copy.29.rg_ref, f32[2,2112,128]{2,1,0:T(8,128)} %get-tuple-element.52.s_hbm, f32[2112,128]{1,0:T(8,128)} %copy-done.7, f32[2112,128]{1,0:T(8,128)} %copy-done.8), custom_call_target="tpu_custom_call" | custom-call | flops 2000000000 | bytes 10000000 | tf_op jit(solution)/shard_map/resample/pallas_call | solution.py:564
  213.7 7.8 %master_looks.1 = (f32[16,512]{1,0:T(8,128)S(1)}, f32[8,512]{1,0:T(8,128)S(1)}) custom-call(f32[16,8,2,16,128]{4,3,2,1,0:T(8,128)} %bitcast.11.x_ref, bf16[16,256,256]{2,1,0:T(8,128)(2,1)} %get-tuple-element.49.ah_hbm, bf16[16,256,256]{2,1,0:T(8,128)(2,1)} %get-tuple-element.50.al_hbm, f32[2,2048,128]{2,1,0:T(8,128)} %resample.1.m_hbm, ...), custom_call_target="tpu_custom_call" | custom-call | flops 5000000000 | bytes 10000000 | tf_op jit(solution)/shard_map/master_looks/pallas_call | solution.py:615
  222.2 1.9 collective-permute-start.19
  224.1 1.9 collective-permute-start.20
  226.0 7.3 %collective-permute-done.20.right_ref = f32[8,512]{1,0:T(8,128)S(1)} collective-permute-done((f32[8,512]{1,0:T(8,128)S(1)}, f32[8,512]{1,0:T(8,128)S(1)}, u32[]{:S(2)}, u32[]{:S(2)}) %collective-permute-start.20) | collective-permute-done | bytes 16416 | tf_op jit(solution)/shard_map/ppermute | solution.py:705
  (87 shorter events, 12.8 us)
Async XLA Ops:
  5.2 41.2 %all-to-all-start = ((f32[16,10,2,16,128]{4,3,2,1,0:T(8,128)}), f32[16,10,2,16,128]{4,3,2,1,0:T(8,128)}, u32[]{:S(2)}, u32[]{:S(2)}) async-start(f32[16,10,2,16,128]{4,3,2,1,0:T(8,128)} %pre.1), calls=%async_computation | async-start | bytes 5242880 | tf_op jit(solution)/shard_map/all_to_all | solution.py:683
  57.6 89.3 %all-to-all-start.2 = ((f32[128,2,16,128]{3,2,1,0:T(8,128)}), f32[128,2,16,128]{3,2,1,0:T(8,128)S(1)}, u32[]{:S(2)}, u32[]{:S(2)}) async-start(f32[128,2,16,128]{3,2,1,0:T(8,128)} %shard_map.173), calls=%async_computation.2 | async-start | bytes 4194304 | tf_op jit(solution)/shard_map/all_to_all | solution.py:665
  70.3 57.7 %copy-start.3 = (f32[2,2048]{1,0:T(2,128)S(1)}, f32[2,2048]{1,0:T(2,128)}, u32[]{:S(2)}) copy-start(f32[2,2048]{1,0:T(2,128)} %param.21) | copy-start | bytes 49156
  75.4 25.9 %collective-permute-start = (f32[10,2,16,128]{3,2,1,0:T(8,128)}, f32[10,2,16,128]{3,2,1,0:T(8,128)S(1)}, u32[]{:S(2)}, u32[]{:S(2)}) collective-permute-start(f32[10,2,16,128]{3,2,1,0:T(8,128)} %get-tuple-element.32), channel_id=1, source_target_pairs={{0,10},{1,11},{2,8},{3,9},{4,14},{5,15},{6,12},{7,13},{8,2},{9,3},... | collective-permute-start | bytes 491528 | tf_op jit(solution)/shard_map/ppermute | solution.py:687
  77.0 29.9 %collective-permute-start.1 = (f32[10,2,16,128]{3,2,1,0:T(8,128)}, f32[10,2,16,128]{3,2,1,0:T(8,128)S(1)}, u32[]{:S(2)}, u32[]{:S(2)}) collective-permute-start(f32[10,2,16,128]{3,2,1,0:T(8,128)} %get-tuple-element.33), channel_id=1, source_target_pairs={{0,9},{1,10},{2,11},{3,8},{4,13},{5,14},{6,15},{7,12},{8,1},{9,2},... | collective-permute-start | bytes 491528 | tf_op jit(solution)/shard_map/ppermute | solution.py:687
  80.9 26.1 %collective-permute-start.10 = (f32[10,2,16,128]{3,2,1,0:T(8,128)}, f32[10,2,16,128]{3,2,1,0:T(8,128)S(1)}, u32[]{:S(2)}, u32[]{:S(2)}) collective-permute-start(f32[10,2,16,128]{3,2,1,0:T(8,128)} %get-tuple-element.42), channel_id=1, source_target_pairs={{0,15},{1,12},{2,13},{3,14},{4,3},{5,0},{6,1},{7,2},{8,7},{9,4},{1... | collective-permute-start | bytes 491528 | tf_op jit(solution)/shard_map/ppermute | solution.py:687
  80.9 26.2 %collective-permute-start.11 = (f32[10,2,16,128]{3,2,1,0:T(8,128)}, f32[10,2,16,128]{3,2,1,0:T(8,128)S(1)}, u32[]{:S(2)}, u32[]{:S(2)}) collective-permute-start(f32[10,2,16,128]{3,2,1,0:T(8,128)} %get-tuple-element.43), channel_id=1, source_target_pairs={{0,4},{1,5},{2,6},{3,7},{4,8},{5,9},{6,10},{7,11},{8,12},{9,13},{1... | collective-permute-start | bytes 491528 | tf_op jit(solution)/shard_map/ppermute | solution.py:687
  82.9 28.0 %collective-permute-start.12 = (f32[10,2,16,128]{3,2,1,0:T(8,128)}, f32[10,2,16,128]{3,2,1,0:T(8,128)S(1)}, u32[]{:S(2)}, u32[]{:S(2)}) collective-permute-start(f32[10,2,16,128]{3,2,1,0:T(8,128)} %get-tuple-element.44), channel_id=1, source_target_pairs={{0,12},{1,13},{2,14},{3,15},{4,0},{5,1},{6,2},{7,3},{8,4},{9,5},{1... | collective-permute-start | bytes 491528 | tf_op jit(solution)/shard_map/ppermute | solution.py:687
  101.3 33.5 %copy-start.9 = (f32[10,2,16,128]{3,2,1,0:T(8,128)}, f32[10,2,16,128]{3,2,1,0:T(8,128)S(1)}, u32[]{:S(2)}) copy-start(f32[10,2,16,128]{3,2,1,0:T(8,128)S(1)} %collective-permute-done.refs_0_) | copy-start | bytes 491524
  101.3 10.8 %collective-permute-start.13 = (f32[10,2,16,128]{3,2,1,0:T(8,128)}, f32[10,2,16,128]{3,2,1,0:T(8,128)S(1)}, u32[]{:S(2)}, u32[]{:S(2)}) collective-permute-start(f32[10,2,16,128]{3,2,1,0:T(8,128)} %get-tuple-element.45), channel_id=1, source_target_pairs={{0,1},{1,2},{2,3},{3,0},{4,5},{5,6},{6,7},{7,4},{8,9},{9,10},{10,1... | collective-permute-start | bytes 491528 | tf_op jit(solution)/shard_map/ppermute | solution.py:687
  106.9 27.9 %copy-start.10 = (f32[10,2,16,128]{3,2,1,0:T(8,128)}, f32[10,2,16,128]{3,2,1,0:T(8,128)S(1)}, u32[]{:S(2)}) copy-start(f32[10,2,16,128]{3,2,1,0:T(8,128)S(1)} %collective-permute-done.1.refs_1_) | copy-start | bytes 491524
  106.9 13.3 %collective-permute-start.14 = (f32[10,2,16,128]{3,2,1,0:T(8,128)}, f32[10,2,16,128]{3,2,1,0:T(8,128)S(1)}, u32[]{:S(2)}, u32[]{:S(2)}) collective-permute-start(f32[10,2,16,128]{3,2,1,0:T(8,128)} %get-tuple-element.46), channel_id=1, source_target_pairs={{0,3},{1,0},{2,1},{3,2},{4,7},{5,4},{6,5},{7,6},{8,11},{9,8},{10,9... | collective-permute-start | bytes 491528 | tf_op jit(solution)/shard_map/ppermute | solution.py:687
  106.9 27.9 %copy-start.11 = (f32[10,2,16,128]{3,2,1,0:T(8,128)}, f32[10,2,16,128]{3,2,1,0:T(8,128)S(1)}, u32[]{:S(2)}) copy-start(f32[10,2,16,128]{3,2,1,0:T(8,128)S(1)} %collective-permute-done.10.refs_10_) | copy-start | bytes 491524
  106.9 13.2 %collective-permute-start.2 = (f32[10,2,16,128]{3,2,1,0:T(8,128)}, f32[10,2,16,128]{3,2,1,0:T(8,128)S(1)}, u32[]{:S(2)}, u32[]{:S(2)}) collective-permute-start(f32[10,2,16,128]{3,2,1,0:T(8,128)} %get-tuple-element.34), channel_id=1, source_target_pairs={{0,6},{1,7},{2,4},{3,5},{4,10},{5,11},{6,8},{7,9},{8,14},{9,15},{1... | collective-permute-start | bytes 491528 | tf_op jit(solution)/shard_map/ppermute | solution.py:687
  107.0 27.8 %copy-start.12 = (f32[10,2,16,128]{3,2,1,0:T(8,128)}, f32[10,2,16,128]{3,2,1,0:T(8,128)S(1)}, u32[]{:S(2)}) copy-start(f32[10,2,16,128]{3,2,1,0:T(8,128)S(1)} %collective-permute-done.11.refs_11_) | copy-start | bytes 491524
  107.0 13.2 %collective-permute-start.3 = (f32[10,2,16,128]{3,2,1,0:T(8,128)}, f32[10,2,16,128]{3,2,1,0:T(8,128)S(1)}, u32[]{:S(2)}, u32[]{:S(2)}) collective-permute-start(f32[10,2,16,128]{3,2,1,0:T(8,128)} %get-tuple-element.35), channel_id=1, source_target_pairs={{0,14},{1,15},{2,12},{3,13},{4,2},{5,3},{6,0},{7,1},{8,6},{9,7},{1... | collective-permute-start | bytes 491528 | tf_op jit(solution)/shard_map/ppermute | solution.py:687
  110.9 24.0 %copy-start.13 = (f32[10,2,16,128]{3,2,1,0:T(8,128)}, f32[10,2,16,128]{3,2,1,0:T(8,128)S(1)}, u32[]{:S(2)}) copy-start(f32[10,2,16,128]{3,2,1,0:T(8,128)S(1)} %collective-permute-done.12.refs_12_) | copy-start | bytes 491524
  110.9 16.4 %collective-permute-start.4 = (f32[10,2,16,128]{3,2,1,0:T(8,128)}, f32[10,2,16,128]{3,2,1,0:T(8,128)S(1)}, u32[]{:S(2)}, u32[]{:S(2)}) collective-permute-start(f32[10,2,16,128]{3,2,1,0:T(8,128)} %get-tuple-element.36), channel_id=1, source_target_pairs={{0,11},{1,8},{2,9},{3,10},{4,15},{5,12},{6,13},{7,14},{8,3},{9,0},... | collective-permute-start | bytes 491528 | tf_op jit(solution)/shard_map/ppermute | solution.py:687
  112.1 22.7 %copy-start.14 = (f32[10,2,16,128]{3,2,1,0:T(8,128)}, f32[10,2,16,128]{3,2,1,0:T(8,128)S(1)}, u32[]{:S(2)}) copy-start(f32[10,2,16,128]{3,2,1,0:T(8,128)S(1)} %collective-permute-done.13.refs_13_) | copy-start | bytes 491524
  112.1 16.6 %collective-permute-start.5 = (f32[10,2,16,128]{3,2,1,0:T(8,128)}, f32[10,2,16,128]{3,2,1,0:T(8,128)}, u32[]{:S(2)}, u32[]{:S(2)}) collective-permute-start(f32[10,2,16,128]{3,2,1,0:T(8,128)} %get-tuple-element.37), channel_id=1, source_target_pairs={{0,8},{1,9},{2,10},{3,11},{4,12},{5,13},{6,14},{7,15},{8,0},{9,1},... | collective-permute-start | bytes 491528 | tf_op jit(solution)/shard_map/ppermute | solution.py:687
  120.2 14.7 %copy-start.15 = (f32[10,2,16,128]{3,2,1,0:T(8,128)}, f32[10,2,16,128]{3,2,1,0:T(8,128)S(1)}, u32[]{:S(2)}) copy-start(f32[10,2,16,128]{3,2,1,0:T(8,128)S(1)} %collective-permute-done.14.refs_14_) | copy-start | bytes 491524
  120.2 8.6 %collective-permute-start.6 = (f32[10,2,16,128]{3,2,1,0:T(8,128)}, f32[10,2,16,128]{3,2,1,0:T(8,128)}, u32[]{:S(2)}, u32[]{:S(2)}) collective-permute-start(f32[10,2,16,128]{3,2,1,0:T(8,128)} %get-tuple-element.38), channel_id=1, source_target_pairs={{0,5},{1,6},{2,7},{3,4},{4,9},{5,10},{6,11},{7,8},{8,13},{9,14},{1... | collective-permute-start | bytes 491528 | tf_op jit(solution)/shard_map/ppermute | solution.py:687
  120.2 10.1 %collective-permute-start.7 = (f32[10,2,16,128]{3,2,1,0:T(8,128)}, f32[10,2,16,128]{3,2,1,0:T(8,128)}, u32[]{:S(2)}, u32[]{:S(2)}) collective-permute-start(f32[10,2,16,128]{3,2,1,0:T(8,128)} %get-tuple-element.39), channel_id=1, source_target_pairs={{0,13},{1,14},{2,15},{3,12},{4,1},{5,2},{6,3},{7,0},{8,5},{9,6},{1... | collective-permute-start | bytes 491528 | tf_op jit(solution)/shard_map/ppermute | solution.py:687
  120.3 10.0 %collective-permute-start.8 = (f32[10,2,16,128]{3,2,1,0:T(8,128)}, f32[10,2,16,128]{3,2,1,0:T(8,128)}, u32[]{:S(2)}, u32[]{:S(2)}) collective-permute-start(f32[10,2,16,128]{3,2,1,0:T(8,128)} %get-tuple-element.40), channel_id=1, source_target_pairs={{0,2},{1,3},{2,0},{3,1},{4,6},{5,7},{6,4},{7,5},{8,10},{9,11},{10,... | collective-permute-start | bytes 491528 | tf_op jit(solution)/shard_map/ppermute | solution.py:687
  127.9 6.9 %collective-permute-start.9 = (f32[10,2,16,128]{3,2,1,0:T(8,128)}, f32[10,2,16,128]{3,2,1,0:T(8,128)}, u32[]{:S(2)}, u32[]{:S(2)}) collective-permute-start(f32[10,2,16,128]{3,2,1,0:T(8,128)} %get-tuple-element.41), channel_id=1, source_target_pairs={{0,7},{1,4},{2,5},{3,6},{4,11},{5,8},{6,9},{7,10},{8,15},{9,12},{1... | collective-permute-start | bytes 491528 | tf_op jit(solution)/shard_map/ppermute | solution.py:687
  148.3 65.3 %all-to-all-start.1 = ((f32[128,2,16,128]{3,2,1,0:T(8,128)}), f32[128,2,16,128]{3,2,1,0:T(8,128)}, u32[]{:S(2)}, u32[]{:S(2)}) async-start(f32[128,2,16,128]{3,2,1,0:T(8,128)} %shard_map.172), calls=%async_computation.1 | async-start | bytes 4194304 | tf_op jit(solution)/shard_map/all_to_all | solution.py:665
  182.5 15.0 %collective-permute-start.16 = (f32[2112,128]{1,0:T(8,128)}, f32[2112,128]{1,0:T(8,128)S(1)}, u32[]{:S(2)}, u32[]{:S(2)}) collective-permute-start(f32[2112,128]{1,0:T(8,128)} %get-tuple-element.53), channel_id=1, source_target_pairs={{0,16},{16,1},{1,17},{17,2},{2,18},{18,3},{3,19},{19,4},{4,20},{20... | collective-permute-start | bytes 3244040 | tf_op jit(solution)/shard_map/ppermute | solution.py:656
  185.1 20.7 %collective-permute-start.17 = (f32[2112,128]{1,0:T(8,128)S(1)}, f32[2112,128]{1,0:T(8,128)S(1)}, u32[]{:S(2)}, u32[]{:S(2)}) collective-permute-start(f32[2112,128]{1,0:T(8,128)S(1)} %get-tuple-element.54), channel_id=1, source_target_pairs={{16,0},{1,16},{17,1},{2,17},{18,2},{3,18},{19,3},{4,19},{20,4},{5,... | collective-permute-start | bytes 3244040 | tf_op jit(solution)/shard_map/ppermute | solution.py:656
  187.1 0.7 collective-permute-start.15
  221.5 11.9 %collective-permute-start.18 = (f32[16,512]{1,0:T(8,128)S(1)}, f32[16,512]{1,0:T(8,128)S(1)}, u32[]{:S(2)}, u32[]{:S(2)}) collective-permute-start(f32[16,512]{1,0:T(8,128)S(1)} %get-tuple-element.56), channel_id=1, source_target_pairs={{0,0},{16,1},{1,2},{17,3},{2,4},{18,5},{3,6},{19,7},{4,8},{20,9},{... | collective-permute-start | bytes 98312 | tf_op jit(solution)/shard_map/ppermute | solution.py:703
  222.2 3.9 %collective-permute-start.19 = (f32[8,512]{1,0:T(8,128)S(1)}, f32[8,512]{1,0:T(8,128)S(1)}, u32[]{:S(2)}, u32[]{:S(2)}) collective-permute-start(f32[8,512]{1,0:T(8,128)S(1)} %get-tuple-element.57), channel_id=1, source_target_pairs={{0,1},{16,2},{1,3},{17,4},{2,5},{18,6},{3,7},{19,8},{4,9},{20,10},... | collective-permute-start | bytes 49160 | tf_op jit(solution)/shard_map/ppermute | solution.py:704
  224.1 9.3 %collective-permute-start.20 = (f32[8,512]{1,0:T(8,128)S(1)}, f32[8,512]{1,0:T(8,128)S(1)}, u32[]{:S(2)}, u32[]{:S(2)}) collective-permute-start(f32[8,512]{1,0:T(8,128)S(1)} %get-tuple-element.57), channel_id=1, source_target_pairs={{16,0},{1,1},{17,2},{2,3},{18,4},{3,5},{19,6},{4,7},{20,8},{5,9},{... | collective-permute-start | bytes 49160 | tf_op jit(solution)/shard_map/ppermute | solution.py:705
  (11 other events, 74.4 us)

commit v5 on v4

--- a/solution.py
+++ b/solution.py
@@ -163,20 +163,13 @@
     t["fh"], t["fl"] = _np_split(np.block([[c, -s], [s, c]]))
     t["gh"], t["gl"] = _np_split(np.block([[c, s], [-s, c]]))
     k2 = np.arange(128)
-    l2 = np.arange(128)
-    ang = -two * ((l2[:, None] * k2[None, :]) % 128) / 128
-    pr, pi = np.cos(ang), np.sin(ang)
-    ang = np.broadcast_to(-two * l2[:, None] / LINES, (128, 128))
-    wr, wi = np.cos(ang), np.sin(ang)
-    t["p"] = np.stack([pr, pi]).astype(np.float32)
-    t["w"] = np.stack([wr, wi]).astype(np.float32)
-    kk = np.arange(256)
-    part, line = (kk // 16) % 2, (kk // 32) * 16 + kk % 16
-    sel = (part == 0)[:, None]
-    t["q"] = np.stack(
-        [np.where(sel, pr[line], -pi[line]), np.where(sel, -pi[line], -pr[line])]
-    ).astype(np.float32)
-    t["v"] = np.stack([wr[line], wi[line]]).astype(np.float32)
+    back = (-np.arange(128)) % 128
+    ang = two * ((k2[:, None] * back[None, :]) % 128) / 128
+    t["dft"] = np.stack([np.cos(ang), np.sin(ang)]).astype(np.float32)
+    ang = two * (np.arange(16)[:, None] * back[None, :]) / LINES
+    t["turn"] = np.stack([np.cos(ang), np.sin(ang)]).astype(np.float32)
+    ang = np.broadcast_to(-two * np.arange(16)[:, None] / 16, (16, 128))
+    t["wrap"] = np.stack([np.cos(ang), np.sin(ang)], 1).astype(np.float32)
     lane = np.arange(128)
     pick = np.zeros((24, 128), np.float32)
     for o in range(16):
@@ -199,40 +192,68 @@
     return pltpu.CompilerParams(vmem_limit_bytes=mib << 20)
 
 
-def _line_tile(x_ref, q, half, c):
-    v = x_ref[pl.ds(500 * q + 2 * half + c, NS, stride=4), :]
-    return jnp.concatenate([v, jnp.zeros((128 - NS, 128), F32)], axis=0).T
-
-
-def _pre_kernel(x_ref, o_ref):
-    for q in range(2):
-        for half in range(2):
-            for c in range(2):
-                v = _line_tile(x_ref, q, half, c)
-                for k in range(8):
-                    o_ref[8 * half + k, q, c] = v[16 * k : 16 * k + 16]
-
-
-def _pre_shift_kernel(me_ref, x_ref, *refs):
-    outs, t_ref = refs[:-1], refs[-1]
-    _pre_kernel(x_ref, t_ref)
-    me = me_ref[0]
-    for shift, o_ref in zip(SHIFTS, outs):
-        o_ref[...] = t_ref[shifted(me, shift)]
-
-
 def _raw_rows(raw):
     raw = raw.transpose(2, 0, 1).reshape(1250, 2, 2, 128)
     return raw.transpose(0, 2, 1, 3).reshape(5000, 128)
 
 
+def _read_lines(x_hbm, x_ref, t_ref, sem, done):
+    def load(q):
+        rows = pl.ds(1000 * q, 1000)
+        return pltpu.make_async_copy(x_hbm.at[rows], x_ref.at[rows], sem.at[q])
+
+    for q in range(5):
+        load(q).start()
+    for q in range(NQ):
+        if q % 2 == 0:
+            load(q // 2).wait()
+        for half in range(2):
+            for c in range(2):
+                v = x_ref[pl.ds(500 * q + 2 * half + c, NS, stride=4), :]
+                v = jnp.concatenate([v, jnp.zeros((128 - NS, 128), F32)], axis=0).T
+                for k in range(8):
+                    t_ref[8 * half + k, q, c] = v[16 * k : 16 * k + 16]
+        done(q)
+
+
+def _pre_kernel(x_hbm, o_hbm, x_ref, t_ref, sem):
+    def store(q):
+        at = pl.ds(2 * (q // 2), 2)
+        return pltpu.make_async_copy(t_ref.at[:, at], o_hbm.at[:, at], sem.at[5 + q // 2])
+
+    _read_lines(x_hbm, x_ref, t_ref, sem, lambda q: store(q).start() if q % 2 else None)
+    for q in range(0, NQ, 2):
+        store(q).wait()
+
+
+def _pre_shift_kernel(me_ref, x_hbm, *refs):
+    outs, (x_ref, t_ref, sem) = refs[:NP], refs[NP:]
+    _read_lines(x_hbm, x_ref, t_ref, sem, lambda q: None)
+    me = me_ref[0]
+    stores = [
+        pltpu.make_async_copy(t_ref.at[shifted(me, shift)], o_hbm, sem.at[5 + k])
+        for k, (shift, o_hbm) in enumerate(zip(SHIFTS, outs))
+    ]
+    for store in stores:
+        store.start()
+    for store in stores:
+        store.wait()
+
+
+PRE_SCRATCH = [
+    pltpu.VMEM((5000, 128), F32),
+    pltpu.VMEM((NP, NQ, 2, 16, 128), F32),
+    pltpu.SemaphoreType.DMA((5 + NP,)),
+]
+
+
 def pre(raw):
     return pl.pallas_call(
         _pre_kernel,
-        grid=(5,),
-        in_specs=[pl.BlockSpec((1000, 128), lambda i: (i, 0))],
-        out_specs=pl.BlockSpec((NP, 2, 2, 16, 128), lambda i: (0, i, 0, 0, 0)),
+        in_specs=[HBM],
+        out_specs=HBM,
         out_shape=jax.ShapeDtypeStruct((NP, NQ, 2, 16, 128), F32),
+        scratch_shapes=PRE_SCRATCH,
         cost_estimate=pl.CostEstimate(flops=10**8, bytes_accessed=10**7, transcendentals=0),
         name="pre",
     )(_raw_rows(raw))
@@ -241,17 +262,17 @@
 def pre_shifts(me, raw):
     return pl.pallas_call(
         _pre_shift_kernel,
-        grid=(5,),
-        in_specs=[SMEM, pl.BlockSpec((1000, 128), lambda i: (i, 0))],
-        out_specs=[pl.BlockSpec((2, 2, 16, 128), lambda i: (i, 0, 0, 0))] * NP,
+        in_specs=[SMEM, HBM],
+        out_specs=[HBM] * NP,
         out_shape=[jax.ShapeDtypeStruct((NQ, 2, 16, 128), F32)] * NP,
-        scratch_shapes=[pltpu.VMEM((NP, 2, 2, 16, 128), F32)],
+        scratch_shapes=PRE_SCRATCH,
         cost_estimate=pl.CostEstimate(flops=10**8, bytes_accessed=10**7, transcendentals=0),
         name="pre_shifts",
     )(me, _raw_rows(raw))
 
 
-def _range_body(ready, twb_ref, hf_ref, fh_ref, fl_ref, gh_ref, gl_ref, twc_ref, o_hbm, d_ref, x_ref, o_ref, out_sem):
+def _range_body(ready, tables, o_hbm, d_ref, x_ref, o_ref, out_sem):
+    twb_ref, hf_ref, fh_ref, fl_ref, gh_ref, gl_ref, twc_ref = tables
     lane = lax.broadcasted_iota(jnp.int32, (16, 128), 1)
 
     def outer(q, carry):
@@ -268,6 +289,7 @@
         return carry
 
     lax.fori_loop(0, NQ, outer, 0)
+    ready(None)
 
     def middle(kp, carry):
         v = [(d_ref[kp * NQ + q, 0], d_ref[kp * NQ + q, 1]) for q in range(NQ)]
@@ -335,20 +357,38 @@
         store(part).wait()
 
 
+def _tables_in(table_hbm, tables, sem):
+    copies = [
+        pltpu.make_async_copy(src, dst, sem.at[k]) for k, (src, dst) in enumerate(zip(table_hbm, tables))
+    ]
+    for copy in copies[::-1]:
+        copy.start()
+    return copies
+
+
 def _range_kernel(x_hbm, *refs):
-    in_sem, x_ref = refs[-1], refs[-4]
+    table_hbm, o_hbm, tables, (d_ref, x_ref, o_ref, out_sem, in_sem, sem) = refs[:7], refs[7], refs[8:15], refs[15:]
 
     def load(q):
         return pltpu.make_async_copy(x_hbm.at[:, q], x_ref.at[:, q], in_sem.at[q])
 
+    def ready(q):
+        if q is None:
+            for copy in copies[:6]:
+                copy.wait()
+        else:
+            load(q).wait()
+
+    copies = _tables_in(table_hbm, tables, sem)
     for q in range(NQ):
         load(q).start()
-    _range_body(lambda q: load(q).wait(), *refs[:-1])
+    copies[6].wait()
+    _range_body(ready, tables, o_hbm, d_ref, x_ref, o_ref, out_sem)
 
 
 def _range_shift_kernel(me_ref, *refs):
     parts, refs = refs[:NP], refs[NP:]
-    in_sem, x_ref = refs[-1], refs[-4]
+    table_hbm, o_hbm, tables, (d_ref, x_ref, o_ref, out_sem, in_sem, sem) = refs[:7], refs[7], refs[8:15], refs[15:]
     me = me_ref[0]
     loads = [
         pltpu.make_async_copy(
@@ -356,29 +396,40 @@
         )
         for k, (shift, part) in enumerate(zip(SHIFTS, parts))
     ]
+
+    def ready(q):
+        if q is None:
+            for copy in copies[:6]:
+                copy.wait()
+
+    copies = _tables_in(table_hbm, tables, sem)
     for load in loads:
         load.start()
     for load in loads:
         load.wait()
-    _range_body(lambda q: None, *refs[:-1])
+    copies[6].wait()
+    _range_body(ready, tables, o_hbm, d_ref, x_ref, o_ref, out_sem)
 
 
 def range_compress(kernel, specs, operands, hf):
     t = TABLES
+    tables = (t["twb"], hf, t["fh"], t["fl"], t["gh"], t["gl"], t["twc"])
     return pl.pallas_call(
         kernel,
-        in_specs=specs + [VMEM] * 7,
+        in_specs=specs + [HBM] * 7,
         out_specs=HBM,
         out_shape=jax.ShapeDtypeStruct((128, 2, 16, 128), F32),
-        scratch_shapes=[
+        scratch_shapes=[pltpu.VMEM(x.shape, x.dtype) for x in tables]
+        + [
             pltpu.VMEM((NP * NQ, 2, 16, 128), F32),
             pltpu.VMEM((NP, NQ, 2, 16, 128), F32),
             pltpu.VMEM((128, 2, 16, 128), F32),
             pltpu.SemaphoreType.DMA((4,)),
             pltpu.SemaphoreType.DMA((NP,)),
+            pltpu.SemaphoreType.DMA((7,)),
         ],
         cost_estimate=pl.CostEstimate(flops=10**10, bytes_accessed=6 * 10**6, transcendentals=0),
-    )(*operands, t["twb"], hf, t["fh"], t["fl"], t["gh"], t["gl"], t["twc"])
+    )(*operands, *tables)
 
 
 def _dot_t(a, b):
@@ -387,32 +438,36 @@
     )
 
 
-def _prep_kernel(h_ref, p0_ref, w_ref, q0_ref, v_ref, ah_ref, al_ref, p_ref, q_ref):
-    p_ref[...] = p0_ref[...]
-    q_ref[...] = q0_ref[...]
+def _prep_kernel(h_ref, dft_ref, turn_ref, wrap_ref, ah_ref, al_ref, g_ref):
+    def mul(a, b):
+        return jnp.dot(a, b, precision=lax.Precision.HIGHEST, preferred_element_type=F32)
+
+    hr, hi = h_ref[0], h_ref[1]
+    dr, di = dft_ref[0], dft_ref[1]
+    g = (mul(hr, dr) - mul(hi, di), mul(hr, di) + mul(hi, dr))
+    r, i = cmul(g, (turn_ref[0], turn_ref[1]))
+    g_ref[:, 0, :] = r
+    g_ref[:, 1, :] = i
+    row = lax.broadcasted_iota(jnp.int32, (128, 128), 0)
+    lane = lax.broadcasted_iota(jnp.int32, (128, 128), 1)
+    over = lane > row
 
     def body(k, carry):
-        pr, pi = p_ref[0], p_ref[1]
-        q1, q2 = q_ref[0], q_ref[1]
-        hr, hi = h_ref[k, 0:1, :], h_ref[k, 1:2, :]
-        vr, vi = cmul((pr, -pi), (hr, hi))
-        top = _dot_t(vr, q1) + _dot_t(vi, q2)
-        bottom = _dot_t(vi, q1) - _dot_t(vr, q2)
-        high, low = split(top)
-        ah_ref[k, 0:128, :] = high
-        al_ref[k, 0:128, :] = low
-        high, low = split(bottom)
-        ah_ref[k, 128:256, :] = high
-        al_ref[k, 128:256, :] = low
-        pr, pi = cmul((pr, pi), (w_ref[0], w_ref[1]))
-        p_ref[0] = pr
-        p_ref[1] = pi
-        wr, wi = v_ref[0], v_ref[1]
-        q_ref[0] = q1 * wr + q2 * wi
-        q_ref[1] = q2 * wr - q1 * wi
+        m = []
+        for c in range(2):
+            line = jnp.broadcast_to(g_ref[k, c : c + 1, :], (128, 128))
+            m.append(pltpu.roll(line, 0, 1, stride=1, stride_axis=0))
+        turned = cmul(m, (wrap_ref[k, 0:1, :], wrap_ref[k, 1:2, :]))
+        re = jnp.where(over, turned[0], m[0])
+        im = jnp.where(over, turned[1], m[1])
+        for rows, cols, block in ((0, 0, re), (0, 1, -im), (1, 0, im), (1, 1, re)):
+            high, low = split(block)
+            at = (k, slice(128 * rows, 128 * rows + 128), slice(128 * cols, 128 * cols + 128))
+            ah_ref[at] = high
+            al_ref[at] = low
         return carry
 
-    lax.fori_loop(0, 16, body, 0)
+    lax.fori_loop(0, 16, body, 0, unroll=2)
 
 
 def prep(h):
@@ -421,10 +476,10 @@
     return pl.pallas_call(
         _prep_kernel,
         out_shape=(shape, shape),
-        scratch_shapes=[pltpu.VMEM((2, 128, 128), F32), pltpu.VMEM((2, 256, 128), F32)],
-        cost_estimate=pl.CostEstimate(flops=5 * 10**9, bytes_accessed=5 * 10**6, transcendentals=0),
+        scratch_shapes=[pltpu.VMEM((16, 2, 128), F32)],
+        cost_estimate=pl.CostEstimate(flops=2 * 10**9, bytes_accessed=5 * 10**6, transcendentals=0),
         name="prep",
-    )(h, t["p"], t["w"], t["q"], t["v"])
+    )(h, t["dft"], t["turn"], t["wrap"])
 
 
 def _azimuth_front(x_ref, ah_hbm, al_hbm, e_ref, ah_ref, al_ref, sem):
@@ -442,7 +497,7 @@
             v = dft16(v, -1)
             for k in range(16):
                 for c in range(2):
-                    at = pl.multiple_of(s * 32 + c * 16 + g * 8, 8)
+                    at = pl.multiple_of(c * 128 + s * 16 + g * 8, 8)
                     e_ref[k, pl.ds(at, 8), :] = v[k][c]
         return carry
 
@@ -659,7 +714,7 @@
 def local(master_raw, slave_raw, range_ref, az_ref, az_shift, rg_shift, valid_lines):
     hf = range_ref.reshape(2, NS, NQ, NP).transpose(3, 2, 0, 1).reshape(NP * NQ, 2, NS)
     hf = jnp.pad(hf * (1.0 / RANGE), ((0, 0), (0, 0), (0, 3)))
-    h = az_ref.reshape(2, 128, 16).transpose(2, 0, 1) * (1.0 / LINES)
+    h = az_ref.reshape(2, 128, 16).transpose(0, 2, 1) * (1.0 / LINES)
 
     def columns_of(ranged):
         return lax.all_to_all(ranged, ALL, 0, 0, tiled=True)
@@ -689,7 +744,6 @@
         else piece
         for shift, piece in zip(SHIFTS, pieces)
     ]
-    slave, hf, scale, col_counts = lax.optimization_barrier((slave, hf, scale, col_counts))
     slave = range_compress(_range_kernel, [HBM], [slave], hf)
     slave = columns_of(slave)
     ah, al = prep(h)

time: 238 us -> 224 us (0.941)
  starting transfers between devices: 58.4 us -> 75.9 us
  waiting for transfers between devices: 92.9 us -> 76.2 us
  Pallas kernels: 72.1 us -> 58.2 us
    ppermute x15, waiting for transfers between devices: 39.1 us -> 23.1 us  [local(): lax.ppermute(piece, 'rg', [(r, shifted(r, shift)) for r in range(NP)])]
    ppermute x15, starting transfers between devices: 18.7 us -> 32.8 us  [local(): lax.ppermute(piece, 'rg', [(r, shifted(r, shift)) for r in range(NP)])]
    pallas_call x1, Pallas kernels: 13.3 us -> 4.74 us  [prep(): pl.pallas_call(_prep_kernel, out_shape=(shape, shape), scratch_shapes=[pl...]
    pallas_call x4, Pallas kernels: 33.6 us -> 28.3 us  [the longest x2 21.5 us: range_compress(): pl.pallas_call(kernel, in_specs=specs + [HBM] * 7, out_specs=HBM, out_sha...]
    all_to_all x1, waiting for transfers between devices: 29.6 us -> 32.4 us  [local(): slave = lax.all_to_all(slave, 'rg', 0, 0, tiled=True)]
    ppermute x2, waiting for transfers between devices: 16.7 us -> 14.1 us  [halo(): return (lax.ppermute(to_right, ALL, up), lax.ppermute(to_left, ALL, down))]
  transfers between devices with their start and end apart: 24 -> 24, of which waited for: 10 -> 8; matrix products, arithmetic and copies ran while one was open for 3% -> 3% of each run, Pallas kernels for 20% -> 17%
where the time goes in v5:
time: 224 us; the launch traced here: 220 us
  waiting for transfers between devices  76.2 us (34%)
  starting transfers between devices  75.9 us (34%)
  Pallas kernels  58.2 us (26%)
  local copies, waits for them, and re-layouts  7.83 us (3%)
    ppermute x15, starting transfers between devices, local(): lax.ppermute(piece, 'rg', [(r, shifted(r, shift)) for r in range(NP)])  32.8 us
    all_to_all x1, waiting for transfers between devices, local(): slave = lax.all_to_all(slave, 'rg', 0, 0, tiled=True)  32.4 us
    all_to_all x2, starting transfers between devices, columns_of(): return lax.all_to_all(ranged, ALL, 0, 0, tiled=True)  24.9 us
    ppermute x15, waiting for transfers between devices, local(): lax.ppermute(piece, 'rg', [(r, shifted(r, shift)) for r in range(NP)])  23.1 us
    pallas_call x2, Pallas kernels, range_compress(): pl.pallas_call(kernel, in_specs=specs + [HBM] * 7, out_specs=HBM, out_sha...  21.5 us
    ppermute x2, waiting for transfers between devices, halo(): return (lax.ppermute(to_right, ALL, up), lax.ppermute(to_left, ALL, down))  14.1 us
    pallas_call x1, Pallas kernels, slave_azimuth(): pl.pallas_call(_slave_kernel, out_shape=(jax.ShapeDtypeStruct((2, LINES +...  9.88 us
    pallas_call x1, Pallas kernels, master_looks(): pl.pallas_call(_master_kernel, out_shape=(jax.ShapeDtypeStruct((16, 512),...  7.84 us
  transfers between devices with their start and end apart: 24, of which 8 were waited for; matrix products, arithmetic and copies ran while one was open for 3% of the time, Pallas kernels for 17%

profile of v5, /device:TPU:103, one launch (start us, length us, event | category | flops | bytes accessed | tf_op | source)
XLA Modules:
  0.0 220.2 jit_solution(12588457752874020700)
XLA Ops:
  0.0 3.1 %pre.1 = f32[16,10,2,16,128]{4,3,2,1,0:T(8,128)} custom-call(f32[5000,128]{1,0:T(8,128)} %bitcast.28), custom_call_target="tpu_custom_call" | custom-call | flops 100000000 | bytes 10000000 | tf_op jit(solution)/shard_map/pre/pallas_call | solution.py:251
  3.1 6.5 %all-to-all-start.1 = ((f32[16,10,2,16,128]{4,3,2,1,0:T(8,128)}), f32[16,10,2,16,128]{4,3,2,1,0:T(8,128)}, u32[]{:S(2)}, u32[]{:S(2)}) async-start(f32[16,10,2,16,128]{4,3,2,1,0:T(8,128)} %pre.1), calls=%async_computation.1 | async-start | bytes 5242880 | tf_op jit(solution)/shard_map/all_to_all | solution.py:738
  11.9 32.4 %all-to-all-done.1.x_hbm = f32[16,10,2,16,128]{4,3,2,1,0:T(8,128)} async-done(((f32[16,10,2,16,128]{4,3,2,1,0:T(8,128)}), f32[16,10,2,16,128]{4,3,2,1,0:T(8,128)}, u32[]{:S(2)}, u32[]{:S(2)}) %all-to-all-start.1) | async-done | bytes 2621472 | tf_op jit(solution)/shard_map/all_to_all | solution.py:738
  44.4 10.3 %shard_map.164 = f32[128,2,16,128]{3,2,1,0:T(8,128)} custom-call(f32[16,10,2,16,128]{4,3,2,1,0:T(8,128)} %all-to-all-done.1.x_hbm, f32[10,2,128]{2,1,0:T(2,128)} %constant.75.clone.refs_16_.refs_0_, f32[160,2,128]{2,1,0:T(2,128)} %pad.8.refs_17_.refs_1_, bf16[256,256]{1,0:T(8,128)(2,1)} %constant.76.clone.refs_18_.refs_2_, ...), custom_call_target="tpu_custom_call" | custom-call | flops 10000000000 | bytes 6000000 | tf_op jit(solution)/shard_map/pallas_call | solution.py:417
  54.6 12.6 %all-to-all-start.2 = ((f32[128,2,16,128]{3,2,1,0:T(8,128)}), f32[128,2,16,128]{3,2,1,0:T(8,128)S(1)}, u32[]{:S(2)}, u32[]{:S(2)}) async-start(f32[128,2,16,128]{3,2,1,0:T(8,128)} %shard_map.164), calls=%async_computation.2 | async-start | bytes 4194304 | tf_op jit(solution)/shard_map/all_to_all | solution.py:720
  67.3 3.8 %pre_shifts.1 = (f32[10,2,16,128]{3,2,1,0:T(8,128)}, f32[10,2,16,128]{3,2,1,0:T(8,128)}, f32[10,2,16,128]{3,2,1,0:T(8,128)}, f32[10,2,16,128]{3,2,1,0:T(8,128)},...) custom-call(s32[1]{0:T(128)} %bitcast.me_ref, ...), custom_call_target="tpu_custom_call" | custom-call | flops 100000000 | bytes 10000000 | tf_op jit(solution)/shard_map/pre_shifts/pallas_call | solution.py:263
  71.0 1.6 collective-permute-start
  72.6 3.8 %collective-permute-start.1 = (f32[10,2,16,128]{3,2,1,0:T(8,128)}, f32[10,2,16,128]{3,2,1,0:T(8,128)S(1)}, u32[]{:S(2)}, u32[]{:S(2)}) collective-permute-start(f32[10,2,16,128]{3,2,1,0:T(8,128)} %get-tuple-element.29), channel_id=1, source_target_pairs={{0,9},{1,10},{2,11},{3,8},{4,13},{5,14},{6,15},{7,12},{8,1},{9,2},... | collective-permute-start | bytes 491528 | tf_op jit(solution)/shard_map/ppermute | solution.py:742
  76.5 3.9 %collective-permute-start.3 = (f32[10,2,16,128]{3,2,1,0:T(8,128)}, f32[10,2,16,128]{3,2,1,0:T(8,128)S(1)}, u32[]{:S(2)}, u32[]{:S(2)}) collective-permute-start(f32[10,2,16,128]{3,2,1,0:T(8,128)} %get-tuple-element.31), channel_id=1, source_target_pairs={{0,14},{1,15},{2,12},{3,13},{4,2},{5,3},{6,0},{7,1},{8,6},{9,7},{1... | collective-permute-start | bytes 491528 | tf_op jit(solution)/shard_map/ppermute | solution.py:742
  80.4 16.1 %collective-permute-done.refs_0_ = f32[10,2,16,128]{3,2,1,0:T(8,128)S(1)} collective-permute-done((f32[10,2,16,128]{3,2,1,0:T(8,128)}, f32[10,2,16,128]{3,2,1,0:T(8,128)S(1)}, u32[]{:S(2)}, u32[]{:S(2)}) %collective-permute-start) | collective-permute-done | bytes 163872 | tf_op jit(solution)/shard_map/ppermute | solution.py:742
  96.5 2.5 %collective-permute-start.5 = (f32[10,2,16,128]{3,2,1,0:T(8,128)}, f32[10,2,16,128]{3,2,1,0:T(8,128)S(1)}, u32[]{:S(2)}, u32[]{:S(2)}) collective-permute-start(f32[10,2,16,128]{3,2,1,0:T(8,128)} %get-tuple-element.33), channel_id=1, source_target_pairs={{0,8},{1,9},{2,10},{3,11},{4,12},{5,13},{6,14},{7,15},{8,0},{9,1},... | collective-permute-start | bytes 491528 | tf_op jit(solution)/shard_map/ppermute | solution.py:742
  99.0 1.7 collective-permute-done.1.refs_1_
  100.7 1.5 collective-permute-start.6
  102.2 5.8 %collective-permute-start.7 = (f32[10,2,16,128]{3,2,1,0:T(8,128)}, f32[10,2,16,128]{3,2,1,0:T(8,128)S(1)}, u32[]{:S(2)}, u32[]{:S(2)}) collective-permute-start(f32[10,2,16,128]{3,2,1,0:T(8,128)} %get-tuple-element.35), channel_id=1, source_target_pairs={{0,13},{1,14},{2,15},{3,12},{4,1},{5,2},{6,3},{7,0},{8,5},{9,6},{1... | collective-permute-start | bytes 491528 | tf_op jit(solution)/shard_map/ppermute | solution.py:742
  108.1 4.2 %collective-permute-start.8 = (f32[10,2,16,128]{3,2,1,0:T(8,128)}, f32[10,2,16,128]{3,2,1,0:T(8,128)}, u32[]{:S(2)}, u32[]{:S(2)}) collective-permute-start(f32[10,2,16,128]{3,2,1,0:T(8,128)} %get-tuple-element.36), channel_id=1, source_target_pairs={{0,2},{1,3},{2,0},{3,1},{4,6},{5,7},{6,4},{7,5},{8,10},{9,11},{10,... | collective-permute-start | bytes 491528 | tf_op jit(solution)/shard_map/ppermute | solution.py:742
  112.3 3.4 %collective-permute-start.9 = (f32[10,2,16,128]{3,2,1,0:T(8,128)}, f32[10,2,16,128]{3,2,1,0:T(8,128)}, u32[]{:S(2)}, u32[]{:S(2)}) collective-permute-start(f32[10,2,16,128]{3,2,1,0:T(8,128)} %get-tuple-element.37), channel_id=1, source_target_pairs={{0,7},{1,4},{2,5},{3,6},{4,11},{5,8},{6,9},{7,10},{8,15},{9,12},{1... | collective-permute-start | bytes 491528 | tf_op jit(solution)/shard_map/ppermute | solution.py:742
  117.3 3.7 %collective-permute-start.13 = (f32[10,2,16,128]{3,2,1,0:T(8,128)}, f32[10,2,16,128]{3,2,1,0:T(8,128)}, u32[]{:S(2)}, u32[]{:S(2)}) collective-permute-start(f32[10,2,16,128]{3,2,1,0:T(8,128)} %get-tuple-element.41), channel_id=1, source_target_pairs={{0,1},{1,2},{2,3},{3,0},{4,5},{5,6},{6,7},{7,4},{8,9},{9,10},{10,1... | collective-permute-start | bytes 491528 | tf_op jit(solution)/shard_map/ppermute | solution.py:742
  121.7 3.3 %collective-permute-done.10.refs_10_ = f32[10,2,16,128]{3,2,1,0:T(8,128)} collective-permute-done((f32[10,2,16,128]{3,2,1,0:T(8,128)}, f32[10,2,16,128]{3,2,1,0:T(8,128)}, u32[]{:S(2)}, u32[]{:S(2)}) %collective-permute-start.10) | collective-permute-done | bytes 163872 | tf_op jit(solution)/shard_map/ppermute | solution.py:742
  125.0 2.0 collective-permute-done.14.refs_14_
  127.1 11.2 %shard_map.163 = f32[128,2,16,128]{3,2,1,0:T(8,128)} custom-call(s32[1]{0:T(128)} %bitcast.me_ref, f32[10,2,16,128]{3,2,1,0:T(8,128)} %copy-done.9, f32[10,2,16,128]{3,2,1,0:T(8,128)} %copy-done.10, f32[10,2,16,128]{3,2,1,0:T(8,128)} %copy-done.11, f32[10,2,16,128]{3,2,1,0:T(8,128)} %copy-done.12, f32[10,2,16,128]{3,2,1,0:T(8,128)} %copy-done.13, ...), custom_call_target="tpu_custom_call" | custom-call | flops 10000000000 | bytes 6000000 | tf_op jit(solution)/shard_map/pallas_call | solution.py:417
  139.6 12.3 %all-to-all-start = ((f32[128,2,16,128]{3,2,1,0:T(8,128)}), f32[128,2,16,128]{3,2,1,0:T(8,128)}, u32[]{:S(2)}, u32[]{:S(2)}) async-start(f32[128,2,16,128]{3,2,1,0:T(8,128)} %shard_map.163), calls=%async_computation | async-start | bytes 4194304 | tf_op jit(solution)/shard_map/all_to_all | solution.py:720
  152.8 4.7 %prep.1 = (bf16[16,256,256]{2,1,0:T(8,128)(2,1)}, bf16[16,256,256]{2,1,0:T(8,128)(2,1)}) custom-call(f32[2,16,128]{2,1,0:T(8,128)} %bitcast.32, f32[2,128,128]{2,1,0:T(8,128)} %constant.81.clone.dft_ref, f32[2,16,128]{2,1,0:T(8,128)} %constant.82.clone.turn_ref, f32[16,2,128]{2,1,0:T(2,128)} %constant.83.clone.wrap_ref), custom_call_target="tpu_custom_call" | custom-call | flops 2000000000 | bytes 5000000 | tf_op jit(solution)/shard_map/prep/pallas_call | solution.py:476
  157.5 9.9 %slave_azimuth.1 = (f32[2,2112,128]{2,1,0:T(8,128)}, f32[2112,128]{1,0:T(8,128)S(1)}, f32[2112,128]{1,0:T(8,128)}) custom-call(f32[16,8,2,16,128]{4,3,2,1,0:T(8,128)} %bitcast.30, bf16[16,256,256]{2,1,0:T(8,128)(2,1)} %get-tuple-element.44.ah_hbm, bf16[16,256,256]{2,1,0:T(8,128)(2,1)} %get-tuple-element.45.al_hbm), custom_call_target="tpu_custom_call" | custom-call | flops 5000000000 | bytes 10000000 | tf_op jit(solution)/shard_map/slave_azimuth/pallas_call | solution.py:558
  167.4 2.7 %collective-permute-start.16 = (f32[2112,128]{1,0:T(8,128)}, f32[2112,128]{1,0:T(8,128)S(1)}, u32[]{:S(2)}, u32[]{:S(2)}) collective-permute-start(f32[2112,128]{1,0:T(8,128)} %get-tuple-element.47), channel_id=1, source_target_pairs={{0,16},{16,1},{1,17},{17,2},{2,18},{18,3},{3,19},{19,4},{4,20},{20... | collective-permute-start | bytes 3244040 | tf_op jit(solution)/shard_map/ppermute | solution.py:711
  170.1 1.9 collective-permute-start.17
  176.7 9.1 %collective-permute-done.16.left_ref = f32[2112,128]{1,0:T(8,128)S(1)} collective-permute-done((f32[2112,128]{1,0:T(8,128)}, f32[2112,128]{1,0:T(8,128)S(1)}, u32[]{:S(2)}, u32[]{:S(2)}) %collective-permute-start.16) | collective-permute-done | bytes 1081376 | tf_op jit(solution)/shard_map/ppermute | solution.py:711
  185.7 5.0 %collective-permute-done.17.right_ref = f32[2112,128]{1,0:T(8,128)S(1)} collective-permute-done((f32[2112,128]{1,0:T(8,128)S(1)}, f32[2112,128]{1,0:T(8,128)S(1)}, u32[]{:S(2)}, u32[]{:S(2)}) %collective-permute-start.17) | collective-permute-done | bytes 1081376 | tf_op jit(solution)/shard_map/ppermute | solution.py:711
  191.7 6.8 %resample.1.m_hbm = f32[2,2048,128]{2,1,0:T(8,128)} custom-call(s32[4,2]{1,0:T(4,128)} %copy.27.az_ref, s32[4,2]{1,0:T(4,128)} %copy.28.rg_ref, f32[2,2112,128]{2,1,0:T(8,128)} %get-tuple-element.46.s_hbm, f32[2112,128]{1,0:T(8,128)} %copy-done.7, f32[2112,128]{1,0:T(8,128)} %copy-done.8), custom_call_target="tpu_custom_call" | custom-call | flops 2000000000 | bytes 10000000 | tf_op jit(solution)/shard_map/resample/pallas_call | solution.py:619
  198.6 7.8 %master_looks.1 = (f32[16,512]{1,0:T(8,128)S(1)}, f32[8,512]{1,0:T(8,128)S(1)}) custom-call(f32[16,8,2,16,128]{4,3,2,1,0:T(8,128)} %bitcast.7.x_ref, bf16[16,256,256]{2,1,0:T(8,128)(2,1)} %get-tuple-element.44.ah_hbm, bf16[16,256,256]{2,1,0:T(8,128)(2,1)} %get-tuple-element.45.al_hbm, f32[2,2048,128]{2,1,0:T(8,128)} %resample.1.m_hbm, ...), custom_call_target="tpu_custom_call" | custom-call | flops 5000000000 | bytes 10000000 | tf_op jit(solution)/shard_map/master_looks/pallas_call | solution.py:670
  206.4 3.9 %collective-permute-start.19 = (f32[8,512]{1,0:T(8,128)S(1)}, f32[8,512]{1,0:T(8,128)S(1)}, u32[]{:S(2)}, u32[]{:S(2)}) collective-permute-start(f32[8,512]{1,0:T(8,128)S(1)} %get-tuple-element.50), channel_id=1, source_target_pairs={{0,1},{16,2},{1,3},{17,4},{2,5},{18,6},{3,7},{19,8},{4,9},{20,10},... | collective-permute-start | bytes 49160 | tf_op jit(solution)/shard_map/ppermute | solution.py:758
  210.3 1.9 collective-permute-start.20
  213.0 6.6 %collective-permute-done.20.right_ref = f32[8,512]{1,0:T(8,128)S(1)} collective-permute-done((f32[8,512]{1,0:T(8,128)S(1)}, f32[8,512]{1,0:T(8,128)S(1)}, u32[]{:S(2)}, u32[]{:S(2)}) %collective-permute-start.20) | collective-permute-done | bytes 16416 | tf_op jit(solution)/shard_map/ppermute | solution.py:759
  (83 shorter events, 13.7 us)
Async XLA Ops:
  3.1 41.2 %all-to-all-start.1 = ((f32[16,10,2,16,128]{4,3,2,1,0:T(8,128)}), f32[16,10,2,16,128]{4,3,2,1,0:T(8,128)}, u32[]{:S(2)}, u32[]{:S(2)}) async-start(f32[16,10,2,16,128]{4,3,2,1,0:T(8,128)} %pre.1), calls=%async_computation.1 | async-start | bytes 5242880 | tf_op jit(solution)/shard_map/all_to_all | solution.py:738
  54.6 83.6 %all-to-all-start.2 = ((f32[128,2,16,128]{3,2,1,0:T(8,128)}), f32[128,2,16,128]{3,2,1,0:T(8,128)S(1)}, u32[]{:S(2)}, u32[]{:S(2)}) async-start(f32[128,2,16,128]{3,2,1,0:T(8,128)} %shard_map.164), calls=%async_computation.2 | async-start | bytes 4194304 | tf_op jit(solution)/shard_map/all_to_all | solution.py:720
  71.0 25.5 %collective-permute-start = (f32[10,2,16,128]{3,2,1,0:T(8,128)}, f32[10,2,16,128]{3,2,1,0:T(8,128)S(1)}, u32[]{:S(2)}, u32[]{:S(2)}) collective-permute-start(f32[10,2,16,128]{3,2,1,0:T(8,128)} %get-tuple-element.28), channel_id=1, source_target_pairs={{0,10},{1,11},{2,8},{3,9},{4,14},{5,15},{6,12},{7,13},{8,2},{9,3},... | collective-permute-start | bytes 491528 | tf_op jit(solution)/shard_map/ppermute | solution.py:742
  72.6 28.1 %collective-permute-start.1 = (f32[10,2,16,128]{3,2,1,0:T(8,128)}, f32[10,2,16,128]{3,2,1,0:T(8,128)S(1)}, u32[]{:S(2)}, u32[]{:S(2)}) collective-permute-start(f32[10,2,16,128]{3,2,1,0:T(8,128)} %get-tuple-element.29), channel_id=1, source_target_pairs={{0,9},{1,10},{2,11},{3,8},{4,13},{5,14},{6,15},{7,12},{8,1},{9,2},... | collective-permute-start | bytes 491528 | tf_op jit(solution)/shard_map/ppermute | solution.py:742
  76.5 25.8 %collective-permute-start.2 = (f32[10,2,16,128]{3,2,1,0:T(8,128)}, f32[10,2,16,128]{3,2,1,0:T(8,128)S(1)}, u32[]{:S(2)}, u32[]{:S(2)}) collective-permute-start(f32[10,2,16,128]{3,2,1,0:T(8,128)} %get-tuple-element.30), channel_id=1, source_target_pairs={{0,6},{1,7},{2,4},{3,5},{4,10},{5,11},{6,8},{7,9},{8,14},{9,15},{1... | collective-permute-start | bytes 491528 | tf_op jit(solution)/shard_map/ppermute | solution.py:742
  76.5 31.6 %collective-permute-start.3 = (f32[10,2,16,128]{3,2,1,0:T(8,128)}, f32[10,2,16,128]{3,2,1,0:T(8,128)S(1)}, u32[]{:S(2)}, u32[]{:S(2)}) collective-permute-start(f32[10,2,16,128]{3,2,1,0:T(8,128)} %get-tuple-element.31), channel_id=1, source_target_pairs={{0,14},{1,15},{2,12},{3,13},{4,2},{5,3},{6,0},{7,1},{8,6},{9,7},{1... | collective-permute-start | bytes 491528 | tf_op jit(solution)/shard_map/ppermute | solution.py:742
  80.3 31.9 %collective-permute-start.4 = (f32[10,2,16,128]{3,2,1,0:T(8,128)}, f32[10,2,16,128]{3,2,1,0:T(8,128)S(1)}, u32[]{:S(2)}, u32[]{:S(2)}) collective-permute-start(f32[10,2,16,128]{3,2,1,0:T(8,128)} %get-tuple-element.32), channel_id=1, source_target_pairs={{0,11},{1,8},{2,9},{3,10},{4,15},{5,12},{6,13},{7,14},{8,3},{9,0},... | collective-permute-start | bytes 491528 | tf_op jit(solution)/shard_map/ppermute | solution.py:742
  96.5 30.5 %copy-start.9 = (f32[10,2,16,128]{3,2,1,0:T(8,128)}, f32[10,2,16,128]{3,2,1,0:T(8,128)S(1)}, u32[]{:S(2)}) copy-start(f32[10,2,16,128]{3,2,1,0:T(8,128)S(1)} %collective-permute-done.refs_0_) | copy-start | bytes 491524
  96.5 19.2 %collective-permute-start.5 = (f32[10,2,16,128]{3,2,1,0:T(8,128)}, f32[10,2,16,128]{3,2,1,0:T(8,128)S(1)}, u32[]{:S(2)}, u32[]{:S(2)}) collective-permute-start(f32[10,2,16,128]{3,2,1,0:T(8,128)} %get-tuple-element.33), channel_id=1, source_target_pairs={{0,8},{1,9},{2,10},{3,11},{4,12},{5,13},{6,14},{7,15},{8,0},{9,1},... | collective-permute-start | bytes 491528 | tf_op jit(solution)/shard_map/ppermute | solution.py:742
  100.7 26.3 %copy-start.10 = (f32[10,2,16,128]{3,2,1,0:T(8,128)}, f32[10,2,16,128]{3,2,1,0:T(8,128)S(1)}, u32[]{:S(2)}) copy-start(f32[10,2,16,128]{3,2,1,0:T(8,128)S(1)} %collective-permute-done.1.refs_1_) | copy-start | bytes 491524
  100.7 15.0 %collective-permute-start.6 = (f32[10,2,16,128]{3,2,1,0:T(8,128)}, f32[10,2,16,128]{3,2,1,0:T(8,128)S(1)}, u32[]{:S(2)}, u32[]{:S(2)}) collective-permute-start(f32[10,2,16,128]{3,2,1,0:T(8,128)} %get-tuple-element.34), channel_id=1, source_target_pairs={{0,5},{1,6},{2,7},{3,4},{4,9},{5,10},{6,11},{7,8},{8,13},{9,14},{1... | collective-permute-start | bytes 491528 | tf_op jit(solution)/shard_map/ppermute | solution.py:742
  102.2 24.8 %copy-start.11 = (f32[10,2,16,128]{3,2,1,0:T(8,128)}, f32[10,2,16,128]{3,2,1,0:T(8,128)S(1)}, u32[]{:S(2)}) copy-start(f32[10,2,16,128]{3,2,1,0:T(8,128)S(1)} %collective-permute-done.2.refs_2_) | copy-start | bytes 491524
  102.2 14.3 %collective-permute-start.7 = (f32[10,2,16,128]{3,2,1,0:T(8,128)}, f32[10,2,16,128]{3,2,1,0:T(8,128)S(1)}, u32[]{:S(2)}, u32[]{:S(2)}) collective-permute-start(f32[10,2,16,128]{3,2,1,0:T(8,128)} %get-tuple-element.35), channel_id=1, source_target_pairs={{0,13},{1,14},{2,15},{3,12},{4,1},{5,2},{6,3},{7,0},{8,5},{9,6},{1... | collective-permute-start | bytes 491528 | tf_op jit(solution)/shard_map/ppermute | solution.py:742
  108.1 18.9 %copy-start.12 = (f32[10,2,16,128]{3,2,1,0:T(8,128)}, f32[10,2,16,128]{3,2,1,0:T(8,128)S(1)}, u32[]{:S(2)}) copy-start(f32[10,2,16,128]{3,2,1,0:T(8,128)S(1)} %collective-permute-done.3.refs_3_) | copy-start | bytes 491524
  108.1 9.2 %collective-permute-start.8 = (f32[10,2,16,128]{3,2,1,0:T(8,128)}, f32[10,2,16,128]{3,2,1,0:T(8,128)}, u32[]{:S(2)}, u32[]{:S(2)}) collective-permute-start(f32[10,2,16,128]{3,2,1,0:T(8,128)} %get-tuple-element.36), channel_id=1, source_target_pairs={{0,2},{1,3},{2,0},{3,1},{4,6},{5,7},{6,4},{7,5},{8,10},{9,11},{10,... | collective-permute-start | bytes 491528 | tf_op jit(solution)/shard_map/ppermute | solution.py:742
  112.3 14.8 %copy-start.13 = (f32[10,2,16,128]{3,2,1,0:T(8,128)}, f32[10,2,16,128]{3,2,1,0:T(8,128)S(1)}, u32[]{:S(2)}) copy-start(f32[10,2,16,128]{3,2,1,0:T(8,128)S(1)} %collective-permute-done.4.refs_4_) | copy-start | bytes 491524
  112.3 8.7 %collective-permute-start.9 = (f32[10,2,16,128]{3,2,1,0:T(8,128)}, f32[10,2,16,128]{3,2,1,0:T(8,128)}, u32[]{:S(2)}, u32[]{:S(2)}) collective-permute-start(f32[10,2,16,128]{3,2,1,0:T(8,128)} %get-tuple-element.37), channel_id=1, source_target_pairs={{0,7},{1,4},{2,5},{3,6},{4,11},{5,8},{6,9},{7,10},{8,15},{9,12},{1... | collective-permute-start | bytes 491528 | tf_op jit(solution)/shard_map/ppermute | solution.py:742
  115.7 9.3 %collective-permute-start.10 = (f32[10,2,16,128]{3,2,1,0:T(8,128)}, f32[10,2,16,128]{3,2,1,0:T(8,128)}, u32[]{:S(2)}, u32[]{:S(2)}) collective-permute-start(f32[10,2,16,128]{3,2,1,0:T(8,128)} %get-tuple-element.38), channel_id=1, source_target_pairs={{0,15},{1,12},{2,13},{3,14},{4,3},{5,0},{6,1},{7,2},{8,7},{9,4},{1... | collective-permute-start | bytes 491528 | tf_op jit(solution)/shard_map/ppermute | solution.py:742
  115.7 9.2 %collective-permute-start.11 = (f32[10,2,16,128]{3,2,1,0:T(8,128)}, f32[10,2,16,128]{3,2,1,0:T(8,128)}, u32[]{:S(2)}, u32[]{:S(2)}) collective-permute-start(f32[10,2,16,128]{3,2,1,0:T(8,128)} %get-tuple-element.39), channel_id=1, source_target_pairs={{0,4},{1,5},{2,6},{3,7},{4,8},{5,9},{6,10},{7,11},{8,12},{9,13},{1... | collective-permute-start | bytes 491528 | tf_op jit(solution)/shard_map/ppermute | solution.py:742
  116.5 8.5 %collective-permute-start.12 = (f32[10,2,16,128]{3,2,1,0:T(8,128)}, f32[10,2,16,128]{3,2,1,0:T(8,128)}, u32[]{:S(2)}, u32[]{:S(2)}) collective-permute-start(f32[10,2,16,128]{3,2,1,0:T(8,128)} %get-tuple-element.40), channel_id=1, source_target_pairs={{0,12},{1,13},{2,14},{3,15},{4,0},{5,1},{6,2},{7,3},{8,4},{9,5},{1... | collective-permute-start | bytes 491528 | tf_op jit(solution)/shard_map/ppermute | solution.py:742
  117.3 7.7 %collective-permute-start.13 = (f32[10,2,16,128]{3,2,1,0:T(8,128)}, f32[10,2,16,128]{3,2,1,0:T(8,128)}, u32[]{:S(2)}, u32[]{:S(2)}) collective-permute-start(f32[10,2,16,128]{3,2,1,0:T(8,128)} %get-tuple-element.41), channel_id=1, source_target_pairs={{0,1},{1,2},{2,3},{3,0},{4,5},{5,6},{6,7},{7,4},{8,9},{9,10},{10,1... | collective-permute-start | bytes 491528 | tf_op jit(solution)/shard_map/ppermute | solution.py:742
  121.0 6.0 %collective-permute-start.14 = (f32[10,2,16,128]{3,2,1,0:T(8,128)}, f32[10,2,16,128]{3,2,1,0:T(8,128)}, u32[]{:S(2)}, u32[]{:S(2)}) collective-permute-start(f32[10,2,16,128]{3,2,1,0:T(8,128)} %get-tuple-element.42), channel_id=1, source_target_pairs={{0,3},{1,0},{2,1},{3,2},{4,7},{5,4},{6,5},{7,6},{8,11},{9,8},{10,9... | collective-permute-start | bytes 491528 | tf_op jit(solution)/shard_map/ppermute | solution.py:742
  139.6 58.9 %all-to-all-start = ((f32[128,2,16,128]{3,2,1,0:T(8,128)}), f32[128,2,16,128]{3,2,1,0:T(8,128)}, u32[]{:S(2)}, u32[]{:S(2)}) async-start(f32[128,2,16,128]{3,2,1,0:T(8,128)} %shard_map.163), calls=%async_computation | async-start | bytes 4194304 | tf_op jit(solution)/shard_map/all_to_all | solution.py:720
  157.5 14.5 %copy-start.5 = (s32[4,2]{0,1:T(2,128)S(1)}, s32[4,2]{0,1:T(2,128)}, u32[]{:S(2)}) copy-start(s32[4,2]{0,1:T(2,128)} %param.22) | copy-start | bytes 100
  157.5 14.5 %copy-start.6 = (s32[4,2]{0,1:T(2,128)S(1)}, s32[4,2]{0,1:T(2,128)}, u32[]{:S(2)}) copy-start(s32[4,2]{0,1:T(2,128)} %param.21) | copy-start | bytes 100
  157.5 15.2 %copy-start.4 = (s32[256]{0:T(256)S(1)}, s32[256]{0:T(256)}, u32[]{:S(2)}) copy-start(s32[256]{0:T(256)} %param.23) | copy-start | bytes 3076
  167.4 18.3 %collective-permute-start.16 = (f32[2112,128]{1,0:T(8,128)}, f32[2112,128]{1,0:T(8,128)S(1)}, u32[]{:S(2)}, u32[]{:S(2)}) collective-permute-start(f32[2112,128]{1,0:T(8,128)} %get-tuple-element.47), channel_id=1, source_target_pairs={{0,16},{16,1},{1,17},{17,2},{2,18},{18,3},{3,19},{19,4},{4,20},{20... | collective-permute-start | bytes 3244040 | tf_op jit(solution)/shard_map/ppermute | solution.py:711
  170.1 20.7 %collective-permute-start.17 = (f32[2112,128]{1,0:T(8,128)S(1)}, f32[2112,128]{1,0:T(8,128)S(1)}, u32[]{:S(2)}, u32[]{:S(2)}) collective-permute-start(f32[2112,128]{1,0:T(8,128)S(1)} %get-tuple-element.48), channel_id=1, source_target_pairs={{16,0},{1,16},{17,1},{2,17},{18,2},{3,18},{19,3},{4,19},{20,4},{5,... | collective-permute-start | bytes 3244040 | tf_op jit(solution)/shard_map/ppermute | solution.py:711
  172.0 3.3 %collective-permute-start.15 = (s32[2,4,2]{1,2,0:T(2,128)S(1)}, s32[2,4,2]{1,2,0:T(2,128)S(1)}, u32[]{:S(2)}, u32[]{:S(2)}) collective-permute-start(s32[2,4,2]{1,2,0:T(2,128)S(1)} %pad_add_fusion), channel_id=1, source_target_pairs={{0,0},{1,16},{2,1},{3,17},{4,2},{5,18},{6,3},{7,19},{8,4},{9,20},{... | collective-permute-start | bytes 200 | tf_op jit(solution)/shard_map/ppermute | solution.py:705
  206.4 6.6 %collective-permute-start.19 = (f32[8,512]{1,0:T(8,128)S(1)}, f32[8,512]{1,0:T(8,128)S(1)}, u32[]{:S(2)}, u32[]{:S(2)}) collective-permute-start(f32[8,512]{1,0:T(8,128)S(1)} %get-tuple-element.50), channel_id=1, source_target_pairs={{0,1},{16,2},{1,3},{17,4},{2,5},{18,6},{3,7},{19,8},{4,9},{20,10},... | collective-permute-start | bytes 49160 | tf_op jit(solution)/shard_map/ppermute | solution.py:758
  210.3 9.3 %collective-permute-start.20 = (f32[8,512]{1,0:T(8,128)S(1)}, f32[8,512]{1,0:T(8,128)S(1)}, u32[]{:S(2)}, u32[]{:S(2)}) collective-permute-start(f32[8,512]{1,0:T(8,128)S(1)} %get-tuple-element.50), channel_id=1, source_target_pairs={{16,0},{1,1},{17,2},{2,3},{18,4},{3,5},{19,6},{4,7},{20,8},{5,9},{... | collective-permute-start | bytes 49160 | tf_op jit(solution)/shard_map/ppermute | solution.py:759
  212.3 7.4 %collective-permute-start.18 = (f32[16,512]{1,0:T(8,128)S(1)}, f32[16,512]{1,0:T(8,128)S(1)}, u32[]{:S(2)}, u32[]{:S(2)}) collective-permute-start(f32[16,512]{1,0:T(8,128)S(1)} %get-tuple-element.49), channel_id=1, source_target_pairs={{0,0},{16,1},{1,2},{17,3},{2,4},{18,5},{3,6},{19,7},{4,8},{20,9},{... | collective-permute-start | bytes 98312 | tf_op jit(solution)/shard_map/ppermute | solution.py:757
  (9 other events, 67.6 us)

commit v6 on v5

--- a/solution.py
+++ b/solution.py
@@ -15,6 +15,7 @@
 BA = 512
 BR = 64
 ASH = 32
+RSH = 64
 NBA = 4
 ALL = ("az", "rg")
 NP = 16
@@ -188,6 +189,9 @@
 SMEM = pl.BlockSpec(memory_space=pltpu.SMEM)
 
 
+AZIMUTH_MIB = 61
+
+
 def limit(mib):
     return pltpu.CompilerParams(vmem_limit_bytes=mib << 20)
 
@@ -288,7 +292,7 @@
                 d_ref[at, 1, rows, :] = i
         return carry
 
-    lax.fori_loop(0, NQ, outer, 0)
+    lax.fori_loop(0, NQ, outer, 0, unroll=2)
     ready(None)
 
     def middle(kp, carry):
@@ -319,7 +323,7 @@
             d_ref[at, 1] = i
         return carry
 
-    lax.fori_loop(0, NP, middle, 0, unroll=2)
+    lax.fori_loop(0, NP, middle, 0, unroll=4)
 
     def inner(q, carry):
         for g in range(2):
@@ -331,7 +335,7 @@
                 d_ref[p * NQ + q, 1, rows, :] = v[p][1]
         return carry
 
-    lax.fori_loop(0, NQ, inner, 0)
+    lax.fori_loop(0, NQ, inner, 0, unroll=2)
 
     def store(part):
         at = pl.ds(32 * part, 32)
@@ -438,7 +442,7 @@
     )
 
 
-def _prep_kernel(h_ref, dft_ref, turn_ref, wrap_ref, ah_ref, al_ref, g_ref):
+def _prep_kernel(h_ref, dft_ref, turn_ref, wrap_ref, a_ref, g_ref):
     def mul(a, b):
         return jnp.dot(a, b, precision=lax.Precision.HIGHEST, preferred_element_type=F32)
 
@@ -460,11 +464,11 @@
         turned = cmul(m, (wrap_ref[k, 0:1, :], wrap_ref[k, 1:2, :]))
         re = jnp.where(over, turned[0], m[0])
         im = jnp.where(over, turned[1], m[1])
-        for rows, cols, block in ((0, 0, re), (0, 1, -im), (1, 0, im), (1, 1, re)):
+        for part, block in enumerate((re, -im)):
+            cols = slice(128 * part, 128 * part + 128)
             high, low = split(block)
-            at = (k, slice(128 * rows, 128 * rows + 128), slice(128 * cols, 128 * cols + 128))
-            ah_ref[at] = high
-            al_ref[at] = low
+            a_ref[k, 0:128, cols] = high
+            a_ref[k, 128:256, cols] = low
         return carry
 
     lax.fori_loop(0, 16, body, 0, unroll=2)
@@ -472,25 +476,26 @@
 
 def prep(h):
     t = TABLES
-    shape = jax.ShapeDtypeStruct((16, 256, 256), BF16)
     return pl.pallas_call(
         _prep_kernel,
-        out_shape=(shape, shape),
+        out_shape=jax.ShapeDtypeStruct((16, 256, 256), BF16),
         scratch_shapes=[pltpu.VMEM((16, 2, 128), F32)],
         cost_estimate=pl.CostEstimate(flops=2 * 10**9, bytes_accessed=5 * 10**6, transcendentals=0),
         name="prep",
     )(h, t["dft"], t["turn"], t["wrap"])
 
 
-def _azimuth_front(x_ref, ah_hbm, al_hbm, e_ref, ah_ref, al_ref, sem):
-    matrices = [
-        pltpu.make_async_copy(ah_hbm, ah_ref, sem.at[0]),
-        pltpu.make_async_copy(al_hbm, al_ref, sem.at[1]),
-    ]
-    for copy in matrices:
-        copy.start()
+def _azimuth_front(x_hbm, a_hbm, e_ref, x_ref, a_ref, sem):
+    def load(s):
+        return pltpu.make_async_copy(x_hbm.at[:, s], x_ref.at[:, s], sem.at[s])
+
+    matrices = pltpu.make_async_copy(a_hbm, a_ref, sem.at[8])
+    for s in range(8):
+        load(s).start()
+    matrices.start()
 
     def first(s, carry):
+        load(s).wait()
         for g in range(2):
             rows = slice(8 * g, 8 * g + 8)
             v = [(x_ref[a, s, 0, rows, :], x_ref[a, s, 1, rows, :]) for a in range(16)]
@@ -501,14 +506,21 @@
                     e_ref[k, pl.ds(at, 8), :] = v[k][c]
         return carry
 
-    lax.fori_loop(0, 8, first, 0)
-    for copy in matrices:
-        copy.wait()
+    lax.fori_loop(0, 8, first, 0, unroll=2)
+    matrices.wait()
 
     def second(k, carry):
-        hi, lo = split(e_ref[k])
-        wide = dot(ah_ref[k], jnp.concatenate([hi, lo], axis=1))
-        e_ref[k] = wide[:, :128] + wide[:, 128:] + dot(al_ref[k], hi)
+        re_hi, re_lo = split(e_ref[k, 0:128, :])
+        im_hi, im_lo = split(e_ref[k, 128:256, :])
+
+        def turned(re, im):
+            straight = jnp.concatenate([re, im], axis=0)
+            return jnp.concatenate([straight, jnp.concatenate([im, -re], axis=0)], axis=1)
+
+        y = dot(a_ref[k], turned(re_hi, im_hi))
+        y = y[:128] + y[128:] + dot(a_ref[k, 0:128, :], turned(re_lo, im_lo))
+        e_ref[k, 0:128, :] = y[:, :128]
+        e_ref[k, 128:256, :] = y[:, 128:]
         return carry
 
     lax.fori_loop(0, 16, second, 0, unroll=4)
@@ -516,9 +528,9 @@
 
 AZIMUTH_SCRATCH = [
     pltpu.VMEM((16, 256, 128), F32),
+    pltpu.VMEM((16, 8, 2, 16, 128), F32),
     pltpu.VMEM((16, 256, 256), BF16),
-    pltpu.VMEM((16, 256, 256), BF16),
-    pltpu.SemaphoreType.DMA((4,)),
+    pltpu.SemaphoreType.DMA((13,)),
 ]
 
 
@@ -528,11 +540,12 @@
     return dft16(v, 1)
 
 
-def _slave_kernel(x_ref, ah_hbm, al_hbm, o_hbm, left_ref, right_ref, o_ref, e_ref, *scratch):
-    _azimuth_front(x_ref, ah_hbm, al_hbm, e_ref, *scratch)
+def _slave_kernel(x_hbm, a_hbm, left_hbm, right_hbm, left_ref, right_ref, *scratch):
+    _azimuth_front(x_hbm, a_hbm, *scratch)
+    e_ref, sem = scratch[0], scratch[-1]
     low = lax.broadcasted_iota(jnp.int32, (8, 128), 1) < 64
     zero = jnp.zeros((ASH, 128), F32)
-    for ref in (o_ref.at[0], o_ref.at[1], left_ref, right_ref):
+    for ref in (left_ref, right_ref):
         ref[0:ASH, :] = zero
         ref[ASH + LINES :, :] = zero
 
@@ -541,101 +554,106 @@
         for a in range(16):
             rows = pl.ds(pl.multiple_of(a * 128 + g * 8 + ASH, 8), 8)
             r, i = v[a]
-            o_ref[0, rows, :] = r
-            o_ref[1, rows, :] = i
             left_ref[rows, :] = jnp.where(low, r, pltpu.roll(i, 64, 1))
             right_ref[rows, :] = jnp.where(low, pltpu.roll(r, 64, 1), i)
         return carry
 
-    lax.fori_loop(0, 16, third, 0)
-    out = pltpu.make_async_copy(o_ref, o_hbm, scratch[-1].at[2])
-    out.start()
-    out.wait()
-
-
-def slave_azimuth(x, ah, al):
+    lax.fori_loop(0, 16, third, 0, unroll=2)
+    copies = [
+        pltpu.make_async_copy(right_ref, right_hbm, sem.at[10]),
+        pltpu.make_async_copy(left_ref, left_hbm, sem.at[9]),
+    ]
+    for copy in copies:
+        copy.start()
+    for copy in copies:
+        copy.wait()
+
+
+def slave_azimuth(x, a):
     side = jax.ShapeDtypeStruct((LINES + 2 * ASH, 128), F32)
     return pl.pallas_call(
         _slave_kernel,
-        out_shape=(jax.ShapeDtypeStruct((2, LINES + 2 * ASH, 128), F32), side, side),
-        in_specs=[VMEM, HBM, HBM],
-        out_specs=(HBM, VMEM, VMEM),
-        scratch_shapes=[pltpu.VMEM((2, LINES + 2 * ASH, 128), F32)] + AZIMUTH_SCRATCH,
-        compiler_params=limit(52),
+        in_specs=[HBM, HBM],
+        out_specs=(HBM, HBM),
+        out_shape=(side, side),
+        scratch_shapes=[pltpu.VMEM(side.shape, F32)] * 2 + AZIMUTH_SCRATCH,
         cost_estimate=pl.CostEstimate(flops=5 * 10**9, bytes_accessed=10**7, transcendentals=0),
+        compiler_params=limit(AZIMUTH_MIB),
         name="slave_azimuth",
-    )(x.reshape(16, 8, 2, 16, 128), ah, al)
-
-
-def _resample_kernel(az_ref, rg_ref, s_hbm, left_ref, right_ref, o_hbm, s_ref, o_ref, sem):
+    )(x.reshape(16, 8, 2, 16, 128), a)
+
+
+def _resample_kernel(az_ref, rg_ref, *refs):
+    packs, o_hbm, w_ref, o_ref, sem = refs[:4], refs[4], refs[5], refs[6], refs[7]
     lane = lax.broadcasted_iota(jnp.int32, (64, 128), 1)
     low = lane < 64
 
     def load(block):
         rows = pl.ds(0, BA + 2 * ASH) if block == 0 else pl.ds(block * BA + 2 * ASH, BA)
-        return pltpu.make_async_copy(s_hbm.at[:, rows], s_ref.at[:, rows], sem.at[block])
+        return [
+            pltpu.make_async_copy(pack.at[rows], w_ref.at[k, rows], sem.at[4 * block + k])
+            for k, pack in enumerate(packs)
+        ]
 
     def store(block):
         rows = pl.ds(block * BA, BA)
-        return pltpu.make_async_copy(o_ref.at[:, rows], o_hbm.at[:, rows], sem.at[4 + block])
+        return pltpu.make_async_copy(o_ref.at[:, rows], o_hbm.at[:, rows], sem.at[16 + block])
 
     for block in range(NBA):
-        load(block).start()
+        for copy in load(block):
+            copy.start()
     for block in range(NBA):
-        load(block).wait()
+        for copy in load(block):
+            copy.wait()
 
         def move(t, carry):
             parts = []
-            for r, side_ref in ((0, left_ref), (1, right_ref)):
-                shift = rg_ref[block, r]
+            for r in range(2):
+                shift = rg_ref[block, r] + RSH
+                first = shift // 64 + r
+                second = jnp.minimum(first + 1, 3)
+                s = lax.rem(shift, 64)
                 rows = pl.ds(block * BA + t * 64 + ASH + az_ref[block, r], 64)
-                whole = lax.rem(256 - shift, 128)
-                half = lax.rem(192 - shift, 128)
-                near = lane + shift >= 0 if r == 0 else lane + shift < 128
-                side = side_ref[rows, :]
-                turns = (half, whole) if r == 0 else (whole, half)
                 parts.append(
-                    [
-                        jnp.where(
-                            near,
-                            pltpu.roll(s_ref[c, rows, :], whole, 1),
-                            pltpu.roll(side, turns[c], 1),
-                        )
-                        for c in range(2)
-                    ]
+                    jnp.where(
+                        (lane & 63) + s < 64,
+                        pltpu.roll(w_ref[first, rows, :], lax.rem(128 - s, 128), 1),
+                        pltpu.roll(w_ref[second, rows, :], 64 - s, 1),
+                    )
                 )
             rows = pl.ds(pl.multiple_of(block * BA + t * 64, 64), 64)
-            for c in range(2):
-                o_ref[c, rows, :] = jnp.where(low, parts[0][c], parts[1][c])
+            o_ref[0, rows, :] = jnp.where(low, parts[0], pltpu.roll(parts[1], 64, 1))
+            o_ref[1, rows, :] = jnp.where(low, pltpu.roll(parts[0], 64, 1), parts[1])
             return carry
 
-        lax.fori_loop(0, BA // 64, move, 0, unroll=2)
+        lax.fori_loop(0, BA // 64, move, 0, unroll=4)
         store(block).start()
     for block in range(NBA):
         store(block).wait()
 
 
-def resample(az_shift, rg_shift, focused, left, right):
+def resample(az_shift, rg_shift, packs):
     return pl.pallas_call(
         _resample_kernel,
-        in_specs=[SMEM, SMEM, HBM, VMEM, VMEM],
+        in_specs=[SMEM, SMEM] + [HBM] * 4,
         out_specs=HBM,
         out_shape=jax.ShapeDtypeStruct((2, LINES, 128), F32),
         scratch_shapes=[
-            pltpu.VMEM((2, LINES + 2 * ASH, 128), F32),
+            pltpu.VMEM((4, LINES + 2 * ASH, 128), F32),
             pltpu.VMEM((2, LINES, 128), F32),
-            pltpu.SemaphoreType.DMA((8,)),
+            pltpu.SemaphoreType.DMA((20,)),
         ],
         cost_estimate=pl.CostEstimate(flops=2 * 10**9, bytes_accessed=10**7, transcendentals=0),
         compiler_params=limit(61),
         name="resample",
-    )(az_shift, rg_shift, focused, left, right)
-
-
-def _master_kernel(x_ref, ah_hbm, al_hbm, m_hbm, n_ref, pick_ref, box_ref, side_ref, c_ref, m_ref, e_ref, *scratch):
-    moved = pltpu.make_async_copy(m_hbm, m_ref, scratch[-1].at[2])
+    )(az_shift, rg_shift, *packs)
+
+
+def _master_kernel(x_hbm, a_hbm, m_hbm, n_ref, pick_ref, box_ref, side_ref, c_ref, m_ref, *scratch):
+    e_ref = scratch[0]
+    moved = pltpu.make_async_copy(m_hbm, m_ref, scratch[-1].at[9])
     moved.start()
-    _azimuth_front(x_ref, ah_hbm, al_hbm, e_ref, *scratch)
+    _azimuth_front(x_hbm, a_hbm, *scratch)
     moved.wait()
     line = lax.broadcasted_iota(jnp.int32, (8, 128), 0)
     count = n_ref[...]
@@ -651,7 +669,7 @@
             c_ref[pl.ds(at + LINES, 8), :] = jnp.where(keep, i * sr - r * si, 0.0)
         return carry
 
-    lax.fori_loop(0, 16, third, 0)
+    lax.fori_loop(0, 16, third, 0, unroll=2)
     total = c_ref[pl.ds(0, 512, stride=LOOK), :]
     for j in range(1, LOOK):
         total = total + c_ref[pl.ds(j, 512, stride=LOOK), :]
@@ -666,20 +684,20 @@
     side_ref[...] = y[16:]
 
 
-def master_looks(x, ah, al, moved, counts):
+def master_looks(x, a, moved, counts):
     return pl.pallas_call(
         _master_kernel,
         out_shape=(
             jax.ShapeDtypeStruct((16, 512), F32),
             jax.ShapeDtypeStruct((8, 512), F32),
         ),
-        in_specs=[VMEM, HBM, HBM, HBM, VMEM, VMEM],
-        compiler_params=limit(52),
+        in_specs=[HBM, HBM, HBM, VMEM, VMEM],
+        compiler_params=limit(AZIMUTH_MIB),
         scratch_shapes=[pltpu.VMEM((2 * LINES, 128), F32), pltpu.VMEM((2, LINES, 128), F32)]
         + AZIMUTH_SCRATCH,
         cost_estimate=pl.CostEstimate(flops=5 * 10**9, bytes_accessed=10**7, transcendentals=0),
         name="master_looks",
-    )(x.reshape(16, 8, 2, 16, 128), ah, al, moved, counts, TABLES["pick"])
+    )(x.reshape(16, 8, 2, 16, 128), a, moved, counts, TABLES["pick"])
 
 
 def _final_kernel(box_ref, left_ref, right_ref, scale_ref, o_ref):
@@ -746,14 +764,14 @@
     ]
     slave = range_compress(_range_kernel, [HBM], [slave], hf)
     slave = columns_of(slave)
-    ah, al = prep(h)
+    matrices = prep(h)
     master = range_compress(_range_shift_kernel, [SMEM] + [HBM] * NP, [me, *master], hf)
     master = columns_of(master)
-    focused, to_left, to_right = slave_azimuth(slave, ah, al)
-    from_left, from_right = halo(to_right, to_left)
-    moved = resample(shifts[0], shifts[1], focused, from_left, from_right)
-
-    box, side = master_looks(master, ah, al, moved, col_counts)
+    low, high = slave_azimuth(slave, matrices)
+    from_left, from_right = halo(high, low)
+    moved = resample(shifts[0], shifts[1], (from_left, low, high, from_right))
+
+    box, side = master_looks(master, matrices, moved, col_counts)
     box = lax.ppermute(box, ALL, [(worker(b), b) for b in range(128)])
     left = lax.ppermute(side, ALL, [(worker(b), b + 1) for b in range(127)])
     right = lax.ppermute(side, ALL, [(worker(b + 1), b) for b in range(127)])

time: 224 us -> 222 us (level)
  the two profiles are of different devices: /device:TPU:103 before, /device:TPU:7 now
where the time goes in v6:
time: 222 us; the launch traced here: 221 us
  starting transfers between devices  81.1 us (37%)
  waiting for transfers between devices  79.1 us (36%)
  Pallas kernels  49.4 us (22%)
  local copies, waits for them, and re-layouts  9.47 us (4%)
    all_to_all x1, waiting for transfers between devices, local(): slave = lax.all_to_all(slave, 'rg', 0, 0, tiled=True)  34.1 us
    ppermute x15, starting transfers between devices, local(): lax.ppermute(piece, 'rg', [(r, shifted(r, shift)) for r in range(NP)])  31.4 us
    ppermute x15, waiting for transfers between devices, local(): lax.ppermute(piece, 'rg', [(r, shifted(r, shift)) for r in range(NP)])  27.2 us
    all_to_all x2, starting transfers between devices, columns_of(): return lax.all_to_all(ranged, ALL, 0, 0, tiled=True)  20 us
    pallas_call x2, Pallas kernels, range_compress(): pl.pallas_call(kernel, in_specs=specs + [HBM] * 7, out_specs=HBM, out_sha...  18.4 us
    ppermute x1, waiting for transfers between devices, to_worker(): return lax.ppermute(x, ALL, [(b, worker(b)) for b in range(128)])  11.1 us
    all_to_all x1, starting transfers between devices, local(): slave = lax.all_to_all(slave, 'rg', 0, 0, tiled=True)  7.85 us
    pallas_call x1, Pallas kernels, master_looks(): pl.pallas_call(_master_kernel, out_shape=(jax.ShapeDtypeStruct((16, 512),...  7.38 us
  transfers between devices with their start and end apart: 24, of which 9 were waited for; matrix products, arithmetic and copies ran while one was open for 3% of the time, Pallas kernels for 13%

profile of v6, /device:TPU:7, one launch (start us, length us, event | category | flops | bytes accessed | tf_op | source)
XLA Modules:
  0.0 221.1 jit_solution(5381152202921504260)
XLA Ops:
  0.0 3.0 %pre.1 = f32[16,10,2,16,128]{4,3,2,1,0:T(8,128)} custom-call(f32[5000,128]{1,0:T(8,128)} %bitcast.28), custom_call_target="tpu_custom_call" | custom-call | flops 100000000 | bytes 10000000 | tf_op jit(solution)/shard_map/pre/pallas_call | solution.py:255
  3.0 7.8 %all-to-all-start.1 = ((f32[16,10,2,16,128]{4,3,2,1,0:T(8,128)}), f32[16,10,2,16,128]{4,3,2,1,0:T(8,128)}, u32[]{:S(2)}, u32[]{:S(2)}) async-start(f32[16,10,2,16,128]{4,3,2,1,0:T(8,128)} %pre.1), calls=%async_computation.1 | async-start | bytes 5242880 | tf_op jit(solution)/shard_map/all_to_all | solution.py:756
  13.2 34.1 %all-to-all-done.1.x_hbm = f32[16,10,2,16,128]{4,3,2,1,0:T(8,128)} async-done(((f32[16,10,2,16,128]{4,3,2,1,0:T(8,128)}), f32[16,10,2,16,128]{4,3,2,1,0:T(8,128)}, u32[]{:S(2)}, u32[]{:S(2)}) %all-to-all-start.1) | async-done | bytes 2621472 | tf_op jit(solution)/shard_map/all_to_all | solution.py:756
  47.3 8.7 %shard_map.164 = f32[128,2,16,128]{3,2,1,0:T(8,128)} custom-call(f32[16,10,2,16,128]{4,3,2,1,0:T(8,128)} %all-to-all-done.1.x_hbm, f32[10,2,128]{2,1,0:T(2,128)} %constant.75.clone.refs_16_.refs_0_, f32[160,2,128]{2,1,0:T(2,128)} %pad.8.refs_17_.refs_1_, bf16[256,256]{1,0:T(8,128)(2,1)} %constant.76.clone.refs_18_.refs_2_, ...), custom_call_target="tpu_custom_call" | custom-call | flops 10000000000 | bytes 6000000 | tf_op jit(solution)/shard_map/pallas_call | solution.py:421
  56.0 10.3 %all-to-all-start.2 = ((f32[128,2,16,128]{3,2,1,0:T(8,128)}), f32[128,2,16,128]{3,2,1,0:T(8,128)S(1)}, u32[]{:S(2)}, u32[]{:S(2)}) async-start(f32[128,2,16,128]{3,2,1,0:T(8,128)} %shard_map.164), calls=%async_computation.2 | async-start | bytes 4194304 | tf_op jit(solution)/shard_map/all_to_all | solution.py:738
  66.3 3.7 %pre_shifts.1 = (f32[10,2,16,128]{3,2,1,0:T(8,128)}, f32[10,2,16,128]{3,2,1,0:T(8,128)}, f32[10,2,16,128]{3,2,1,0:T(8,128)}, f32[10,2,16,128]{3,2,1,0:T(8,128)},...) custom-call(s32[1]{0:T(128)} %bitcast.me_ref, ...), custom_call_target="tpu_custom_call" | custom-call | flops 100000000 | bytes 10000000 | tf_op jit(solution)/shard_map/pre_shifts/pallas_call | solution.py:267
  70.1 4.1 %collective-permute-start = (f32[10,2,16,128]{3,2,1,0:T(8,128)}, f32[10,2,16,128]{3,2,1,0:T(8,128)S(1)}, u32[]{:S(2)}, u32[]{:S(2)}) collective-permute-start(f32[10,2,16,128]{3,2,1,0:T(8,128)} %get-tuple-element.25), channel_id=1, source_target_pairs={{0,10},{1,11},{2,8},{3,9},{4,14},{5,15},{6,12},{7,13},{8,2},{9,3},... | collective-permute-start | bytes 491528 | tf_op jit(solution)/shard_map/ppermute | solution.py:760
  76.2 4.4 %collective-permute-start.3 = (f32[10,2,16,128]{3,2,1,0:T(8,128)}, f32[10,2,16,128]{3,2,1,0:T(8,128)S(1)}, u32[]{:S(2)}, u32[]{:S(2)}) collective-permute-start(f32[10,2,16,128]{3,2,1,0:T(8,128)} %get-tuple-element.28), channel_id=1, source_target_pairs={{0,14},{1,15},{2,12},{3,13},{4,2},{5,3},{6,0},{7,1},{8,6},{9,7},{1... | collective-permute-start | bytes 491528 | tf_op jit(solution)/shard_map/ppermute | solution.py:760
  81.9 16.0 %collective-permute-done.refs_0_ = f32[10,2,16,128]{3,2,1,0:T(8,128)S(1)} collective-permute-done((f32[10,2,16,128]{3,2,1,0:T(8,128)}, f32[10,2,16,128]{3,2,1,0:T(8,128)S(1)}, u32[]{:S(2)}, u32[]{:S(2)}) %collective-permute-start) | collective-permute-done | bytes 163872 | tf_op jit(solution)/shard_map/ppermute | solution.py:760
  98.2 6.2 %collective-permute-done.1.refs_1_ = f32[10,2,16,128]{3,2,1,0:T(8,128)S(1)} collective-permute-done((f32[10,2,16,128]{3,2,1,0:T(8,128)}, f32[10,2,16,128]{3,2,1,0:T(8,128)S(1)}, u32[]{:S(2)}, u32[]{:S(2)}) %collective-permute-start.1) | collective-permute-done | bytes 163872 | tf_op jit(solution)/shard_map/ppermute | solution.py:760
  104.4 6.8 %collective-permute-start.7 = (f32[10,2,16,128]{3,2,1,0:T(8,128)}, f32[10,2,16,128]{3,2,1,0:T(8,128)S(1)}, u32[]{:S(2)}, u32[]{:S(2)}) collective-permute-start(f32[10,2,16,128]{3,2,1,0:T(8,128)} %get-tuple-element.32), channel_id=1, source_target_pairs={{0,13},{1,14},{2,15},{3,12},{4,1},{5,2},{6,3},{7,0},{8,5},{9,6},{1... | collective-permute-start | bytes 491528 | tf_op jit(solution)/shard_map/ppermute | solution.py:760
  111.2 1.8 collective-permute-start.8
  113.0 2.7 %collective-permute-start.9 = (f32[10,2,16,128]{3,2,1,0:T(8,128)}, f32[10,2,16,128]{3,2,1,0:T(8,128)}, u32[]{:S(2)}, u32[]{:S(2)}) collective-permute-start(f32[10,2,16,128]{3,2,1,0:T(8,128)} %get-tuple-element.34), channel_id=1, source_target_pairs={{0,7},{1,4},{2,5},{3,6},{4,11},{5,8},{6,9},{7,10},{8,15},{9,12},{1... | collective-permute-start | bytes 491528 | tf_op jit(solution)/shard_map/ppermute | solution.py:760
  116.8 1.9 collective-permute-start.12
  118.7 4.3 %collective-permute-start.13 = (f32[10,2,16,128]{3,2,1,0:T(8,128)}, f32[10,2,16,128]{3,2,1,0:T(8,128)}, u32[]{:S(2)}, u32[]{:S(2)}) collective-permute-start(f32[10,2,16,128]{3,2,1,0:T(8,128)} %get-tuple-element.38), channel_id=1, source_target_pairs={{0,1},{1,2},{2,3},{3,0},{4,5},{5,6},{6,7},{7,4},{8,9},{9,10},{10,1... | collective-permute-start | bytes 491528 | tf_op jit(solution)/shard_map/ppermute | solution.py:760
  124.7 2.1 collective-permute-done.13.refs_13_
  126.8 1.9 collective-permute-done.14.refs_14_
  128.7 9.6 %shard_map.163 = f32[128,2,16,128]{3,2,1,0:T(8,128)} custom-call(s32[1]{0:T(128)} %bitcast.me_ref, f32[10,2,16,128]{3,2,1,0:T(8,128)} %copy-done.8, f32[10,2,16,128]{3,2,1,0:T(8,128)} %copy-done.9, f32[10,2,16,128]{3,2,1,0:T(8,128)} %copy-done.10, f32[10,2,16,128]{3,2,1,0:T(8,128)} %copy-done.11, f32[10,2,16,128]{3,2,1,0:T(8,128)} %copy-done.12, ...), custom_call_target="tpu_custom_call" | custom-call | flops 10000000000 | bytes 6000000 | tf_op jit(solution)/shard_map/pallas_call | solution.py:421
  138.4 1.4 copy-done
  139.8 9.7 %all-to-all-start = ((f32[128,2,16,128]{3,2,1,0:T(8,128)}), f32[128,2,16,128]{3,2,1,0:T(8,128)}, u32[]{:S(2)}, u32[]{:S(2)}) async-start(f32[128,2,16,128]{3,2,1,0:T(8,128)} %shard_map.163), calls=%async_computation | async-start | bytes 4194304 | tf_op jit(solution)/shard_map/all_to_all | solution.py:738
  150.3 3.9 %prep.1.a_hbm = bf16[16,256,256]{2,1,0:T(8,128)(2,1)} custom-call(f32[2,16,128]{2,1,0:T(8,128)} %bitcast.32, f32[2,128,128]{2,1,0:T(8,128)} %constant.81.clone.dft_ref, f32[2,16,128]{2,1,0:T(8,128)} %constant.82.clone.turn_ref, f32[16,2,128]{2,1,0:T(2,128)} %constant.83.clone.wrap_ref), custom_call_target="tpu_custom_call" | custom-call | flops 2000000000 | bytes 5000000 | tf_op jit(solution)/shard_map/prep/pallas_call | solution.py:479
  154.2 6.5 %slave_azimuth.1 = (f32[2112,128]{1,0:T(8,128)}, f32[2112,128]{1,0:T(8,128)}) custom-call(f32[16,8,2,16,128]{4,3,2,1,0:T(8,128)} %bitcast.30, bf16[16,256,256]{2,1,0:T(8,128)(2,1)} %prep.1.a_hbm), custom_call_target="tpu_custom_call" | custom-call | flops 5000000000 | bytes 10000000 | tf_op jit(solution)/shard_map/slave_azimuth/pallas_call | solution.py:574
  160.7 3.5 %collective-permute-start.16 = (f32[2112,128]{1,0:T(8,128)}, f32[2112,128]{1,0:T(8,128)S(1)}, u32[]{:S(2)}, u32[]{:S(2)}) collective-permute-start(f32[2112,128]{1,0:T(8,128)} %get-tuple-element.41.refs_2_), channel_id=1, source_target_pairs={{0,16},{16,1},{1,17},{17,2},{2,18},{18,3},{3,19},{19,4},{4,20},{20... | collective-permute-start | bytes 3244040 | tf_op jit(solution)/shard_map/ppermute | solution.py:729
  164.2 1.9 collective-permute-start.17
  166.2 5.8 %collective-permute-start.15 = (s32[2,4,2]{1,2,0:T(2,128)S(1)}, s32[2,4,2]{1,2,0:T(2,128)S(1)}, u32[]{:S(2)}, u32[]{:S(2)}) collective-permute-start(s32[2,4,2]{1,2,0:T(2,128)S(1)} %pad_add_fusion), channel_id=1, source_target_pairs={{0,0},{1,16},{2,1},{3,17},{4,2},{5,18},{6,3},{7,19},{8,4},{9,20},{... | collective-permute-start | bytes 200 | tf_op jit(solution)/shard_map/ppermute | solution.py:723
  175.2 11.1 %collective-permute-done.15 = s32[2,4,2]{1,2,0:T(2,128)S(1)} collective-permute-done((s32[2,4,2]{1,2,0:T(2,128)S(1)}, s32[2,4,2]{1,2,0:T(2,128)S(1)}, u32[]{:S(2)}, u32[]{:S(2)}) %collective-permute-start.15) | collective-permute-done | bytes 96 | tf_op jit(solution)/shard_map/ppermute | solution.py:723
  189.7 5.8 %resample.1.m_hbm = f32[2,2048,128]{2,1,0:T(8,128)} custom-call(s32[4,2]{1,0:T(4,128)} %copy.27.az_ref, s32[4,2]{1,0:T(4,128)} %copy.28.rg_ref, f32[2112,128]{1,0:T(8,128)} %copy-done.6, f32[2112,128]{1,0:T(8,128)} %get-tuple-element.42.refs_1_, f32[2112,128]{1,0:T(8,128)} %get-tuple-element.41.refs_2_, f32[2112,128]{1,0:T(8,128)} %copy-done.7), custom_call_target="tpu_custom_call" | custom-call | flops 2000000000 | bytes 10000000 | tf_op jit(solution)/shard_map/resample/pallas_call | solution.py:636
  195.5 7.4 %master_looks.1 = (f32[16,512]{1,0:T(8,128)}, f32[8,512]{1,0:T(8,128)}) custom-call(f32[16,8,2,16,128]{4,3,2,1,0:T(8,128)} %bitcast.7.x_hbm, bf16[16,256,256]{2,1,0:T(8,128)(2,1)} %prep.1.a_hbm, f32[2,2048,128]{2,1,0:T(8,128)} %resample.1.m_hbm, s32[1,128]{1,0:T(1,128)} %broadcast_in_dim_reshape.3.n_ref, f32[24,128]{1,0:T(8,128)} %constant.84.clone.pick_ref), custom_call_target="tpu_custom_call" | custom-call | flops 5000000000 | bytes 10000000 | tf_op jit(solution)/shard_map/master_looks/pallas_call | solution.py:688
  202.9 1.9 collective-permute-start.20
  204.8 6.9 %collective-permute-start.19 = (f32[8,512]{1,0:T(8,128)}, f32[8,512]{1,0:T(8,128)S(1)}, u32[]{:S(2)}, u32[]{:S(2)}) collective-permute-start(f32[8,512]{1,0:T(8,128)} %get-tuple-element.44), channel_id=1, source_target_pairs={{0,1},{16,2},{1,3},{17,4},{2,5},{18,6},{3,7},{19,8},{4,9},{20,10},... | collective-permute-start | bytes 49160 | tf_op jit(solution)/shard_map/ppermute | solution.py:776
  211.7 1.9 collective-permute-start.18
  214.0 6.5 %collective-permute-done.18.box_ref = f32[16,512]{1,0:T(8,128)S(1)} collective-permute-done((f32[16,512]{1,0:T(8,128)}, f32[16,512]{1,0:T(8,128)S(1)}, u32[]{:S(2)}, u32[]{:S(2)}) %collective-permute-start.18) | collective-permute-done | bytes 32800 | tf_op jit(solution)/shard_map/ppermute | solution.py:775
  (81 shorter events, 17.0 us)
Async XLA Ops:
  3.0 44.2 %all-to-all-start.1 = ((f32[16,10,2,16,128]{4,3,2,1,0:T(8,128)}), f32[16,10,2,16,128]{4,3,2,1,0:T(8,128)}, u32[]{:S(2)}, u32[]{:S(2)}) async-start(f32[16,10,2,16,128]{4,3,2,1,0:T(8,128)} %pre.1), calls=%async_computation.1 | async-start | bytes 5242880 | tf_op jit(solution)/shard_map/all_to_all | solution.py:756
  56.0 82.3 %all-to-all-start.2 = ((f32[128,2,16,128]{3,2,1,0:T(8,128)}), f32[128,2,16,128]{3,2,1,0:T(8,128)S(1)}, u32[]{:S(2)}, u32[]{:S(2)}) async-start(f32[128,2,16,128]{3,2,1,0:T(8,128)} %shard_map.164), calls=%async_computation.2 | async-start | bytes 4194304 | tf_op jit(solution)/shard_map/all_to_all | solution.py:738
  70.1 27.8 %collective-permute-start = (f32[10,2,16,128]{3,2,1,0:T(8,128)}, f32[10,2,16,128]{3,2,1,0:T(8,128)S(1)}, u32[]{:S(2)}, u32[]{:S(2)}) collective-permute-start(f32[10,2,16,128]{3,2,1,0:T(8,128)} %get-tuple-element.25), channel_id=1, source_target_pairs={{0,10},{1,11},{2,8},{3,9},{4,14},{5,15},{6,12},{7,13},{8,2},{9,3},... | collective-permute-start | bytes 491528 | tf_op jit(solution)/shard_map/ppermute | solution.py:760
  74.1 30.3 %collective-permute-start.1 = (f32[10,2,16,128]{3,2,1,0:T(8,128)}, f32[10,2,16,128]{3,2,1,0:T(8,128)S(1)}, u32[]{:S(2)}, u32[]{:S(2)}) collective-permute-start(f32[10,2,16,128]{3,2,1,0:T(8,128)} %get-tuple-element.26), channel_id=1, source_target_pairs={{0,9},{1,10},{2,11},{3,8},{4,13},{5,14},{6,15},{7,12},{8,1},{9,2},... | collective-permute-start | bytes 491528 | tf_op jit(solution)/shard_map/ppermute | solution.py:760
  75.5 28.9 %collective-permute-start.2 = (f32[10,2,16,128]{3,2,1,0:T(8,128)}, f32[10,2,16,128]{3,2,1,0:T(8,128)S(1)}, u32[]{:S(2)}, u32[]{:S(2)}) collective-permute-start(f32[10,2,16,128]{3,2,1,0:T(8,128)} %get-tuple-element.27), channel_id=1, source_target_pairs={{0,6},{1,7},{2,4},{3,5},{4,10},{5,11},{6,8},{7,9},{8,14},{9,15},{1... | collective-permute-start | bytes 491528 | tf_op jit(solution)/shard_map/ppermute | solution.py:760
  76.2 35.0 %collective-permute-start.3 = (f32[10,2,16,128]{3,2,1,0:T(8,128)}, f32[10,2,16,128]{3,2,1,0:T(8,128)S(1)}, u32[]{:S(2)}, u32[]{:S(2)}) collective-permute-start(f32[10,2,16,128]{3,2,1,0:T(8,128)} %get-tuple-element.28), channel_id=1, source_target_pairs={{0,14},{1,15},{2,12},{3,13},{4,2},{5,3},{6,0},{7,1},{8,6},{9,7},{1... | collective-permute-start | bytes 491528 | tf_op jit(solution)/shard_map/ppermute | solution.py:760
  80.6 32.4 %collective-permute-start.4 = (f32[10,2,16,128]{3,2,1,0:T(8,128)}, f32[10,2,16,128]{3,2,1,0:T(8,128)S(1)}, u32[]{:S(2)}, u32[]{:S(2)}) collective-permute-start(f32[10,2,16,128]{3,2,1,0:T(8,128)} %get-tuple-element.29), channel_id=1, source_target_pairs={{0,11},{1,8},{2,9},{3,10},{4,15},{5,12},{6,13},{7,14},{8,3},{9,0},... | collective-permute-start | bytes 491528 | tf_op jit(solution)/shard_map/ppermute | solution.py:760
  97.9 30.8 %copy-start.8 = (f32[10,2,16,128]{3,2,1,0:T(8,128)}, f32[10,2,16,128]{3,2,1,0:T(8,128)S(1)}, u32[]{:S(2)}) copy-start(f32[10,2,16,128]{3,2,1,0:T(8,128)S(1)} %collective-permute-done.refs_0_) | copy-start | bytes 491524
  97.9 17.8 %collective-permute-start.5 = (f32[10,2,16,128]{3,2,1,0:T(8,128)}, f32[10,2,16,128]{3,2,1,0:T(8,128)S(1)}, u32[]{:S(2)}, u32[]{:S(2)}) collective-permute-start(f32[10,2,16,128]{3,2,1,0:T(8,128)} %get-tuple-element.30), channel_id=1, source_target_pairs={{0,8},{1,9},{2,10},{3,11},{4,12},{5,13},{6,14},{7,15},{8,0},{9,1},... | collective-permute-start | bytes 491528 | tf_op jit(solution)/shard_map/ppermute | solution.py:760
  104.4 24.3 %copy-start.9 = (f32[10,2,16,128]{3,2,1,0:T(8,128)}, f32[10,2,16,128]{3,2,1,0:T(8,128)S(1)}, u32[]{:S(2)}) copy-start(f32[10,2,16,128]{3,2,1,0:T(8,128)S(1)} %collective-permute-done.1.refs_1_) | copy-start | bytes 491524
  104.4 11.6 %collective-permute-start.6 = (f32[10,2,16,128]{3,2,1,0:T(8,128)}, f32[10,2,16,128]{3,2,1,0:T(8,128)S(1)}, u32[]{:S(2)}, u32[]{:S(2)}) collective-permute-start(f32[10,2,16,128]{3,2,1,0:T(8,128)} %get-tuple-element.31), channel_id=1, source_target_pairs={{0,5},{1,6},{2,7},{3,4},{4,9},{5,10},{6,11},{7,8},{8,13},{9,14},{1... | collective-permute-start | bytes 491528 | tf_op jit(solution)/shard_map/ppermute | solution.py:760
  104.4 24.3 %copy-start.10 = (f32[10,2,16,128]{3,2,1,0:T(8,128)}, f32[10,2,16,128]{3,2,1,0:T(8,128)S(1)}, u32[]{:S(2)}) copy-start(f32[10,2,16,128]{3,2,1,0:T(8,128)S(1)} %collective-permute-done.2.refs_2_) | copy-start | bytes 491524
  104.4 12.3 %collective-permute-start.7 = (f32[10,2,16,128]{3,2,1,0:T(8,128)}, f32[10,2,16,128]{3,2,1,0:T(8,128)S(1)}, u32[]{:S(2)}, u32[]{:S(2)}) collective-permute-start(f32[10,2,16,128]{3,2,1,0:T(8,128)} %get-tuple-element.32), channel_id=1, source_target_pairs={{0,13},{1,14},{2,15},{3,12},{4,1},{5,2},{6,3},{7,0},{8,5},{9,6},{1... | collective-permute-start | bytes 491528 | tf_op jit(solution)/shard_map/ppermute | solution.py:760
  111.2 17.5 %copy-start.11 = (f32[10,2,16,128]{3,2,1,0:T(8,128)}, f32[10,2,16,128]{3,2,1,0:T(8,128)S(1)}, u32[]{:S(2)}) copy-start(f32[10,2,16,128]{3,2,1,0:T(8,128)S(1)} %collective-permute-done.3.refs_3_) | copy-start | bytes 491524
  111.2 7.5 %collective-permute-start.8 = (f32[10,2,16,128]{3,2,1,0:T(8,128)}, f32[10,2,16,128]{3,2,1,0:T(8,128)}, u32[]{:S(2)}, u32[]{:S(2)}) collective-permute-start(f32[10,2,16,128]{3,2,1,0:T(8,128)} %get-tuple-element.33), channel_id=1, source_target_pairs={{0,2},{1,3},{2,0},{3,1},{4,6},{5,7},{6,4},{7,5},{8,10},{9,11},{10,... | collective-permute-start | bytes 491528 | tf_op jit(solution)/shard_map/ppermute | solution.py:760
  113.0 15.7 %copy-start.12 = (f32[10,2,16,128]{3,2,1,0:T(8,128)}, f32[10,2,16,128]{3,2,1,0:T(8,128)S(1)}, u32[]{:S(2)}) copy-start(f32[10,2,16,128]{3,2,1,0:T(8,128)S(1)} %collective-permute-done.4.refs_4_) | copy-start | bytes 491524
  113.0 10.0 %collective-permute-start.9 = (f32[10,2,16,128]{3,2,1,0:T(8,128)}, f32[10,2,16,128]{3,2,1,0:T(8,128)}, u32[]{:S(2)}, u32[]{:S(2)}) collective-permute-start(f32[10,2,16,128]{3,2,1,0:T(8,128)} %get-tuple-element.34), channel_id=1, source_target_pairs={{0,7},{1,4},{2,5},{3,6},{4,11},{5,8},{6,9},{7,10},{8,15},{9,12},{1... | collective-permute-start | bytes 491528 | tf_op jit(solution)/shard_map/ppermute | solution.py:760
  115.7 13.0 %copy-start.13 = (f32[10,2,16,128]{3,2,1,0:T(8,128)}, f32[10,2,16,128]{3,2,1,0:T(8,128)S(1)}, u32[]{:S(2)}) copy-start(f32[10,2,16,128]{3,2,1,0:T(8,128)S(1)} %collective-permute-done.5.refs_5_) | copy-start | bytes 491524
  115.7 8.9 %collective-permute-start.10 = (f32[10,2,16,128]{3,2,1,0:T(8,128)}, f32[10,2,16,128]{3,2,1,0:T(8,128)}, u32[]{:S(2)}, u32[]{:S(2)}) collective-permute-start(f32[10,2,16,128]{3,2,1,0:T(8,128)} %get-tuple-element.35), channel_id=1, source_target_pairs={{0,15},{1,12},{2,13},{3,14},{4,3},{5,0},{6,1},{7,2},{8,7},{9,4},{1... | collective-permute-start | bytes 491528 | tf_op jit(solution)/shard_map/ppermute | solution.py:760
  116.0 12.7 %copy-start.14 = (f32[10,2,16,128]{3,2,1,0:T(8,128)}, f32[10,2,16,128]{3,2,1,0:T(8,128)S(1)}, u32[]{:S(2)}) copy-start(f32[10,2,16,128]{3,2,1,0:T(8,128)S(1)} %collective-permute-done.6.refs_6_) | copy-start | bytes 491524
  116.0 8.7 %collective-permute-start.11 = (f32[10,2,16,128]{3,2,1,0:T(8,128)}, f32[10,2,16,128]{3,2,1,0:T(8,128)}, u32[]{:S(2)}, u32[]{:S(2)}) collective-permute-start(f32[10,2,16,128]{3,2,1,0:T(8,128)} %get-tuple-element.36), channel_id=1, source_target_pairs={{0,4},{1,5},{2,6},{3,7},{4,8},{5,9},{6,10},{7,11},{8,12},{9,13},{1... | collective-permute-start | bytes 491528 | tf_op jit(solution)/shard_map/ppermute | solution.py:760
  116.8 7.9 %collective-permute-start.12 = (f32[10,2,16,128]{3,2,1,0:T(8,128)}, f32[10,2,16,128]{3,2,1,0:T(8,128)}, u32[]{:S(2)}, u32[]{:S(2)}) collective-permute-start(f32[10,2,16,128]{3,2,1,0:T(8,128)} %get-tuple-element.37), channel_id=1, source_target_pairs={{0,12},{1,13},{2,14},{3,15},{4,0},{5,1},{6,2},{7,3},{8,4},{9,5},{1... | collective-permute-start | bytes 491528 | tf_op jit(solution)/shard_map/ppermute | solution.py:760
  118.7 8.1 %collective-permute-start.13 = (f32[10,2,16,128]{3,2,1,0:T(8,128)}, f32[10,2,16,128]{3,2,1,0:T(8,128)}, u32[]{:S(2)}, u32[]{:S(2)}) collective-permute-start(f32[10,2,16,128]{3,2,1,0:T(8,128)} %get-tuple-element.38), channel_id=1, source_target_pairs={{0,1},{1,2},{2,3},{3,0},{4,5},{5,6},{6,7},{7,4},{8,9},{9,10},{10,1... | collective-permute-start | bytes 491528 | tf_op jit(solution)/shard_map/ppermute | solution.py:760
  123.0 5.7 %collective-permute-start.14 = (f32[10,2,16,128]{3,2,1,0:T(8,128)}, f32[10,2,16,128]{3,2,1,0:T(8,128)}, u32[]{:S(2)}, u32[]{:S(2)}) collective-permute-start(f32[10,2,16,128]{3,2,1,0:T(8,128)} %get-tuple-element.39), channel_id=1, source_target_pairs={{0,3},{1,0},{2,1},{3,2},{4,7},{5,4},{6,5},{7,6},{8,11},{9,8},{10,9... | collective-permute-start | bytes 491528 | tf_op jit(solution)/shard_map/ppermute | solution.py:760
  139.8 55.7 %all-to-all-start = ((f32[128,2,16,128]{3,2,1,0:T(8,128)}), f32[128,2,16,128]{3,2,1,0:T(8,128)}, u32[]{:S(2)}, u32[]{:S(2)}) async-start(f32[128,2,16,128]{3,2,1,0:T(8,128)} %shard_map.163), calls=%async_computation | async-start | bytes 4194304 | tf_op jit(solution)/shard_map/all_to_all | solution.py:738
  154.2 17.8 %copy-start.3 = (s32[256]{0:T(256)S(1)}, s32[256]{0:T(256)}, u32[]{:S(2)}) copy-start(s32[256]{0:T(256)} %param.23) | copy-start | bytes 3076
  160.7 26.9 %collective-permute-start.16 = (f32[2112,128]{1,0:T(8,128)}, f32[2112,128]{1,0:T(8,128)S(1)}, u32[]{:S(2)}, u32[]{:S(2)}) collective-permute-start(f32[2112,128]{1,0:T(8,128)} %get-tuple-element.41.refs_2_), channel_id=1, source_target_pairs={{0,16},{16,1},{1,17},{17,2},{2,18},{18,3},{3,19},{19,4},{4,20},{20... | collective-permute-start | bytes 3244040 | tf_op jit(solution)/shard_map/ppermute | solution.py:729
  164.2 23.4 %collective-permute-start.17 = (f32[2112,128]{1,0:T(8,128)}, f32[2112,128]{1,0:T(8,128)S(1)}, u32[]{:S(2)}, u32[]{:S(2)}) collective-permute-start(f32[2112,128]{1,0:T(8,128)} %get-tuple-element.42.refs_1_), channel_id=1, source_target_pairs={{16,0},{1,16},{17,1},{2,17},{18,2},{3,18},{19,3},{4,19},{20,4},{5,... | collective-permute-start | bytes 3244040 | tf_op jit(solution)/shard_map/ppermute | solution.py:729
  166.2 20.1 %collective-permute-start.15 = (s32[2,4,2]{1,2,0:T(2,128)S(1)}, s32[2,4,2]{1,2,0:T(2,128)S(1)}, u32[]{:S(2)}, u32[]{:S(2)}) collective-permute-start(s32[2,4,2]{1,2,0:T(2,128)S(1)} %pad_add_fusion), channel_id=1, source_target_pairs={{0,0},{1,16},{2,1},{3,17},{4,2},{5,18},{6,3},{7,19},{8,4},{9,20},{... | collective-permute-start | bytes 200 | tf_op jit(solution)/shard_map/ppermute | solution.py:723
  202.9 10.8 %collective-permute-start.20 = (f32[8,512]{1,0:T(8,128)}, f32[8,512]{1,0:T(8,128)S(1)}, u32[]{:S(2)}, u32[]{:S(2)}) collective-permute-start(f32[8,512]{1,0:T(8,128)} %get-tuple-element.44), channel_id=1, source_target_pairs={{16,0},{1,1},{17,2},{2,3},{18,4},{3,5},{19,6},{4,7},{20,8},{5,9},{... | collective-permute-start | bytes 49160 | tf_op jit(solution)/shard_map/ppermute | solution.py:777
  204.8 9.2 %collective-permute-start.19 = (f32[8,512]{1,0:T(8,128)}, f32[8,512]{1,0:T(8,128)S(1)}, u32[]{:S(2)}, u32[]{:S(2)}) collective-permute-start(f32[8,512]{1,0:T(8,128)} %get-tuple-element.44), channel_id=1, source_target_pairs={{0,1},{16,2},{1,3},{17,4},{2,5},{18,6},{3,7},{19,8},{4,9},{20,10},... | collective-permute-start | bytes 49160 | tf_op jit(solution)/shard_map/ppermute | solution.py:776
  211.7 8.8 %collective-permute-start.18 = (f32[16,512]{1,0:T(8,128)}, f32[16,512]{1,0:T(8,128)S(1)}, u32[]{:S(2)}, u32[]{:S(2)}) collective-permute-start(f32[16,512]{1,0:T(8,128)} %get-tuple-element.43), channel_id=1, source_target_pairs={{0,0},{16,1},{1,2},{17,3},{2,4},{18,5},{3,6},{19,7},{4,8},{20,9},{... | collective-permute-start | bytes 98312 | tf_op jit(solution)/shard_map/ppermute | solution.py:775
  (8 other events, 58.3 us)
